TPU v7x, 32 devices: a whole 2x2x4 slice. The times are simulated.
32 devices in a mesh: gx: 8 (over z, x), gy: 4 (over y, core).
Axes of the slice: x: 2, y: 2, z: 4, core: 2. Of those that a mesh axis runs over, the one named last changes fastest.
Arguments:
- density: float32 [512, 128, 128], P('gx', 'gy'), may hold values from -6 to 6
- slowness: float32 [512, 128, 128], P('gx', 'gy'), may hold values from -6 to 6
- pressure_obs: float32 [512, 128, 128], P('gx', 'gy'), may hold values from -6 to 6
- time_obs: float32 [512, 128, 128], P('gx', 'gy'), may hold values from -6 to 6
- zone_map: int32 [512, 128, 128], P('gx', 'gy'), may hold values from 0 to 7
- zone_low: float32 [8], replicated, may hold values from -2.5 to -0.5
- zone_high: float32 [8], replicated, may hold values from 0.5 to 2.5
Outputs:
- density_out: float32 [512, 128, 128], P('gx', 'gy')
- slowness_out: float32 [512, 128, 128], P('gx', 'gy')
- objective: float32 [3], replicated
All inputs are finite; a program needn't handle non-finite values.
Results may differ from a plain program's by a relative error of at most 0.00013.
Values sent between devices are 32-bit elements; how exact they have to be, the bound alone decides.
No kernel may reach another device: no remote copies, remote signals or barrier semaphores. Data moves between devices by JAX's collectives and lax.ppermute only.
A program may use at most 128 MiB of HBM per device.

v0:
```python
import math

import jax
import jax.numpy as jnp
from jax import lax
from jax.sharding import PartitionSpec as P

ITERS = 3


BETA = 1.0
ETA = 0.5
EPSILON = 1e-06


def with_halo(value, sides, width):
    for axis, dim in sides:
        size, length = (lax.axis_size(axis), value.shape[dim])
        up = [(i, (i + 1) % size) for i in range(size - 1)]
        down = [(j, i) for i, j in up]
        last = lax.slice_in_dim(value, length - width, length, axis=dim)
        initial = lax.slice_in_dim(value, 0, width, axis=dim)
        before = lax.ppermute(last, axis, up)
        after = lax.ppermute(initial, axis, down)
        value = jnp.concatenate([before, value, after], axis=dim)
    return value


def cross_product(first_vec, second_vec):
    return (
        first_vec[1] * second_vec[2] - first_vec[2] * second_vec[1],
        first_vec[2] * second_vec[0] - first_vec[0] * second_vec[2],
        first_vec[0] * second_vec[1] - first_vec[1] * second_vec[0],
    )


def depth_slope(inner):
    padded = jnp.pad(inner, [(0, 0)] * (inner.ndim - 1) + [(1, 1)])
    return (padded[..., 2:] - padded[..., :-2]) * 0.5


def depth_adjoint(values):
    padded = jnp.pad(values, [(0, 0)] * (values.ndim - 1) + [(1, 1)])
    return (padded[..., :-2] - padded[..., 2:]) * 0.5


def block_slopes(padded):
    along_x = (padded[:, 2:, 1:-1] - padded[:, :-2, 1:-1]) * 0.5
    along_y = (padded[:, 1:-1, 2:] - padded[:, 1:-1, :-2]) * 0.5
    along_z = depth_slope(padded[:, 1:-1, 1:-1])
    return (along_x, along_y, along_z)


def triangle(length, upward):
    first = jnp.arange(length)[:, None]
    second = jnp.arange(length)[None, :]
    if upward:
        return (first <= second).astype(jnp.float32)
    return (first >= second).astype(jnp.float32)


def depth_prefix(values, upward):
    table = triangle(values.shape[-1], upward)
    return jnp.einsum("xyj,jk->xyk", values, table, precision=lax.Precision.HIGHEST)


def rows_prefix(values, upward):
    table = triangle(values.shape[0], not upward)
    return jnp.einsum("ij,jyz->iyz", table, values, precision=lax.Precision.HIGHEST)


def global_sums(values):
    return lax.psum((values[0], values[1]), ("gx", "gy"))


def local(density, slowness, pressure_obs, time_obs, zone_map, zone_low, zone_high):
    size_x, size_y, depth = density.shape
    parts_x = lax.axis_size("gx")
    parts_y = lax.axis_size("gy")
    total_x = size_x * parts_x
    total_y = size_y * parts_y
    cells = float(total_x * total_y * depth)
    zscale = 1.0 / math.sqrt(depth)
    xscale = 1.0 / math.sqrt(total_x)
    lower_bound = jnp.zeros(density.shape, jnp.float32)
    upper_bound = jnp.zeros(density.shape, jnp.float32)
    for zone_index in range(zone_low.shape[0]):
        hit = zone_map == zone_index
        lower_bound = jnp.where(hit, zone_low[zone_index], lower_bound)
        upper_bound = jnp.where(hit, zone_high[zone_index], upper_bound)
    my_x = lax.axis_index("gx")
    shard_ids = jnp.arange(parts_x)
    own_weight = (shard_ids == my_x).astype(jnp.float32)
    later_weight = (shard_ids > my_x).astype(jnp.float32)
    earlier_table = (shard_ids[:, None] > shard_ids[None, :]).astype(jnp.float32)
    observed_totals = lax.all_gather(jnp.sum(time_obs, 0)[None], "gx", axis=0, tiled=True)
    observed_later = jnp.einsum(
        "k,kyz->yz", later_weight, observed_totals, precision=lax.Precision.HIGHEST
    )
    density_now = density
    slowness_now = slowness
    history = []
    for iteration in range(ITERS):
        fields = jnp.stack((density_now, slowness_now))
        padded = with_halo(fields, (("gx", 1), ("gy", 2)), 1)
        along_x, along_y, along_z = block_slopes(padded)
        first_vec = (along_x[0], along_y[0], along_z[0])
        second_vec = (along_x[1], along_y[1], along_z[1])
        crossed = cross_product(first_vec, second_vec)
        toward_density = cross_product(second_vec, crossed)
        toward_slowness = cross_product(crossed, first_vec)
        lateral = jnp.stack(
            (
                jnp.stack((toward_density[0], toward_slowness[0])),
                jnp.stack((toward_density[1], toward_slowness[1])),
            )
        )
        rims = with_halo(lateral, (("gx", 2), ("gy", 3)), 1)
        back_x = (rims[0, :, :-2, 1:-1] - rims[0, :, 2:, 1:-1]) * 0.5
        back_y = (rims[1, :, 1:-1, :-2] - rims[1, :, 1:-1, 2:]) * 0.5
        back_z = depth_adjoint(jnp.stack((toward_density[2], toward_slowness[2])))
        cross_term = back_x + back_y + back_z
        pressure_miss = depth_prefix(density_now, True) * zscale - pressure_obs
        running = rows_prefix(slowness_now, True)
        stacked = jnp.stack((running[-1], jnp.sum(running, 0)))[None]
        gathered = lax.all_gather(stacked, "gx", axis=0, tiled=True)
        befores = jnp.einsum(
            "kj,jyz->kyz", earlier_table, gathered[:, 0], precision=lax.Precision.HIGHEST
        )
        before = jnp.einsum("k,kyz->yz", own_weight, befores, precision=lax.Precision.HIGHEST)
        shard_sums = gathered[:, 1] + float(size_x) * befores
        after_early = (
            jnp.einsum("k,kyz->yz", later_weight, shard_sums, precision=lax.Precision.HIGHEST)
            * xscale
            - observed_later
        )
        time_miss = (running + before[None]) * xscale - time_obs
        backward = rows_prefix(time_miss, False)
        column_back = depth_prefix(pressure_miss, False)
        grad_density = column_back * zscale + BETA * cross_term[0]
        grad_slowness = (backward + after_early[None]) * xscale + BETA * cross_term[1]
        crossed_sq = (
            jnp.sum(crossed[0] * crossed[0])
            + jnp.sum(crossed[1] * crossed[1])
            + jnp.sum(crossed[2] * crossed[2])
        )
        local_objective = (
            0.5
            * (
                jnp.sum(pressure_miss * pressure_miss)
                + jnp.sum(time_miss * time_miss)
                + BETA * crossed_sq
            )
            / cells
        )
        local_density = jnp.sum(grad_density * grad_density)
        local_slowness = jnp.sum(grad_slowness * grad_slowness)
        history.append(lax.psum(local_objective, ("gx", "gy")))
        norm_density, norm_slowness = global_sums((local_density, local_slowness))
        moved = density_now - ETA * grad_density * lax.rsqrt(norm_density / cells + EPSILON)
        density_now = jnp.minimum(jnp.maximum(moved, lower_bound), upper_bound)
        slowness_now = slowness_now - ETA * grad_slowness * lax.rsqrt(
            norm_slowness / cells + EPSILON
        )
    objective = jnp.stack(history)
    return (density_now, slowness_now, objective)


def solution(mesh):
    placed = (
        P("gx", "gy", None),
        P("gx", "gy", None),
        P("gx", "gy", None),
        P("gx", "gy", None),
        P("gx", "gy", None),
        P(),
        P(),
    )
    return jax.shard_map(
        local,
        mesh=mesh,
        in_specs=placed,
        out_specs=(P("gx", "gy", None), P("gx", "gy", None), P()),
        check_vma=False,
    )
```

profile of v0, /device:TPU:0, one launch (start us, length us, event | category | flops | bytes accessed | tf_op | source)
XLA Modules:
  0.0 458.1 jit_solution(14566495879301720909)
XLA Ops:
  3.5 5.5 %collective-permute-start = (f32[2,1,32,128]{3,2,1,0:T(8,128)S(1)}, f32[2,1,32,128]{3,2,1,0:T(8,128)S(1)}, u32[]{:S(2)}, u32[]{:S(2)}) collective-permute-start(f32[2,1,32,128]{3,2,1,0:T(8,128)S(1)} %get-tuple-element.107), channel_id=1, source_target_pairs={{0,4},{4,8},{8,12},{12,16},{16,20},{20,24},{24,28},{1,5},{5,9},{9,... | collective-permute-start | bytes 98312 | tf_op jit(solution)/shard_map/ppermute | solution.py:23
  10.4 3.4 multiply_reduce_fusion.14
  13.8 31.7 %all-gather = f32[16,32,128]{2,1,0:T(8,128)S(1)} all-gather(f32[2,32,128]{2,1,0:T(8,128)S(1)} %copy.76), channel_id=2, replica_groups=mesh['gx'=8,'gy'=4] {'gx'}, dimensions={0}, use_global_device_ids=true | all-gather | bytes 294912 | tf_op jit(solution)/shard_map/all_gather | solution.py:126
  46.1 2.6 multiply_reduce_fusion.13
  48.7 30.6 %all-gather.1 = f32[256,128]{1,0:T(8,128)S(1)} all-gather(f32[32,128]{1,0:T(8,128)S(1)} %get-tuple-element.116), channel_id=3, replica_groups=mesh['gx'=8,'gy'=4] {'gx'}, dimensions={0}, use_global_device_ids=true | all-gather | bytes 147456 | tf_op jit(solution)/shard_map/all_gather | solution.py:96
  105.0 4.5 collective-permute-start.4
  115.0 4.9 %collective-permute-start.6 = (f32[2,2,66,1,128]{4,3,2,1,0:T(1,128)S(1)}, f32[2,2,66,1,128]{4,3,2,1,0:T(1,128)S(1)}, u32[]{:S(2)}, u32[]{:S(2)}) collective-permute-start(f32[2,2,66,1,128]{4,3,2,1,0:T(1,128)S(1)} %get-tuple-element.61), channel_id=1, source_target_pairs={{0,1},{1,2},{2,3},{4,5},{5,6},{6,7},{8,9},{9,10},{10,11},{12,13},{... | collective-permute-start | bytes 405512 | tf_op jit(solution)/shard_map/ppermute | solution.py:23
  123.3 2.8 multiply_reduce_fusion.20
  127.3 41.4 %all-reduce.8 = (f32[]{:T(128)}, f32[]{:T(128)}) all-reduce(f32[]{:T(128)} %get-tuple-element.139, f32[]{:T(128)} %multiply_reduce_fusion.19), channel_id=1, replica_groups=mesh['gx'=8,'gy'=4] {'gx','gy'}, use_global_device_ids=true, to_apply=%region_1.2 | all-reduce | flops 2 | bytes 16 | tf_op jit(solution)/shard_map/psum | solution.py:73
  172.8 12.6 %maximum_minimum_fusion.2 = (f32[64,32,128]{2,1,0:T(8,128)S(1)}, f32[64,32,128]{2,1,0:T(8,128)}, f32[64,32,128]{2,1,0:T(8,128)}) fusion(f32[64,32,128]{2,1,0:T(8,128)S(1)} %copy-done.12, f32[64,32,128]{2,1,0:T(8,128)S(1)} %copy-done.32, f32[]{:T(128)S(6)} %mul.549, pred[64,32,128]{2,1,0:T(8,128)(4,1)S(1)} %copy-done.47, ...), kind=kLoop, calls=%fused_computation.239 | loop fusion | flops 5242880 | bytes 7340100 | tf_op jit(solution)/shard_map/min | solution.py:161
  190.3 4.8 %collective-permute-start.8 = (f32[2,1,32,128]{3,2,1,0:T(8,128)S(1)}, f32[2,1,32,128]{3,2,1,0:T(8,128)S(1)}, u32[]{:S(2)}, u32[]{:S(2)}) collective-permute-start(f32[2,1,32,128]{3,2,1,0:T(8,128)S(1)} %get-tuple-element.102), channel_id=1, source_target_pairs={{0,4},{4,8},{8,12},{12,16},{16,20},{20,24},{24,28},{1,5},{5,9},{9,... | collective-permute-start | bytes 98312 | tf_op jit(solution)/shard_map/ppermute | solution.py:23
  195.2 31.0 %all-gather.2 = f32[16,32,128]{2,1,0:T(8,128)S(1)} all-gather(f32[2,32,128]{2,1,0:T(8,128)S(1)} %copy.83), channel_id=4, replica_groups=mesh['gx'=8,'gy'=4] {'gx'}, dimensions={0}, use_global_device_ids=true | all-gather | bytes 294912 | tf_op jit(solution)/shard_map/all_gather | solution.py:126
  232.5 3.6 collective-permute-done.10
  243.1 2.6 multiply_subtract_fusion.14
  249.9 4.5 collective-permute-start.12
  260.7 4.9 %collective-permute-start.14 = (f32[2,2,66,1,128]{4,3,2,1,0:T(1,128)S(1)}, f32[2,2,66,1,128]{4,3,2,1,0:T(1,128)S(1)}, u32[]{:S(2)}, u32[]{:S(2)}) collective-permute-start(f32[2,2,66,1,128]{4,3,2,1,0:T(1,128)S(1)} %get-tuple-element.59), channel_id=1, source_target_pairs={{0,1},{1,2},{2,3},{4,5},{5,6},{6,7},{8,9},{9,10},{10,11},{12,13},{... | collective-permute-start | bytes 405512 | tf_op jit(solution)/shard_map/ppermute | solution.py:23
  273.2 40.7 %all-reduce.7 = (f32[]{:T(128)}, f32[]{:T(128)}) all-reduce(f32[]{:T(128)} %get-tuple-element.143, f32[]{:T(128)} %multiply_reduce_fusion.17), channel_id=1, replica_groups=mesh['gx'=8,'gy'=4] {'gx','gy'}, use_global_device_ids=true, to_apply=%region_7.8 | all-reduce | flops 2 | bytes 16 | tf_op jit(solution)/shard_map/psum | solution.py:73
  324.1 4.8 %collective-permute-start.16 = (f32[2,1,32,128]{3,2,1,0:T(8,128)S(1)}, f32[2,1,32,128]{3,2,1,0:T(8,128)S(1)}, u32[]{:S(2)}, u32[]{:S(2)}) collective-permute-start(f32[2,1,32,128]{3,2,1,0:T(8,128)S(1)} %get-tuple-element.97), channel_id=1, source_target_pairs={{0,4},{4,8},{8,12},{12,16},{16,20},{20,24},{24,28},{1,5},{5,9},{9,... | collective-permute-start | bytes 98312 | tf_op jit(solution)/shard_map/ppermute | solution.py:23
  329.0 30.9 %all-gather.3 = f32[16,32,128]{2,1,0:T(8,128)S(1)} all-gather(f32[2,32,128]{2,1,0:T(8,128)S(1)} %copy.90), channel_id=5, replica_groups=mesh['gx'=8,'gy'=4] {'gx'}, dimensions={0}, use_global_device_ids=true | all-gather | bytes 294912 | tf_op jit(solution)/shard_map/all_gather | solution.py:126
  366.3 3.6 collective-permute-done.18
  383.6 4.5 collective-permute-start.20
  394.5 4.9 %collective-permute-start.22 = (f32[2,2,66,1,128]{4,3,2,1,0:T(1,128)S(1)}, f32[2,2,66,1,128]{4,3,2,1,0:T(1,128)S(1)}, u32[]{:S(2)}, u32[]{:S(2)}) collective-permute-start(f32[2,2,66,1,128]{4,3,2,1,0:T(1,128)S(1)} %get-tuple-element.57), channel_id=1, source_target_pairs={{0,1},{1,2},{2,3},{4,5},{5,6},{6,7},{8,9},{9,10},{10,11},{12,13},{... | collective-permute-start | bytes 405512 | tf_op jit(solution)/shard_map/ppermute | solution.py:23
  406.9 42.2 %all-reduce.6 = (f32[]{:T(128)}, f32[]{:T(128)}, f32[1]{0:T(128)}, f32[1]{0:T(128)}, f32[1]{0:T(128)}) all-reduce(f32[]{:T(128)} %get-tuple-element.147, f32[]{:T(128)} %multiply_reduce_fusion.15, f32[1]{0:T(128)} %bitcast.85, f32[1]{0:T(128)} %bitcast.84, f32[1]{0:T(128)} %bitcast.83), channel_id=1, replica_groups=mesh['gx'=8,'gy'=4] {'gx','gy'}, use_global_device_ids=true, to_apply=%region_12.13 | all-reduce | flops 5 | bytes 40 | tf_op jit(solution)/shard_map/psum | solution.py:73
  450.6 3.1 multiply_subtract_fusion
  (226 shorter events, 115.7 us)
Async XLA Ops:
  2.2 84.0 %collective-permute-start.1 = (f32[2,1,32,128]{3,2,1,0:T(8,128)}, f32[2,1,32,128]{3,2,1,0:T(8,128)S(1)}, u32[]{:S(2)}, u32[]{:S(2)}) collective-permute-start(f32[2,1,32,128]{3,2,1,0:T(8,128)} %get-tuple-element.106), channel_id=1, source_target_pairs={{4,0},{8,4},{12,8},{16,12},{20,16},{24,20},{28,24},{5,1},{9,5},{13... | collective-permute-start | bytes 98312 | tf_op jit(solution)/shard_map/ppermute | solution.py:24
  3.5 82.7 %collective-permute-start = (f32[2,1,32,128]{3,2,1,0:T(8,128)S(1)}, f32[2,1,32,128]{3,2,1,0:T(8,128)S(1)}, u32[]{:S(2)}, u32[]{:S(2)}) collective-permute-start(f32[2,1,32,128]{3,2,1,0:T(8,128)S(1)} %get-tuple-element.107), channel_id=1, source_target_pairs={{0,4},{4,8},{8,12},{12,16},{16,20},{20,24},{24,28},{1,5},{5,9},{9,... | collective-permute-start | bytes 98312 | tf_op jit(solution)/shard_map/ppermute | solution.py:23
  86.3 3.7 collective-permute-start.3
  87.6 4.9 %collective-permute-start.2 = (f32[2,66,1,128]{3,2,1,0:T(1,128)S(1)}, f32[2,66,1,128]{3,2,1,0:T(1,128)S(1)}, u32[]{:S(2)}, u32[]{:S(2)}) collective-permute-start(f32[2,66,1,128]{3,2,1,0:T(1,128)S(1)} %get-tuple-element.91), channel_id=1, source_target_pairs={{1,0},{2,1},{3,2},{5,4},{6,5},{7,6},{9,8},{10,9},{11,10},{13,12},{... | collective-permute-start | bytes 202760 | tf_op jit(solution)/shard_map/ppermute | solution.py:24
  103.7 8.4 %collective-permute-start.5 = (f32[2,2,1,32,128]{4,3,2,1,0:T(8,128)}, f32[2,2,1,32,128]{4,3,2,1,0:T(8,128)S(1)}, u32[]{:S(2)}, u32[]{:S(2)}) collective-permute-start(f32[2,2,1,32,128]{4,3,2,1,0:T(8,128)} %get-tuple-element.72), channel_id=1, source_target_pairs={{4,0},{8,4},{12,8},{16,12},{20,16},{24,20},{28,24},{5,1},{9,5},{13... | collective-permute-start | bytes 196616 | tf_op jit(solution)/shard_map/ppermute | solution.py:24
  105.0 7.1 %collective-permute-start.4 = (f32[2,2,1,32,128]{4,3,2,1,0:T(8,128)}, f32[2,2,1,32,128]{4,3,2,1,0:T(8,128)S(1)}, u32[]{:S(2)}, u32[]{:S(2)}) collective-permute-start(f32[2,2,1,32,128]{4,3,2,1,0:T(8,128)} %get-tuple-element.71), channel_id=1, source_target_pairs={{0,4},{4,8},{8,12},{12,16},{16,20},{20,24},{24,28},{1,5},{5,9},{9,... | collective-permute-start | bytes 196616 | tf_op jit(solution)/shard_map/ppermute | solution.py:23
  113.7 7.4 %collective-permute-start.7 = (f32[2,2,66,1,128]{4,3,2,1,0:T(1,128)S(1)}, f32[2,2,66,1,128]{4,3,2,1,0:T(1,128)S(1)}, u32[]{:S(2)}, u32[]{:S(2)}) collective-permute-start(f32[2,2,66,1,128]{4,3,2,1,0:T(1,128)S(1)} %get-tuple-element.62), channel_id=1, source_target_pairs={{1,0},{2,1},{3,2},{5,4},{6,5},{7,6},{9,8},{10,9},{11,10},{13,12},{... | collective-permute-start | bytes 405512 | tf_op jit(solution)/shard_map/ppermute | solution.py:24
  115.0 6.1 %collective-permute-start.6 = (f32[2,2,66,1,128]{4,3,2,1,0:T(1,128)S(1)}, f32[2,2,66,1,128]{4,3,2,1,0:T(1,128)S(1)}, u32[]{:S(2)}, u32[]{:S(2)}) collective-permute-start(f32[2,2,66,1,128]{4,3,2,1,0:T(1,128)S(1)} %get-tuple-element.61), channel_id=1, source_target_pairs={{0,1},{1,2},{2,3},{4,5},{5,6},{6,7},{8,9},{9,10},{10,11},{12,13},{... | collective-permute-start | bytes 405512 | tf_op jit(solution)/shard_map/ppermute | solution.py:23
  188.9 40.4 %collective-permute-start.9 = (f32[2,1,32,128]{3,2,1,0:T(8,128)S(1)}, f32[2,1,32,128]{3,2,1,0:T(8,128)S(1)}, u32[]{:S(2)}, u32[]{:S(2)}) collective-permute-start(f32[2,1,32,128]{3,2,1,0:T(8,128)S(1)} %get-tuple-element.101), channel_id=1, source_target_pairs={{4,0},{8,4},{12,8},{16,12},{20,16},{24,20},{28,24},{5,1},{9,5},{13... | collective-permute-start | bytes 98312 | tf_op jit(solution)/shard_map/ppermute | solution.py:24
  190.3 39.0 %collective-permute-start.8 = (f32[2,1,32,128]{3,2,1,0:T(8,128)S(1)}, f32[2,1,32,128]{3,2,1,0:T(8,128)S(1)}, u32[]{:S(2)}, u32[]{:S(2)}) collective-permute-start(f32[2,1,32,128]{3,2,1,0:T(8,128)S(1)} %get-tuple-element.102), channel_id=1, source_target_pairs={{0,4},{4,8},{8,12},{12,16},{16,20},{20,24},{24,28},{1,5},{5,9},{9,... | collective-permute-start | bytes 98312 | tf_op jit(solution)/shard_map/ppermute | solution.py:23
  229.4 3.1 collective-permute-start.11
  230.7 5.4 %collective-permute-start.10 = (f32[2,66,1,128]{3,2,1,0:T(1,128)S(1)}, f32[2,66,1,128]{3,2,1,0:T(1,128)S(1)}, u32[]{:S(2)}, u32[]{:S(2)}) collective-permute-start(f32[2,66,1,128]{3,2,1,0:T(1,128)S(1)} %get-tuple-element.87), channel_id=1, source_target_pairs={{1,0},{2,1},{3,2},{5,4},{6,5},{7,6},{9,8},{10,9},{11,10},{13,12},{... | collective-permute-start | bytes 202760 | tf_op jit(solution)/shard_map/ppermute | solution.py:24
  248.6 8.9 %collective-permute-start.13 = (f32[2,2,1,32,128]{4,3,2,1,0:T(8,128)S(1)}, f32[2,2,1,32,128]{4,3,2,1,0:T(8,128)S(1)}, u32[]{:S(2)}, u32[]{:S(2)}) collective-permute-start(f32[2,2,1,32,128]{4,3,2,1,0:T(8,128)S(1)} %get-tuple-element.68), channel_id=1, source_target_pairs={{4,0},{8,4},{12,8},{16,12},{20,16},{24,20},{28,24},{5,1},{9,5},{13... | collective-permute-start | bytes 196616 | tf_op jit(solution)/shard_map/ppermute | solution.py:24
  249.9 7.7 %collective-permute-start.12 = (f32[2,2,1,32,128]{4,3,2,1,0:T(8,128)S(1)}, f32[2,2,1,32,128]{4,3,2,1,0:T(8,128)S(1)}, u32[]{:S(2)}, u32[]{:S(2)}) collective-permute-start(f32[2,2,1,32,128]{4,3,2,1,0:T(8,128)S(1)} %get-tuple-element.67), channel_id=1, source_target_pairs={{0,4},{4,8},{8,12},{12,16},{16,20},{20,24},{24,28},{1,5},{5,9},{9,... | collective-permute-start | bytes 196616 | tf_op jit(solution)/shard_map/ppermute | solution.py:23
  259.4 7.4 %collective-permute-start.15 = (f32[2,2,66,1,128]{4,3,2,1,0:T(1,128)S(1)}, f32[2,2,66,1,128]{4,3,2,1,0:T(1,128)S(1)}, u32[]{:S(2)}, u32[]{:S(2)}) collective-permute-start(f32[2,2,66,1,128]{4,3,2,1,0:T(1,128)S(1)} %get-tuple-element.60), channel_id=1, source_target_pairs={{1,0},{2,1},{3,2},{5,4},{6,5},{7,6},{9,8},{10,9},{11,10},{13,12},{... | collective-permute-start | bytes 405512 | tf_op jit(solution)/shard_map/ppermute | solution.py:24
  260.7 6.2 %collective-permute-start.14 = (f32[2,2,66,1,128]{4,3,2,1,0:T(1,128)S(1)}, f32[2,2,66,1,128]{4,3,2,1,0:T(1,128)S(1)}, u32[]{:S(2)}, u32[]{:S(2)}) collective-permute-start(f32[2,2,66,1,128]{4,3,2,1,0:T(1,128)S(1)} %get-tuple-element.59), channel_id=1, source_target_pairs={{0,1},{1,2},{2,3},{4,5},{5,6},{6,7},{8,9},{9,10},{10,11},{12,13},{... | collective-permute-start | bytes 405512 | tf_op jit(solution)/shard_map/ppermute | solution.py:23
  322.6 40.4 %collective-permute-start.17 = (f32[2,1,32,128]{3,2,1,0:T(8,128)S(1)}, f32[2,1,32,128]{3,2,1,0:T(8,128)S(1)}, u32[]{:S(2)}, u32[]{:S(2)}) collective-permute-start(f32[2,1,32,128]{3,2,1,0:T(8,128)S(1)} %get-tuple-element.96), channel_id=1, source_target_pairs={{4,0},{8,4},{12,8},{16,12},{20,16},{24,20},{28,24},{5,1},{9,5},{13... | collective-permute-start | bytes 98312 | tf_op jit(solution)/shard_map/ppermute | solution.py:24
  324.1 39.0 %collective-permute-start.16 = (f32[2,1,32,128]{3,2,1,0:T(8,128)S(1)}, f32[2,1,32,128]{3,2,1,0:T(8,128)S(1)}, u32[]{:S(2)}, u32[]{:S(2)}) collective-permute-start(f32[2,1,32,128]{3,2,1,0:T(8,128)S(1)} %get-tuple-element.97), channel_id=1, source_target_pairs={{0,4},{4,8},{8,12},{12,16},{16,20},{20,24},{24,28},{1,5},{5,9},{9,... | collective-permute-start | bytes 98312 | tf_op jit(solution)/shard_map/ppermute | solution.py:23
  363.1 3.2 collective-permute-start.19
  364.4 5.5 %collective-permute-start.18 = (f32[2,66,1,128]{3,2,1,0:T(1,128)S(1)}, f32[2,66,1,128]{3,2,1,0:T(1,128)S(1)}, u32[]{:S(2)}, u32[]{:S(2)}) collective-permute-start(f32[2,66,1,128]{3,2,1,0:T(1,128)S(1)} %get-tuple-element.83), channel_id=1, source_target_pairs={{1,0},{2,1},{3,2},{5,4},{6,5},{7,6},{9,8},{10,9},{11,10},{13,12},{... | collective-permute-start | bytes 202760 | tf_op jit(solution)/shard_map/ppermute | solution.py:24
  382.3 9.0 %collective-permute-start.21 = (f32[2,2,1,32,128]{4,3,2,1,0:T(8,128)S(1)}, f32[2,2,1,32,128]{4,3,2,1,0:T(8,128)S(1)}, u32[]{:S(2)}, u32[]{:S(2)}) collective-permute-start(f32[2,2,1,32,128]{4,3,2,1,0:T(8,128)S(1)} %get-tuple-element.64), channel_id=1, source_target_pairs={{4,0},{8,4},{12,8},{16,12},{20,16},{24,20},{28,24},{5,1},{9,5},{13... | collective-permute-start | bytes 196616 | tf_op jit(solution)/shard_map/ppermute | solution.py:24
  383.6 7.7 %collective-permute-start.20 = (f32[2,2,1,32,128]{4,3,2,1,0:T(8,128)S(1)}, f32[2,2,1,32,128]{4,3,2,1,0:T(8,128)S(1)}, u32[]{:S(2)}, u32[]{:S(2)}) collective-permute-start(f32[2,2,1,32,128]{4,3,2,1,0:T(8,128)S(1)} %get-tuple-element.63), channel_id=1, source_target_pairs={{0,4},{4,8},{8,12},{12,16},{16,20},{20,24},{24,28},{1,5},{5,9},{9,... | collective-permute-start | bytes 196616 | tf_op jit(solution)/shard_map/ppermute | solution.py:23
  393.2 7.4 %collective-permute-start.23 = (f32[2,2,66,1,128]{4,3,2,1,0:T(1,128)S(1)}, f32[2,2,66,1,128]{4,3,2,1,0:T(1,128)S(1)}, u32[]{:S(2)}, u32[]{:S(2)}) collective-permute-start(f32[2,2,66,1,128]{4,3,2,1,0:T(1,128)S(1)} %get-tuple-element.58), channel_id=1, source_target_pairs={{1,0},{2,1},{3,2},{5,4},{6,5},{7,6},{9,8},{10,9},{11,10},{13,12},{... | collective-permute-start | bytes 405512 | tf_op jit(solution)/shard_map/ppermute | solution.py:24
  394.5 6.2 %collective-permute-start.22 = (f32[2,2,66,1,128]{4,3,2,1,0:T(1,128)S(1)}, f32[2,2,66,1,128]{4,3,2,1,0:T(1,128)S(1)}, u32[]{:S(2)}, u32[]{:S(2)}) collective-permute-start(f32[2,2,66,1,128]{4,3,2,1,0:T(1,128)S(1)} %get-tuple-element.57), channel_id=1, source_target_pairs={{0,1},{1,2},{2,3},{4,5},{5,6},{6,7},{8,9},{9,10},{10,11},{12,13},{... | collective-permute-start | bytes 405512 | tf_op jit(solution)/shard_map/ppermute | solution.py:23
  (52 other events, 371.6 us)
where the time goes:
time: 466 us; the launch traced here: 458 us
  blocking collectives  249 us (53%)
  other arithmetic  82.6 us (18%)
  starting transfers between devices  64.1 us (14%)
  matrix products  26.4 us (6%)
  between operations  16 us (3%)
  local copies, waits for them, and re-layouts  10.7 us (2%)
  waiting for transfers between devices  9.75 us (2%)
    psum x3, blocking collectives, global_sums(): return lax.psum((values[0], values[1]), ('gx', 'gy'))  124 us
    all_gather x3, blocking collectives, local(): gathered = lax.all_gather(stacked, 'gx', axis=0, tiled=True)  93.6 us
    ppermute x12, starting transfers between devices, with_halo(): before = lax.ppermute(last, axis, up)  47.5 us
    all_gather x1, blocking collectives, local(): lax.all_gather(jnp.sum(time_obs, 0)[None], 'gx', axis=0, tiled=True)  30.6 us
    ppermute x12, starting transfers between devices, with_halo(): after = lax.ppermute(initial, axis, down)  16.7 us
    dot_general x6, matrix products, depth_prefix(): jnp.einsum('xyj,jk->xyk', values, table, precision=lax.Precision.HIGHEST)  15.1 us
    min x3, other arithmetic, local(): density_now = jnp.minimum(jnp.maximum(moved, lower_bound), upper_bound)  14.5 us
    ppermute x12, waiting for transfers between devices, with_halo(): after = lax.ppermute(initial, axis, down)  9.72 us
  transfers between devices with their start and end apart: 24, of which 3 were waited for; matrix products, arithmetic and copies ran while one was open for 5% of the time, Pallas kernels for 0%

commit v1 on v0

v1 whole, which is shorter than its diff:
```python
import functools
import math

import jax
import jax.numpy as jnp
from jax import lax
from jax.experimental import pallas as pl
from jax.experimental.pallas import tpu as pltpu
from jax.sharding import PartitionSpec as P

ITERS = 3
BETA = 1.0
ETA = 0.5
EPSILON = 1e-06

XO = 2
YO = 4
F32 = jnp.float32
BF16 = jnp.bfloat16


class Geo:
    def __init__(self, nx, ny, nz, px, py):
        self.nx, self.ny, self.nz, self.px, self.py = nx, ny, nz, px, py
        self.pl = ny + 2 * YO
        self.planes = nx + 2 * XO
        self.ext = (nx + 8) * self.pl
        self.xp = nx + 8
        self.cells = float(nx * px * ny * py * nz)
        self.zs = 1.0 / math.sqrt(nz)
        self.xs = 1.0 / math.sqrt(nx * px)
        self.win = (nx + 2) * self.pl + 8

    def own(self, x):
        return (x + XO) * self.pl + YO


def fold8(v):
    total = v[0:8]
    for i in range(8, v.shape[0], 8):
        total = total + v[i : i + 8]
    return total


def pick_sides(even, first, last, a, b):
    low = jnp.where(even, b, a)
    high = jnp.where(even, a, b)
    return jnp.where(first, 0.0, low), jnp.where(last, 0.0, high)


def put_pair(even, low, high, a_ref, b_ref, at):
    n = low.shape[0]
    a_ref[at : at + n, :] = jnp.where(even, high, low)
    b_ref[at : at + n, :] = jnp.where(even, low, high)


def flags_of(g, flags):
    ix, iy = flags[0], flags[1]
    return ((ix % 2) == 0, ix == 0, ix == g.px - 1), ((iy % 2) == 0, iy == 0, iy == g.py - 1)


def split2(v):
    high = v.astype(BF16)
    low = (v - high.astype(F32)).astype(BF16)
    return jnp.concatenate([high, low], axis=1)


def first_kernel(g, flags, rho, sigma, zone, t, tr, xa, xb):
    (even, _, _), _ = flags_of(g, flags)

    def body(x, carry):
        run, total, seen = carry
        run = run + sigma[x]
        return run, total + run, seen + t[x]

    zero = jnp.zeros((g.ny, g.nz), F32)
    run, total, seen = lax.fori_loop(0, g.nx, body, (zero, zero, zero), unroll=4)
    rest = total * g.xs - seen
    for s in range(g.px):
        tr[s, 0 : g.ny, :] = run
        tr[s, g.ny : 2 * g.ny, :] = rest
    at = 0
    for f, ref in enumerate((rho, sigma, zone)):
        for r in range(2):
            low = ref[r].astype(F32)
            high = ref[g.nx - 2 + r].astype(F32)
            put_pair(even, low, high, xa, xb, at)
            at += g.ny


def spread_kernel(g, zones, zlow, zhigh, rho, sigma, zone, p, rho_e, sig_e, low_e, high_e, q, table):
    nz = g.nz
    row = lax.broadcasted_iota(jnp.int32, (2 * nz, 2 * nz), 0) % nz
    col = lax.broadcasted_iota(jnp.int32, (2 * nz, 2 * nz), 1)
    first = (row <= col).astype(F32)
    second = (nz - jnp.maximum(row, col - nz)).astype(F32)
    table[...] = jnp.where(col < nz, first, second).astype(BF16)
    r2 = lax.broadcasted_iota(jnp.int32, (2 * nz, nz), 0) % nz
    c2 = lax.broadcasted_iota(jnp.int32, (2 * nz, nz), 1)
    back = (r2 >= c2).astype(F32).astype(BF16)
    step = 8

    def body(c, carry):
        for k in range(step):
            x = c * step + k
            at = pl.ds(g.own(x), g.ny)
            rho_e[at, :] = rho[x]
            sig_e[at, :] = sigma[x]
            z = zone[x]
            low = jnp.full((g.ny, nz), zlow[0], F32)
            high = jnp.full((g.ny, nz), zhigh[0], F32)
            for i in range(1, zones):
                hit = z == i
                low = jnp.where(hit, zlow[i], low)
                high = jnp.where(hit, zhigh[i], high)
            low_e[at, :] = low
            high_e[at, :] = high
        rows = p[pl.ds(c * step, step)].reshape(step * g.ny, nz)
        out = jnp.dot(split2(rows), back, preferred_element_type=F32) * g.zs
        q[pl.ds(c * step, step)] = out.reshape(step, g.ny, nz)
        return carry

    lax.fori_loop(0, g.nx // step, body, 0)


def sides_kernel(g, fields, flags, xa, xb, *refs):
    exts, (ya, yb) = refs[:fields], refs[fields:]
    (xeven, xfirst, xlast), (yeven, _, _) = flags_of(g, flags)
    n = g.xp
    for f in range(fields):
        ext = exts[f]
        for r in range(2):
            low = ext[pl.ds(YO + r, n, stride=g.pl), :]
            high = ext[pl.ds(YO + g.ny - 2 + r, n, stride=g.pl), :]
            put_pair(yeven, low, high, ya, yb, (f * 2 + r) * n)
    for f in range(fields):
        for px in range(2):
            base = (f * 2 + px) * g.ny
            for r in range(2):
                for side in range(2):
                    at = base + (r if side == 0 else g.ny - 2 + r)
                    left, right = pick_sides(xeven, xfirst, xlast, xa[at : at + 1, :], xb[at : at + 1, :])
                    for plane, value in ((px, left), (XO + g.nx + px, right)):
                        spot = (f * 2 + r) * n + plane

                        @pl.when(yeven if side == 1 else jnp.logical_not(yeven))
                        def _():
                            ya[spot : spot + 1, :] = value

                        @pl.when(jnp.logical_not(yeven) if side == 1 else yeven)
                        def _():
                            yb[spot : spot + 1, :] = value


def halos(g, flags, fields, xa, xb, ya, yb):
    (xeven, xfirst, xlast), (yeven, yfirst, ylast) = flags_of(g, flags)
    out = []
    for f in range(fields):
        for r in range(2):
            at = (f * 2 + r) * g.ny
            low, high = pick_sides(xeven, xfirst, xlast, xa[at : at + g.ny, :], xb[at : at + g.ny, :])
            out.append((f, pl.ds(r * g.pl + YO, g.ny), low))
            out.append((f, pl.ds((XO + g.nx + r) * g.pl + YO, g.ny), high))
    n = g.xp
    for f in range(fields):
        for r in range(2):
            at = (f * 2 + r) * n
            low, high = pick_sides(yeven, yfirst, ylast, ya[at : at + n, :], yb[at : at + n, :])
            out.append((f, pl.ds(YO - 2 + r, n, stride=g.pl), low))
            out.append((f, pl.ds(YO + g.ny + r, n, stride=g.pl), high))
    return out


def lane_value(row, lane):
    ids = lax.broadcasted_iota(jnp.int32, row.shape, 1)
    return jnp.sum(jnp.where(ids == lane, row, 0.0), axis=1, keepdims=True)


def alphas(g, sums):
    row = jnp.sum(sums[...], axis=0, keepdims=True)
    return tuple(ETA * lax.rsqrt(lane_value(row, k) / g.cells + EPSILON) for k in range(2))


def copy_rows(g, pairs, fn):
    def body(i, carry):
        at = pl.ds(pl.multiple_of(i * g.pl, 8), g.pl)
        fn(at)
        return carry

    lax.fori_loop(0, g.planes, body, 0, unroll=4)


def step_core(g, flags, rho_e, sig_e, trs, p, q, t, table, outs, scratch):
    grho_e, gsig_e, sums, tr, xa, xb = outs
    vxr, vxs, vyr, vys, gyr, gys, dr, rt_s, yu, ym = scratch
    nx, ny, nz = g.nx, g.ny, g.nz
    (even, _, _), _ = flags_of(g, flags)
    ix = flags[0]
    zero = jnp.zeros((ny, nz), F32)
    zero8 = jnp.zeros((8, nz), F32)
    run = zero
    before = zero
    after = zero
    for s in range(g.px):
        total = trs[s, 0:ny, :]
        after = after + jnp.where(s > ix, trs[s, ny : 2 * ny, :] + run * (nx * g.xs), 0.0)
        before = before + jnp.where(s < ix, total, 0.0)
        run = run + total

    def rays(x, carry):
        run, acc = carry
        run = run + sig_e[pl.ds(g.own(x), ny), :]
        miss = run * g.xs - t[x]
        rt_s[pl.ds(x * ny, ny), :] = miss
        return run, acc + fold8(miss * miss)

    _, acc_t = lax.fori_loop(0, nx, rays, (before, zero8), unroll=4)

    step = 8
    rows = step * g.pl

    def columns(c, acc):
        x = rho_e[pl.ds((c * step + XO) * g.pl, rows), :]
        y = jnp.dot(split2(x), table[...], preferred_element_type=F32)
        yu[...] = y[:, :nz]
        ym[...] = y[:, nz:]
        for k in range(step):
            plane = c * step + k
            at = pl.ds(k * g.pl + YO, ny)
            miss = yu[at, :] * g.zs - p[plane]
            acc = acc + fold8(miss * miss)
            dr[pl.ds(plane * ny, ny), :] = ym[at, :] * (g.zs * g.zs) - q[plane]
        return acc

    acc_p = lax.fori_loop(0, nx // step, columns, zero8)

    lanes = lax.broadcasted_iota(jnp.int32, (g.pl, nz), 1)
    below = lanes > 0
    above = lanes < nz - 1
    rowid = lax.broadcasted_iota(jnp.int32, (g.pl, nz), 0)
    mine = jnp.logical_and(rowid >= 1, rowid <= ny)

    def slopes(ref, base):
        w = g.pl
        c = ref[pl.ds(base, w), :]
        sx = ref[pl.ds(base + g.pl, w), :] - ref[pl.ds(base - g.pl, w), :]
        sy = ref[pl.ds(base + 1, w), :] - ref[pl.ds(base - 1, w), :]
        sz = jnp.where(above, pltpu.roll(c, nz - 1, 1), 0.0) - jnp.where(below, pltpu.roll(c, 1, 1), 0.0)
        return sx, sy, sz

    def adjoint_z(v):
        return jnp.where(below, pltpu.roll(v, 1, 1), 0.0) - jnp.where(above, pltpu.roll(v, nz - 1, 1), 0.0)

    def cross_plane(xi, acc, inside):
        base = (xi + XO - 1) * g.pl + YO - 1
        w = g.pl
        a0, a1, a2 = slopes(rho_e, base)
        b0, b1, b2 = slopes(sig_e, base)
        c0 = a1 * b2 - a2 * b1
        c1 = a2 * b0 - a0 * b2
        c2 = a0 * b1 - a1 * b0
        at = xi * w
        vxr[pl.ds(at, w), :] = b1 * c2 - b2 * c1
        vxs[pl.ds(at, w), :] = c1 * a2 - c2 * a1
        if not inside:
            return acc
        acc = acc + fold8(jnp.where(mine, c0 * c0 + c1 * c1 + c2 * c2, 0.0))
        vyr[pl.ds(at, w), :] = b2 * c0 - b0 * c2
        vys[pl.ds(at, w), :] = c2 * a0 - c0 * a2
        zr = adjoint_z(b0 * c1 - b1 * c0)
        zs = adjoint_z(c0 * a1 - c1 * a0)
        gyr[pl.ds(at, w), :] = zr + (vyr[pl.ds(at - 1, w), :] - vyr[pl.ds(at + 1, w), :])
        gys[pl.ds(at, w), :] = zs + (vys[pl.ds(at - 1, w), :] - vys[pl.ds(at + 1, w), :])
        return acc

    cross_plane(0, None, False)
    acc_c = lax.fori_loop(1, nx + 1, lambda xi, acc: cross_plane(xi, acc, True), zero8)
    cross_plane(nx + 1, None, False)

    def gradients(i, carry):
        back, sum_t, sum_r, nr, ns = carry
        x = nx - 1 - i
        w = g.pl
        lower = pl.ds(x * w + 1, ny)
        here = pl.ds((x + 1) * w + 1, ny)
        upper = pl.ds((x + 2) * w + 1, ny)
        cr = (vxr[lower, :] - vxr[upper, :] + gyr[here, :]) * (BETA / 16.0)
        cs = (vxs[lower, :] - vxs[upper, :] + gys[here, :]) * (BETA / 16.0)
        back = back + rt_s[pl.ds(x * ny, ny), :]
        gr = dr[pl.ds(x * ny, ny), :] + cr
        gs = back * g.xs + cs
        at = pl.ds(g.own(x), ny)
        grho_e[at, :] = gr
        gsig_e[at, :] = gs
        weight = (i + 1).astype(F32)
        return back, sum_t + gs, sum_r + gs * weight, nr + fold8(gr * gr), ns + fold8(gs * gs)

    _, sum_t, sum_r, nr, ns = lax.fori_loop(0, nx, gradients, (after, zero, zero, zero8, zero8), unroll=2)

    total = lambda v: jnp.sum(jnp.sum(v, axis=0, keepdims=True), axis=1, keepdims=True)
    lane = lax.broadcasted_iota(jnp.int32, sums.shape, 1)
    obj = acc_t + acc_p + acc_c * (BETA / 16.0)
    sums[...] = jnp.where(lane == 0, total(nr), jnp.where(lane == 1, total(ns), jnp.where(lane == 2, total(obj), 0.0)))
    if tr is not None:
        rest = sum_r * g.xs
        for s in range(g.px):
            tr[s, 0:ny, :] = sum_t
            tr[s, ny : 2 * ny, :] = rest
        pos = 0
        for ext in (grho_e, gsig_e):
            for r in range(2):
                put_pair(even, ext[pl.ds(g.own(r), ny), :], ext[pl.ds(g.own(nx - 2 + r), ny), :], xa, xb, pos)
                pos += ny


def opening_step(g, zones, flags, zlow, zhigh, xa, xb, ya, yb, rho_i, sig_i, low_i, high_i, trs, p, q, t, table,
                 rho_e, sig_e, low_e, high_e, *rest):
    def move(at):
        rho_e[at, :] = rho_i[at, :]
        sig_e[at, :] = sig_i[at, :]
        low_e[at, :] = low_i[at, :]
        high_e[at, :] = high_i[at, :]

    copy_rows(g, None, move)
    for f, at, value in halos(g, flags, 3, xa, xb, ya, yb):
        if f == 0:
            rho_e[at, :] = value
        elif f == 1:
            sig_e[at, :] = value
        else:
            low = jnp.full(value.shape, zlow[0], F32)
            high = jnp.full(value.shape, zhigh[0], F32)
            for i in range(1, zones):
                hit = value == float(i)
                low = jnp.where(hit, zlow[i], low)
                high = jnp.where(hit, zhigh[i], high)
            low_e[at, :] = low
            high_e[at, :] = high
    step_core(g, flags, rho_e, sig_e, trs, p, q, t, table, rest[:6], rest[6:])


def later_step(g, last, flags, xa, xb, ya, yb, sums_i, grho_i, gsig_i, tr_i, rho_i, sig_i, low_e, high_e, trs_i,
               p, q, t, table, rho_e, sig_e, trs, *rest):
    ar, asig = alphas(g, sums_i)

    def move(at):
        rho_e[at, :] = jnp.minimum(jnp.maximum(rho_i[at, :] - ar * grho_i[at, :], low_e[at, :]), high_e[at, :])
        sig_e[at, :] = sig_i[at, :] - asig * gsig_i[at, :]

    copy_rows(g, None, move)
    for f, at, value in halos(g, flags, 2, xa, xb, ya, yb):
        if f == 0:
            rho_e[at, :] = jnp.minimum(jnp.maximum(rho_i[at, :] - ar * value, low_e[at, :]), high_e[at, :])
        else:
            sig_e[at, :] = sig_i[at, :] - asig * value
    for s in range(g.px):
        trs[s] = trs_i[s] - asig * tr_i[s]
    if last:
        outs, scratch = (rest[0], rest[1], rest[2], None, None, None), rest[3:]
    else:
        outs, scratch = rest[:6], rest[6:]
    step_core(g, flags, rho_e, sig_e, trs, p, q, t, table, outs, scratch)


def closing_kernel(g, sums0, sums1, sums2, grho_e, gsig_e, rho_e, sig_e, low_e, high_e, rho_o, sig_o, obj):
    ar, asig = alphas(g, sums2)

    def body(x, carry):
        at = pl.ds(g.own(x), g.ny)
        rho_o[x] = jnp.minimum(jnp.maximum(rho_e[at, :] - ar * grho_e[at, :], low_e[at, :]), high_e[at, :])
        sig_o[x] = sig_e[at, :] - asig * gsig_e[at, :]
        return carry

    lax.fori_loop(0, g.nx, body, 0, unroll=4)
    lane = lax.broadcasted_iota(jnp.int32, obj.shape, 1)
    total = jnp.zeros(obj.shape, F32)
    for k, sums in enumerate((sums0, sums1, sums2)):
        row = jnp.sum(sums[...], axis=0, keepdims=True)
        total = jnp.where(lane == k, lane_value(row, 2) * (0.5 / g.cells), total)
    obj[...] = total


def pairs_of(size):
    a = [(i, i ^ 1) for i in range(size)]
    b = [(i, i if i in (0, size - 1) else ((i + 1) ^ 1) - 1) for i in range(size)]
    return a, b


def exchange(axis, a, b):
    pa, pb = pairs_of(lax.axis_size(axis))
    return lax.ppermute(a, axis, pa), lax.ppermute(b, axis, pb)


SMEM = pl.BlockSpec(memory_space=pltpu.SMEM)
VMEM = pl.BlockSpec(memory_space=pltpu.VMEM)


def call(body, name, shapes, specs, args, scratch=(), limit=24):
    return pl.pallas_call(
        body,
        name=name,
        out_shape=[jax.ShapeDtypeStruct(s, d) for s, d in shapes],
        in_specs=specs,
        out_specs=[VMEM] * len(shapes),
        scratch_shapes=list(scratch),
        compiler_params=pltpu.CompilerParams(vmem_limit_bytes=limit * 1024 * 1024),
    )(*args)


def local(density, slowness, pressure_obs, time_obs, zone_map, zone_low, zone_high):
    nx, ny, nz = density.shape
    px, py = lax.axis_size("gx"), lax.axis_size("gy")
    g = Geo(nx, ny, nz, px, py)
    zones = zone_low.shape[0]
    both = ("gx", "gy")
    flags = jnp.stack([lax.axis_index("gx"), lax.axis_index("gy")]).astype(jnp.int32)

    ext = ((g.ext, nz), F32)
    tr_shape = ((px, 2 * ny, nz), F32)
    sums_shape = ((px * py, nz), F32)
    block = ((nx, ny, nz), F32)
    xmsg = lambda f: ((f * 2 * ny, nz), F32)
    ymsg = lambda f: ((f * 2 * g.xp, nz), F32)
    win = pltpu.VMEM((g.win, nz), F32)
    core_scratch = [win] * 6 + [pltpu.VMEM((nx * ny, nz), F32)] * 2 + [pltpu.VMEM((8 * g.pl, nz), F32)] * 2

    tr, xa, xb = call(
        functools.partial(first_kernel, g), "first", [tr_shape, xmsg(3), xmsg(3)],
        [SMEM] + [VMEM] * 4, (flags, density, slowness, zone_map, time_obs),
    )
    trs = lax.all_to_all(tr, "gx", 0, 0)
    xa, xb = exchange("gx", xa, xb)
    rho_e, sig_e, low_e, high_e, q, table = call(
        functools.partial(spread_kernel, g, zones), "spread", [ext] * 4 + [block, ((2 * nz, 2 * nz), BF16)],
        [SMEM, SMEM] + [VMEM] * 4, (zone_low, zone_high, density, slowness, zone_map, pressure_obs),
    )
    zone_e = jnp.pad(zone_map.astype(F32), ((XO, g.xp - nx - XO), (YO, YO), (0, 0))).reshape(g.ext, nz)
    ya, yb = call(
        functools.partial(sides_kernel, g, 3), "sides", [ymsg(3)] * 2,
        [SMEM] + [VMEM] * 5, (flags, xa, xb, rho_e, sig_e, zone_e),
    )
    ya, yb = exchange("gy", ya, yb)
    outs = call(
        functools.partial(opening_step, g, zones), "opening", [ext] * 4 + [ext, ext, sums_shape, tr_shape, xmsg(2), xmsg(2)],
        [SMEM] * 3 + [VMEM] * 13,
        (flags, zone_low, zone_high, xa, xb, ya, yb, rho_e, sig_e, low_e, high_e, trs, pressure_obs, q, time_obs, table),
        core_scratch,
    )
    rho_e, sig_e, low_e, high_e, grho_e, gsig_e, sums, tr, xa, xb = outs
    history = []
    for iteration in range(1, ITERS):
        last = iteration == ITERS - 1
        sums = lax.all_to_all(sums, both, 0, 0, tiled=True)
        history.append(sums)
        tr = lax.all_to_all(tr, "gx", 0, 0)
        xa, xb = exchange("gx", xa, xb)
        ya, yb = call(
            functools.partial(sides_kernel, g, 2), "sides", [ymsg(2)] * 2,
            [SMEM] + [VMEM] * 4, (flags, xa, xb, grho_e, gsig_e),
        )
        ya, yb = exchange("gy", ya, yb)
        shapes = [ext, ext, tr_shape, ext, ext, sums_shape] + ([] if last else [tr_shape, xmsg(2), xmsg(2)])
        outs = call(
            functools.partial(later_step, g, last), "step", shapes, [SMEM] + [VMEM] * 17,
            (flags, xa, xb, ya, yb, sums, grho_e, gsig_e, tr, rho_e, sig_e, low_e, high_e, trs, pressure_obs, q, time_obs, table),
            core_scratch,
        )
        if last:
            rho_e, sig_e, trs, grho_e, gsig_e, sums = outs
        else:
            rho_e, sig_e, trs, grho_e, gsig_e, sums, tr, xa, xb = outs
    sums = lax.all_to_all(sums, both, 0, 0, tiled=True)
    history.append(sums)
    rho, sigma, obj = call(
        functools.partial(closing_kernel, g), "closing", [block, block, ((8, nz), F32)],
        [VMEM] * 9, (*history, grho_e, gsig_e, rho_e, sig_e, low_e, high_e),
    )
    return rho, sigma, obj[0, :ITERS]


def solution(mesh):
    placed = (P("gx", "gy", None),) * 5 + (P(), P())
    return jax.shard_map(
        local,
        mesh=mesh,
        in_specs=placed,
        out_specs=(P("gx", "gy", None), P("gx", "gy", None), P()),
        check_vma=False,
    )
```

time: 466 us -> 226 us (0.48); the launches traced: 458 us -> 224 us
  blocking collectives: 249 us -> 55.4 us
  other arithmetic: 82.6 us -> 0.16 us
  local copies, waits for them, and re-layouts: 10.7 us -> 73.2 us
  Pallas kernels: 0 us -> 60.2 us
  starting transfers between devices: 64.1 us -> 27.2 us
  matrix products: 26.4 us -> 0 us
  between operations: 16 us -> 0.96 us
    psum x3 -> x0, blocking collectives: 124 us -> none  [global_sums(): return lax.psum((values[0], values[1]), ('gx', 'gy'))]
    all_gather x4 -> x0, blocking collectives: 124 us -> none  [the longest x3 93.6 us: local(): gathered = lax.all_gather(stacked, 'gx', axis=0, tiled=True)]
    unnamed x104 -> x174, local copies, waits for them, and re-layouts: 9.23 us -> 72.6 us
    pallas_call x0 -> x9, Pallas kernels: none -> 60.2 us  [call(): pl.pallas_call(body, name=name, out_shape=[jax.ShapeDtypeStruct(s, d) for...]
    all_to_all x0 -> x3, blocking collectives: none -> 55.4 us  [local(): sums = lax.all_to_all(sums, both, 0, 0, tiled=True)]
    ppermute x24 -> x12, starting transfers between devices: 64.1 us -> 12.5 us  [exchange(): return (lax.ppermute(a, axis, pa), lax.ppermute(b, axis, pb))]
    dot_general x16 -> x0, matrix products: 25 us -> none  [the longest x6 15.1 us: depth_prefix(): jnp.einsum('xyj,jk->xyk', values, table, precision=lax.Precision.HIGHEST)]
    sub x12 -> x0, other arithmetic: 20.8 us -> none  [the longest x3 7.89 us: local(): slowness_now - ETA * grad_slowness * lax.rsqrt(norm_slowness / cells + EP...]
  transfers between devices with their start and end apart: 24 -> 15, of which waited for: 3 -> 5; matrix products, arithmetic and copies ran while one was open for 5% -> 0% of each run, Pallas kernels for 0% -> 2%
where the time goes in v1:
time: 226 us; the launch traced here: 224 us
  local copies, waits for them, and re-layouts  73.2 us (32%)
  Pallas kernels  60.2 us (27%)
  blocking collectives  55.4 us (25%)
  starting transfers between devices  27.2 us (12%)
  waiting for transfers between devices  7.12 us (3%)
    unnamed x174, local copies, waits for them, and re-layouts  72.6 us
    pallas_call x9, Pallas kernels, call(): pl.pallas_call(body, name=name, out_shape=[jax.ShapeDtypeStruct(s, d) for...  60.2 us
    all_to_all x3, blocking collectives, local(): sums = lax.all_to_all(sums, both, 0, 0, tiled=True)  55.4 us
    ppermute x12, starting transfers between devices, exchange(): return (lax.ppermute(a, axis, pa), lax.ppermute(b, axis, pb))  12.5 us
    all_to_all x2, starting transfers between devices, local(): tr = lax.all_to_all(tr, 'gx', 0, 0)  7.45 us
    all_to_all x1, starting transfers between devices, local(): trs = lax.all_to_all(tr, 'gx', 0, 0)  7.28 us
    ppermute x12, waiting for transfers between devices, exchange(): return (lax.ppermute(a, axis, pa), lax.ppermute(b, axis, pb))  7.12 us
  transfers between devices with their start and end apart: 15, of which 5 were waited for; matrix products, arithmetic and copies ran while one was open for 0% of the time, Pallas kernels for 2%

profile of v1, /device:TPU:0, one launch (start us, length us, event | category | flops | bytes accessed | tf_op | source)
XLA Modules:
  0.0 224.2 jit_solution(7453880645418580367)
XLA Ops:
  5.6 1.4 first.1
  8.4 7.3 %all-to-all-start = ((f32[8,64,128]{2,1,0:T(8,128)}), f32[8,64,128]{2,1,0:T(8,128)S(1)}, u32[]{:S(2)}, u32[]{:S(2)}) async-start(f32[8,64,128]{2,1,0:T(8,128)} %copy-done.61), calls=%async_computation | async-start | bytes 524288 | tf_op jit(solution)/shard_map/all_to_all | solution.py:431
  15.6 2.0 collective-permute-start
  17.7 1.5 collective-permute-start.1
  21.1 2.7 %spread.1 = (f32[2880,128]{1,0:T(8,128)S(1)}, f32[2880,128]{1,0:T(8,128)S(1)}, f32[2880,128]{1,0:T(8,128)S(1)}, f32[2880,128]{1,0:T(8,128)S(1)}, f32[64,32,128]{...) custom-call(f32[8]{0:T(128)S(1)} %copy-done.80, f32[8]{0:T(128)S(1)} %copy-done.81, f32[64,32,128]{2,1,0:T(8,128)S(1)} %copy-done.30, ...), custom_call_target="tpu_custom_call" | custom-call | tf_op jit(solution)/shard_map/spread/pallas_call | solution.py:399
  39.0 16.9 %opening.1 = (f32[2880,128]{1,0:T(8,128)S(1)}, f32[2880,128]{1,0:T(8,128)S(1)}, f32[2880,128]{1,0:T(8,128)S(1)}, f32[2880,128]{1,0:T(8,128)S(1)}, f32[2880,128]{...) custom-call(s32[2]{0:T(128)S(1)} %pad_add_fusion.flags, ...), custom_call_target="tpu_custom_call" | custom-call | tf_op jit(solution)/shard_map/opening/pallas_call | solution.py:399
  64.7 18.5 %all_to_all.48 = f32[32,1,128]{2,1,0:T(1,128)S(1)} all-to-all(f32[32,1,128]{2,1,0:T(1,128)S(1)} %bitcast.25), channel_id=1, replica_groups=mesh['gx'=8,'gy'=4] {'gx','gy'}, dimensions={0} | all-to-all | bytes 32768 | tf_op jit(solution)/shard_map/all_to_all | solution.py:453
  83.2 4.0 %all-to-all-start.2 = ((f32[8,64,128]{2,1,0:T(8,128)}), f32[8,64,128]{2,1,0:T(8,128)}, u32[]{:S(2)}, u32[]{:S(2)}) async-start(f32[8,64,128]{2,1,0:T(8,128)} %copy-done.60), calls=%async_computation.2 | async-start | bytes 524288 | tf_op jit(solution)/shard_map/all_to_all | solution.py:455
  87.3 1.9 collective-permute-start.4
  89.1 1.5 collective-permute-start.5
  90.6 2.4 %collective-permute-done.4.xa = f32[128,128]{1,0:T(8,128)S(1)} collective-permute-done((f32[128,128]{1,0:T(8,128)}, f32[128,128]{1,0:T(8,128)S(1)}, u32[]{:S(2)}, u32[]{:S(2)}) %collective-permute-start.4) | collective-permute-done | bytes 65568 | tf_op jit(solution)/shard_map/ppermute | solution.py:391
  93.0 1.4 copy-done.14
  100.0 1.4 copy-done.4
  112.4 17.5 %step.2 = (f32[2880,128]{1,0:T(8,128)S(1)}, f32[2880,128]{1,0:T(8,128)S(1)}, f32[8,64,128]{2,1,0:T(8,128)S(1)}, f32[2880,128]{1,0:T(8,128)S(1)}, f32[2880,128]{1...) custom-call(s32[2]{0:T(128)S(1)} %copy-done.77, ...), custom_call_target="tpu_custom_call" | custom-call | tf_op jit(solution)/shard_map/step/pallas_call | solution.py:399
  137.1 18.5 %all_to_all.49 = f32[32,1,128]{2,1,0:T(1,128)} all-to-all(f32[32,1,128]{2,1,0:T(1,128)S(1)} %bitcast.23), channel_id=1, replica_groups=mesh['gx'=8,'gy'=4] {'gx','gy'}, dimensions={0} | all-to-all | bytes 32768 | tf_op jit(solution)/shard_map/all_to_all | solution.py:453
  155.6 3.4 %all-to-all-start.4 = ((f32[8,64,128]{2,1,0:T(8,128)}), f32[8,64,128]{2,1,0:T(8,128)S(1)}, u32[]{:S(2)}, u32[]{:S(2)}) async-start(f32[8,64,128]{2,1,0:T(8,128)} %copy-done.59), calls=%async_computation.4 | async-start | bytes 524288 | tf_op jit(solution)/shard_map/all_to_all | solution.py:455
  159.0 1.9 collective-permute-start.8
  160.9 1.5 collective-permute-start.9
  162.4 2.6 %collective-permute-done.8.xa = f32[128,128]{1,0:T(8,128)S(1)} collective-permute-done((f32[128,128]{1,0:T(8,128)}, f32[128,128]{1,0:T(8,128)S(1)}, u32[]{:S(2)}, u32[]{:S(2)}) %collective-permute-start.8) | collective-permute-done | bytes 65568 | tf_op jit(solution)/shard_map/ppermute | solution.py:391
  165.0 1.4 copy-done.20
  172.0 1.4 copy-done.5
  186.1 17.5 %step.3 = (f32[2880,128]{1,0:T(8,128)S(1)}, f32[2880,128]{1,0:T(8,128)S(1)}, f32[8,64,128]{2,1,0:T(8,128)}, f32[2880,128]{1,0:T(8,128)S(1)}, f32[2880,128]{1,0:T(8,128)S(1)}, /*index=5*/f32[32,128]{1,0:T(8,128)S(1)}) custom-call(s32[2]{0:T(128)S(1)} %copy-done.79, f32[128,128]{1,0:T(8,128)S(1)} %copy-done.52, f32[128,128]{1,0:T(8,128)S(1)} %copy-done.56, ...), custom_call_target="tpu_custom_call" | custom-call | tf_op jit(solution)/shard_map/step/pallas_call | solution.py:399
  203.6 18.4 %all_to_all.50 = f32[32,1,128]{2,1,0:T(1,128)S(1)} all-to-all(f32[32,1,128]{2,1,0:T(1,128)S(1)} %bitcast.24), channel_id=1, replica_groups=mesh['gx'=8,'gy'=4] {'gx','gy'}, dimensions={0} | all-to-all | bytes 32768 | tf_op jit(solution)/shard_map/all_to_all | solution.py:472
  222.0 1.8 closing.1
  (196 shorter events, 74.6 us)
Async XLA Ops:
  5.6 24.2 %copy-start.75 = (s32[2]{0:T(128)}, s32[2]{0:T(128)S(1)}, u32[]{:S(2)}) copy-start(s32[2]{0:T(128)S(1)} %pad_add_fusion.flags) | copy-start | bytes 28
  5.6 13.6 %copy-start.12 = (s32[64,32,128]{2,1,0:T(8,128)S(1)}, s32[64,32,128]{2,1,0:T(8,128)}, u32[]{:S(2)}) copy-start(s32[64,32,128]{2,1,0:T(8,128)} %zone.3) | copy-start | bytes 3145732
  8.4 21.5 %all-to-all-start = ((f32[8,64,128]{2,1,0:T(8,128)}), f32[8,64,128]{2,1,0:T(8,128)S(1)}, u32[]{:S(2)}, u32[]{:S(2)}) async-start(f32[8,64,128]{2,1,0:T(8,128)} %copy-done.61), calls=%async_computation | async-start | bytes 524288 | tf_op jit(solution)/shard_map/all_to_all | solution.py:431
  15.6 9.3 %collective-permute-start = (f32[192,128]{1,0:T(8,128)}, f32[192,128]{1,0:T(8,128)S(1)}, u32[]{:S(2)}, u32[]{:S(2)}) collective-permute-start(f32[192,128]{1,0:T(8,128)} %get-tuple-element.45), channel_id=1, source_target_pairs={{0,4},{4,0},{8,12},{12,8},{16,20},{20,16},{24,28},{28,24},{1,5},{5... | collective-permute-start | bytes 294920 | tf_op jit(solution)/shard_map/ppermute | solution.py:391
  17.7 7.3 %collective-permute-start.1 = (f32[192,128]{1,0:T(8,128)}, f32[192,128]{1,0:T(8,128)S(1)}, u32[]{:S(2)}, u32[]{:S(2)}) collective-permute-start(f32[192,128]{1,0:T(8,128)} %copy-done.82), channel_id=1, source_target_pairs={{0,0},{4,8},{8,4},{12,16},{16,12},{20,24},{24,20},{28,28},{1,1},{5... | collective-permute-start | bytes 294920 | tf_op jit(solution)/shard_map/ppermute | solution.py:391
  25.0 4.9 %copy-start.1 = (f32[64,32,128]{2,1,0:T(8,128)S(1)}, f32[64,32,128]{2,1,0:T(8,128)}, u32[]{:S(2)}) copy-start(f32[64,32,128]{2,1,0:T(8,128)} %t.7) | copy-start | bytes 3145732
  27.0 1.5 collective-permute-start.2
  27.0 2.2 collective-permute-start.3
  83.2 16.8 %all-to-all-start.2 = ((f32[8,64,128]{2,1,0:T(8,128)}), f32[8,64,128]{2,1,0:T(8,128)}, u32[]{:S(2)}, u32[]{:S(2)}) async-start(f32[8,64,128]{2,1,0:T(8,128)} %copy-done.60), calls=%async_computation.2 | async-start | bytes 524288 | tf_op jit(solution)/shard_map/all_to_all | solution.py:455
  87.3 5.8 %collective-permute-start.4 = (f32[128,128]{1,0:T(8,128)}, f32[128,128]{1,0:T(8,128)S(1)}, u32[]{:S(2)}, u32[]{:S(2)}) collective-permute-start(f32[128,128]{1,0:T(8,128)} %copy-done.86), channel_id=1, source_target_pairs={{0,4},{4,0},{8,12},{12,8},{16,20},{20,16},{24,28},{28,24},{1,5},{5... | collective-permute-start | bytes 196616 | tf_op jit(solution)/shard_map/ppermute | solution.py:391
  89.1 3.9 %collective-permute-start.5 = (f32[128,128]{1,0:T(8,128)}, f32[128,128]{1,0:T(8,128)S(1)}, u32[]{:S(2)}, u32[]{:S(2)}) collective-permute-start(f32[128,128]{1,0:T(8,128)} %copy-done.84), channel_id=1, source_target_pairs={{0,0},{4,8},{8,4},{12,16},{16,12},{20,24},{24,20},{28,28},{1,1},{5... | collective-permute-start | bytes 196616 | tf_op jit(solution)/shard_map/ppermute | solution.py:391
  93.0 4.2 %copy-start.49 = (f32[128,128]{1,0:T(8,128)}, f32[128,128]{1,0:T(8,128)S(1)}, u32[]{:S(2)}) copy-start(f32[128,128]{1,0:T(8,128)S(1)} %collective-permute-done.4.xa) | copy-start | bytes 196612
  93.0 4.2 %copy-start.53 = (f32[128,128]{1,0:T(8,128)}, f32[128,128]{1,0:T(8,128)S(1)}, u32[]{:S(2)}) copy-start(f32[128,128]{1,0:T(8,128)S(1)} %collective-permute-done.5.xb) | copy-start | bytes 196612
  97.3 1.4 collective-permute-start.6
  97.3 2.0 collective-permute-start.7
  155.6 16.4 %all-to-all-start.4 = ((f32[8,64,128]{2,1,0:T(8,128)}), f32[8,64,128]{2,1,0:T(8,128)S(1)}, u32[]{:S(2)}, u32[]{:S(2)}) async-start(f32[8,64,128]{2,1,0:T(8,128)} %copy-done.59), calls=%async_computation.4 | async-start | bytes 524288 | tf_op jit(solution)/shard_map/all_to_all | solution.py:455
  159.0 6.0 %collective-permute-start.8 = (f32[128,128]{1,0:T(8,128)}, f32[128,128]{1,0:T(8,128)S(1)}, u32[]{:S(2)}, u32[]{:S(2)}) collective-permute-start(f32[128,128]{1,0:T(8,128)} %copy-done.85), channel_id=1, source_target_pairs={{0,4},{4,0},{8,12},{12,8},{16,20},{20,16},{24,28},{28,24},{1,5},{5... | collective-permute-start | bytes 196616 | tf_op jit(solution)/shard_map/ppermute | solution.py:391
  160.9 4.0 %collective-permute-start.9 = (f32[128,128]{1,0:T(8,128)}, f32[128,128]{1,0:T(8,128)S(1)}, u32[]{:S(2)}, u32[]{:S(2)}) collective-permute-start(f32[128,128]{1,0:T(8,128)} %copy-done.83), channel_id=1, source_target_pairs={{0,0},{4,8},{8,4},{12,16},{16,12},{20,24},{24,20},{28,28},{1,1},{5... | collective-permute-start | bytes 196616 | tf_op jit(solution)/shard_map/ppermute | solution.py:391
  165.0 4.2 %copy-start.51 = (f32[128,128]{1,0:T(8,128)}, f32[128,128]{1,0:T(8,128)S(1)}, u32[]{:S(2)}) copy-start(f32[128,128]{1,0:T(8,128)S(1)} %collective-permute-done.8.xa) | copy-start | bytes 196612
  165.0 4.2 %copy-start.55 = (f32[128,128]{1,0:T(8,128)}, f32[128,128]{1,0:T(8,128)S(1)}, u32[]{:S(2)}) copy-start(f32[128,128]{1,0:T(8,128)S(1)} %collective-permute-done.9.xb) | copy-start | bytes 196612
  169.2 1.4 collective-permute-start.10
  169.3 2.0 collective-permute-start.11
  186.1 35.9 %copy-start.6 = (f32[2880,128]{1,0:T(8,128)S(1)}, f32[2880,128]{1,0:T(8,128)}, u32[]{:S(2)}) copy-start(f32[2880,128]{1,0:T(8,128)} %copy-done.3) | copy-start | bytes 4423684
  186.1 35.9 %copy-start.10 = (f32[2880,128]{1,0:T(8,128)S(1)}, f32[2880,128]{1,0:T(8,128)}, u32[]{:S(2)}) copy-start(f32[2880,128]{1,0:T(8,128)} %copy-done.7) | copy-start | bytes 4423684
  (78 other events, 86.8 us)

commit v2 on v1

v2 whole, which is shorter than its diff:
```python
import functools
import math

import jax
import jax.numpy as jnp
from jax import lax
from jax.experimental import pallas as pl
from jax.experimental.pallas import tpu as pltpu
from jax.sharding import PartitionSpec as P

ITERS = 3
BETA = 1.0
ETA = 0.5
EPSILON = 1e-06

XO = 2
YO = 4
F32 = jnp.float32
BF16 = jnp.bfloat16


class Geo:
    def __init__(self, nx, ny, nz, px, py):
        self.nx, self.ny, self.nz, self.px, self.py = nx, ny, nz, px, py
        self.pl = ny + 2 * YO
        self.planes = nx + 2 * XO
        self.ext = (nx + 8) * self.pl
        self.xp = nx + 8
        self.cells = float(nx * px * ny * py * nz)
        self.zs = 1.0 / math.sqrt(nz)
        self.xs = 1.0 / math.sqrt(nx * px)
        self.win = (nx + 2) * self.pl + 8
        self.pairs = px // 2

    def own(self, x):
        return (x + XO) * self.pl + YO


def fold8(v):
    total = v[0:8]
    for i in range(8, v.shape[0], 8):
        total = total + v[i : i + 8]
    return total


def pick_sides(even, first, last, a, b):
    low = jnp.where(even, b, a)
    high = jnp.where(even, a, b)
    return jnp.where(first, 0.0, low), jnp.where(last, 0.0, high)


def put_pair(even, low, high, a_ref, b_ref, at):
    n = low.shape[0]
    a_ref[at : at + n, :] = jnp.where(even, high, low)
    b_ref[at : at + n, :] = jnp.where(even, low, high)


def flags_of(g, flags):
    ix, iy = flags[0], flags[1]
    return ((ix % 2) == 0, ix == 0, ix == g.px - 1), ((iy % 2) == 0, iy == 0, iy == g.py - 1)


def split2(v):
    high = v.astype(BF16)
    low = (v - high.astype(F32)).astype(BF16)
    return jnp.concatenate([high, low], axis=1)


def bounds_of(zones, z, zlow, zhigh):
    low = jnp.full(z.shape, zlow[0], F32)
    high = jnp.full(z.shape, zhigh[0], F32)
    for i in range(1, zones):
        hit = z == i
        low = jnp.where(hit, zlow[i], low)
        high = jnp.where(hit, zhigh[i], high)
    return low, high


def first_kernel(g, flags, rho, sigma, zone, t, own, xa, xb, rims, zrims, sig_v, t_v, sems):
    (even, _, _), _ = flags_of(g, flags)
    step = 8
    small = []
    for k, at in enumerate((0, g.nx - 2)):
        small.append(pltpu.make_async_copy(rho.at[pl.ds(at, 2)], rims.at[k, 0], sems.at[2 * k]))
        small.append(pltpu.make_async_copy(zone.at[pl.ds(at, 2)], zrims.at[k], sems.at[2 * k + 1]))
    big = []
    for c in range(g.nx // step):
        at = pl.ds(c * step, step)
        big.append((
            pltpu.make_async_copy(sigma.at[at], sig_v.at[at], sems.at[4 + 2 * c]),
            pltpu.make_async_copy(t.at[at], t_v.at[at], sems.at[5 + 2 * c]),
        ))
    for a, b in big:
        a.start()
        b.start()
    for copy in small:
        copy.start()
    zero = jnp.zeros((g.ny, g.nz), F32)
    run, total, seen = zero, zero, zero
    for c, (a, b) in enumerate(big):
        a.wait()
        b.wait()
        for k in range(step):
            run = run + sig_v[c * step + k]
            total = total + run
            seen = seen + t_v[c * step + k]
    own[0 : g.ny, :] = run
    own[g.ny : 2 * g.ny, :] = total * g.xs - seen
    for copy in small:
        copy.wait()
    at = 0
    for r in range(2):
        put_pair(even, rims[0, 0, r], rims[1, 0, r], xa, xb, at)
        at += g.ny
    for r in range(2):
        put_pair(even, sig_v[r], sig_v[g.nx - 2 + r], xa, xb, at)
        at += g.ny
    for r in range(2):
        put_pair(even, zrims[0, r].astype(F32), zrims[1, r].astype(F32), xa, xb, at)
        at += g.ny
    xa[at : at + g.ny, :] = run
    xa[at + g.ny : at + 2 * g.ny, :] = total * g.xs - seen


def spread_kernel(g, zones, zlow, zhigh, zone, p, low_o, high_o, q, table, ztable):
    nz = g.nz
    row = lax.broadcasted_iota(jnp.int32, (2 * nz, 2 * nz), 0) % nz
    col = lax.broadcasted_iota(jnp.int32, (2 * nz, 2 * nz), 1)
    first = (row <= col).astype(F32)
    second = (nz - jnp.maximum(row, col - nz)).astype(F32)
    table[...] = jnp.where(col < nz, first, second).astype(BF16)
    r2 = lax.broadcasted_iota(jnp.int32, (2 * nz, nz), 0) % nz
    c2 = lax.broadcasted_iota(jnp.int32, (2 * nz, nz), 1)
    back = (r2 >= c2).astype(F32).astype(BF16)
    ztable[...] = ((r2 == c2 + 1).astype(F32) - (r2 == c2 - 1).astype(F32)).astype(BF16)
    step = 8

    def body(c, carry):
        for k in range(step):
            x = c * step + k
            low_o[x], high_o[x] = bounds_of(zones, zone[x], zlow, zhigh)
        rows = p[pl.ds(c * step, step)].reshape(step * g.ny, nz)
        out = jnp.dot(split2(rows), back, preferred_element_type=F32) * g.zs
        q[pl.ds(c * step, step)] = out.reshape(step, g.ny, nz)
        return carry

    lax.fori_loop(0, g.nx // step, body, 0)


def sides_kernel(g, fields, flags, xa, xb, own, order, *refs):
    blocks, (ya, yb, pair) = refs[:fields], refs[fields:]
    (xeven, xfirst, xlast), (yeven, _, _) = flags_of(g, flags)
    n = g.xp
    for f in range(fields):
        for r in range(2):
            low = blocks[f][pl.ds(r, g.nx, stride=g.ny), :].astype(F32)
            high = blocks[f][pl.ds(g.ny - 2 + r, g.nx, stride=g.ny), :].astype(F32)
            put_pair(yeven, low, high, ya, yb, (f * 2 + r) * n + XO)
    for f in range(fields):
        for px in range(2):
            at = (f * 2 + px) * g.ny
            sides = pick_sides(xeven, xfirst, xlast, xa[at : at + g.ny, :], xb[at : at + g.ny, :])
            for plane, value in zip((px, XO + g.nx + px), sides):
                for r in range(2):
                    spot = (f * 2 + r) * n + plane
                    put_pair(yeven, value[r : r + 1], value[g.ny - 2 + r : g.ny - 1 + r], ya, yb, spot)
    at = fields * 2 * g.ny
    mine_t, mine_s = own[0 : g.ny, :], own[g.ny : 2 * g.ny, :]
    other_t, other_s = xa[at : at + g.ny, :], xa[at + g.ny : at + 2 * g.ny, :]
    pair[0 : g.ny, :] = mine_t + other_t
    pair[g.ny : 2 * g.ny, :] = mine_s + other_s + jnp.where(xeven, mine_t, other_t) * (g.nx * g.xs)


def halo_slots(g):
    xs = []
    for r in range(2):
        xs.append((r * g.ny, pl.ds(r * g.pl + YO, g.ny), pl.ds((XO + g.nx + r) * g.pl + YO, g.ny)))
    ys = []
    for r in range(2):
        ys.append((r * g.xp, pl.ds(YO - 2 + r, g.xp, stride=g.pl), pl.ds(YO + g.ny + r, g.xp, stride=g.pl)))
    return xs, ys


def halo_values(g, flags, field, xa, xb, ya, yb):
    (xeven, xfirst, xlast), (yeven, yfirst, ylast) = flags_of(g, flags)
    xs, ys = halo_slots(g)
    for axis, slots, n, a, b, even, first, last in (
        (0, xs, g.ny, xa, xb, xeven, xfirst, xlast),
        (1, ys, g.xp, ya, yb, yeven, yfirst, ylast),
    ):
        for at, low_rows, high_rows in slots:
            here = pl.ds(field * 2 * n + at, n)
            low, high = pick_sides(even, first, last, a[here, :], b[here, :])
            yield axis, 0, at, low_rows, low
            yield axis, 1, at, high_rows, high


def lane_value(row, lane):
    ids = lax.broadcasted_iota(jnp.int32, row.shape, 1)
    return jnp.sum(jnp.where(ids == lane, row, 0.0), axis=1, keepdims=True)


def alphas(g, sums):
    row = jnp.sum(sums[...], axis=0, keepdims=True)
    return tuple(ETA * lax.rsqrt(lane_value(row, k) / g.cells + EPSILON) for k in range(2))


def ray_offsets(g, flags, trs):
    ix = flags[0]
    q = ix // 2
    even = (ix % 2) == 0
    ny = g.ny
    mine, other = trs[0, 0:ny, :], trs[1, 0:ny, :]
    reach = float(g.nx * g.xs)
    before = jnp.where(even, 0.0, other)
    sums = jnp.zeros_like(mine)
    spread = (mine + other) * (g.pairs - 1 - q).astype(F32)
    for m in range(1, g.pairs):
        p = q ^ m
        total = trs[1 + m, 0:ny, :]
        before = before + jnp.where(p < q, total, 0.0)
        sums = sums + jnp.where(p > q, trs[1 + m, ny : 2 * ny, :], 0.0)
        spread = spread + total * (g.pairs - 1 - jnp.maximum(p, q)).astype(F32)
    near = jnp.where(even, trs[1, ny : 2 * ny, :] + (before + mine) * reach, 0.0)
    return before, near + sums + spread * (2.0 * reach)


def step_core(g, flags, update, rho_e, sig_e, trs, p, q, t, table, ztable, outs, scratch):
    grho, gsig, sums, own, xa, xb = outs
    vxr, vxs, vyr, vys, vzr, vzs, gyr, gys, rt_s, az, bz, yu, ym = scratch
    nx, ny, nz, w = g.nx, g.ny, g.nz, g.pl
    (even, _, _), _ = flags_of(g, flags)
    zero = jnp.zeros((ny, nz), F32)
    zero8 = jnp.zeros((8, nz), F32)
    before, after = ray_offsets(g, flags, trs)
    step = 8
    rows = step * w

    def zdiff(v):
        return jnp.dot(split2(v), ztable[...], preferred_element_type=F32)

    edge = [ref[pl.ds(k * w, w), :] for ref in (rho_e, sig_e) for k in (1, XO + nx)]
    out = zdiff(jnp.concatenate(edge, axis=0))
    for i, (ref, k) in enumerate(((az, 1), (az, XO + nx), (bz, 1), (bz, XO + nx))):
        ref[pl.ds(k * w, w), :] = out[i * w : (i + 1) * w]

    def fields(c, carry):
        run, acc = carry
        for k in range(step):
            x = c * step + k
            at = pl.ds(g.own(x), ny)
            rho, sig = update(x, at)
            rho_e[at, :] = rho
            sig_e[at, :] = sig
            run = run + sig
            miss = run * g.xs - t[x]
            rt_s[pl.ds(x * ny, ny), :] = miss
            acc = acc + fold8(miss * miss)
        at = pl.ds((c * step + XO) * w, rows)
        pieces = split2(rho_e[at, :])
        az[at, :] = jnp.dot(pieces, ztable[...], preferred_element_type=F32)
        y = jnp.dot(pieces, table[...], preferred_element_type=F32)
        yu[at, :] = y[:, :nz]
        ym[at, :] = y[:, nz:]
        bz[at, :] = zdiff(sig_e[at, :])
        return run, acc

    _, acc_t = lax.fori_loop(0, nx // step, fields, (before, zero8))

    rowid = lax.broadcasted_iota(jnp.int32, (w, nz), 0)
    mine = jnp.logical_and(rowid >= 1, rowid <= ny)

    def slopes(ref, z, base):
        sx = ref[pl.ds(base + w, w), :] - ref[pl.ds(base - w, w), :]
        sy = ref[pl.ds(base + 1, w), :] - ref[pl.ds(base - 1, w), :]
        return sx, sy, z[pl.ds(base, w), :]

    def cross_plane(xi, acc, inside):
        base = (xi + XO - 1) * w + YO - 1
        a0, a1, a2 = slopes(rho_e, az, base)
        b0, b1, b2 = slopes(sig_e, bz, base)
        c0 = a1 * b2 - a2 * b1
        c1 = a2 * b0 - a0 * b2
        c2 = a0 * b1 - a1 * b0
        at = pl.ds(pl.multiple_of(xi * w, 8), w)
        vxr[at, :] = b1 * c2 - b2 * c1
        vxs[at, :] = c1 * a2 - c2 * a1
        if not inside:
            return acc
        vyr[at, :] = b2 * c0 - b0 * c2
        vys[at, :] = c2 * a0 - c0 * a2
        vzr[at, :] = b0 * c1 - b1 * c0
        vzs[at, :] = c0 * a1 - c1 * a0
        return acc + fold8(jnp.where(mine, c0 * c0 + c1 * c1 + c2 * c2, 0.0))

    cross_plane(0, None, False)
    cross_plane(nx + 1, None, False)
    acc_c = lax.fori_loop(1, nx + 1, lambda xi, acc: cross_plane(xi, acc, True), zero8, unroll=2)

    def adjoints(c, carry):
        start = (1 + c * step) * w
        at = pl.ds(pl.multiple_of(start, 8), rows)
        for vy, vz, out in ((vyr, vzr, gyr), (vys, vzs, gys)):
            along_y = vy[pl.ds(start - 1, rows), :] - vy[pl.ds(start + 1, rows), :]
            out[at, :] = along_y - zdiff(vz[at, :])
        return carry

    lax.fori_loop(0, nx // step, adjoints, 0)

    def gradients(i, carry):
        back, sum_t, sum_r, nr, ns, acc = carry
        x = nx - 1 - i
        lower = pl.ds(x * w + 1, ny)
        here = pl.ds((x + 1) * w + 1, ny)
        upper = pl.ds((x + 2) * w + 1, ny)
        at = pl.ds(g.own(x), ny)
        cr = (vxr[lower, :] - vxr[upper, :] + gyr[here, :]) * (BETA / 16.0)
        cs = (vxs[lower, :] - vxs[upper, :] + gys[here, :]) * (BETA / 16.0)
        back = back + rt_s[pl.ds(x * ny, ny), :]
        miss = yu[at, :] * g.zs - p[x]
        gr = ym[at, :] * (g.zs * g.zs) - q[x] + cr
        gs = back * g.xs + cs
        out = pl.ds(pl.multiple_of(x * ny, 8), ny)
        grho[out, :] = gr
        gsig[out, :] = gs
        weight = (i + 1).astype(F32)
        return (back, sum_t + gs, sum_r + gs * weight, nr + fold8(gr * gr), ns + fold8(gs * gs),
                acc + fold8(miss * miss))

    start = (after, zero, zero, zero8, zero8, zero8)
    _, sum_t, sum_r, nr, ns, acc_p = lax.fori_loop(0, nx, gradients, start, unroll=4)

    total = lambda v: jnp.sum(jnp.sum(v, axis=0, keepdims=True), axis=1, keepdims=True)
    lane = lax.broadcasted_iota(jnp.int32, sums.shape, 1)
    obj = acc_t + acc_p + acc_c * (BETA / 16.0)
    sums[...] = jnp.where(lane == 0, total(nr), jnp.where(lane == 1, total(ns), jnp.where(lane == 2, total(obj), 0.0)))
    if own is not None:
        rest = sum_r * g.xs
        pos = 0
        for block in (grho, gsig):
            for r in range(2):
                put_pair(even, block[pl.ds(r * ny, ny), :], block[pl.ds((nx - 2 + r) * ny, ny), :], xa, xb, pos)
                pos += ny
        for ref, at in ((own, 0), (xa, pos)):
            ref[at : at + ny, :] = sum_t
            ref[at + ny : at + 2 * ny, :] = rest


def opening_step(g, zones, flags, zlow, zhigh, xa, xb, ya, yb, own, rho, sig, p, q, t, table, ztable, *refs):
    others, rest = refs[: g.pairs - 1], refs[g.pairs - 1 :]
    rho_e, sig_e, trs, xlow, xhigh, ylow, yhigh = rest[:7]
    ny = g.ny
    for f, ext in ((0, rho_e), (1, sig_e)):
        for axis, side, at, spot, value in halo_values(g, flags, f, xa, xb, ya, yb):
            ext[spot, :] = value
    for axis, side, at, spot, value in halo_values(g, flags, 2, xa, xb, ya, yb):
        low, high = bounds_of(zones, value, zlow, zhigh)
        lows, highs = ((xlow, xhigh), (ylow, yhigh))[axis]
        lows[side, pl.ds(at, value.shape[0]), :] = low
        highs[side, pl.ds(at, value.shape[0]), :] = high
    pos = 6 * ny
    trs[0] = own[...]
    trs[1] = xa[pos : pos + 2 * ny, :]
    for m, other in enumerate(others):
        trs[2 + m] = other[...]
    step_core(g, flags, lambda x, at: (rho[x], sig[x]), rho_e, sig_e, trs, p, q, t, table, ztable, rest[7:13], rest[13:])


def later_step(g, last, flags, xa, xb, ya, yb, sums_i, own_i, grho_i, gsig_i, rho_i, sig_i, low, high,
               xlow, xhigh, ylow, yhigh, trs_i, p, q, t, table, ztable, *refs):
    others, rest = refs[: g.pairs - 1], refs[g.pairs - 1 :]
    rho_e, sig_e, trs = rest[:3]
    ny = g.ny
    ar, asig = alphas(g, sums_i)
    for axis, side, at, spot, value in halo_values(g, flags, 0, xa, xb, ya, yb):
        lows, highs = ((xlow, xhigh), (ylow, yhigh))[axis]
        here = pl.ds(at, value.shape[0])
        moved = rho_i[spot, :] - ar * value
        rho_e[spot, :] = jnp.minimum(jnp.maximum(moved, lows[side, here, :]), highs[side, here, :])
    for axis, side, at, spot, value in halo_values(g, flags, 1, xa, xb, ya, yb):
        sig_e[spot, :] = sig_i[spot, :] - asig * value
    pos = 4 * ny
    trs[0] = trs_i[0] - asig * own_i[...]
    trs[1] = trs_i[1] - asig * xa[pos : pos + 2 * ny, :]
    for m, other in enumerate(others):
        trs[2 + m] = trs_i[2 + m] - asig * other[...]

    def update(x, at):
        here = pl.ds(pl.multiple_of(x * ny, 8), ny)
        moved = rho_i[at, :] - ar * grho_i[here, :]
        return jnp.minimum(jnp.maximum(moved, low[x]), high[x]), sig_i[at, :] - asig * gsig_i[here, :]

    if last:
        outs, scratch = (*rest[3:6], None, None, None), rest[6:]
    else:
        outs, scratch = rest[3:9], rest[9:]
    step_core(g, flags, update, rho_e, sig_e, trs, p, q, t, table, ztable, outs, scratch)


def closing_kernel(g, sums0, sums1, sums2, grho, gsig, rho_e, sig_e, low, high, rho_o, sig_o, obj):
    ar, asig = alphas(g, sums2)

    def body(x, carry):
        at = pl.ds(g.own(x), g.ny)
        here = pl.ds(pl.multiple_of(x * g.ny, 8), g.ny)
        rho_o[x] = jnp.minimum(jnp.maximum(rho_e[at, :] - ar * grho[here, :], low[x]), high[x])
        sig_o[x] = sig_e[at, :] - asig * gsig[here, :]
        return carry

    lax.fori_loop(0, g.nx, body, 0, unroll=4)
    lane = lax.broadcasted_iota(jnp.int32, obj.shape, 1)
    total = jnp.zeros(obj.shape, F32)
    for k, sums in enumerate((sums0, sums1, sums2)):
        row = jnp.sum(sums[...], axis=0, keepdims=True)
        total = jnp.where(lane == k, lane_value(row, 2) * (0.5 / g.cells), total)
    obj[...] = total


def pairs_of(size):
    a = [(i, i ^ 1) for i in range(size)]
    b = [(i, i if i in (0, size - 1) else ((i + 1) ^ 1) - 1) for i in range(size)]
    return a, b


def exchange(axis, a, b):
    pa, pb = pairs_of(lax.axis_size(axis))
    return lax.ppermute(a, axis, pa), lax.ppermute(b, axis, pb)


def pair_totals(pair, size):
    return [lax.ppermute(pair, "gx", [(i, i ^ (2 * m)) for i in range(size)]) for m in range(1, size // 2)]


SMEM = pl.BlockSpec(memory_space=pltpu.SMEM)
VMEM = pl.BlockSpec(memory_space=pltpu.VMEM)
HBM = pl.BlockSpec(memory_space=pltpu.HBM)


def call(body, name, shapes, specs, args, scratch=(), limit=12):
    return pl.pallas_call(
        body,
        name=name,
        out_shape=[jax.ShapeDtypeStruct(s, d) for s, d in shapes],
        in_specs=specs,
        out_specs=[VMEM] * len(shapes),
        scratch_shapes=list(scratch),
        compiler_params=pltpu.CompilerParams(vmem_limit_bytes=limit * 1024 * 1024),
    )(*args)


def local(density, slowness, pressure_obs, time_obs, zone_map, zone_low, zone_high):
    nx, ny, nz = density.shape
    px, py = lax.axis_size("gx"), lax.axis_size("gy")
    g = Geo(nx, ny, nz, px, py)
    zones = zone_low.shape[0]
    both = ("gx", "gy")
    flags = jnp.stack([lax.axis_index("gx"), lax.axis_index("gy")]).astype(jnp.int32)

    ext = ((g.ext, nz), F32)
    own_shape = ((2 * ny, nz), F32)
    trs_shape = ((g.pairs + 1, 2 * ny, nz), F32)
    sums_shape = ((px * py, nz), F32)
    block = ((nx, ny, nz), F32)
    flat = ((nx * ny, nz), F32)
    xa_shape = lambda f: (((f + 1) * 2 * ny, nz), F32)
    xb_shape = lambda f: ((f * 2 * ny, nz), F32)
    ymsg = lambda f: ((f * 2 * g.xp, nz), F32)
    xbound = ((2, 2 * ny, nz), F32)
    ybound = ((2, 2 * g.xp, nz), F32)
    win = pltpu.VMEM((g.win, nz), F32)
    ext_v = pltpu.VMEM((g.ext, nz), F32)
    core_scratch = [win] * 8 + [pltpu.VMEM((nx * ny, nz), F32)] + [ext_v] * 4

    own, xa, xb = call(
        functools.partial(first_kernel, g), "first", [own_shape, xa_shape(3), xb_shape(3)],
        [SMEM] + [HBM] * 4, (flags, density, slowness, zone_map, time_obs),
        [pltpu.VMEM((2, 1, 2, ny, nz), F32), pltpu.VMEM((2, 2, ny, nz), jnp.int32),
         pltpu.VMEM((nx, ny, nz), F32), pltpu.VMEM((nx, ny, nz), F32), pltpu.SemaphoreType.DMA((4 + nx // 4,))],
    )
    xa, xb = exchange("gx", xa, xb)
    low, high, q, table, ztable = call(
        functools.partial(spread_kernel, g, zones), "spread",
        [block] * 3 + [((2 * nz, 2 * nz), BF16), ((2 * nz, nz), BF16)],
        [SMEM, SMEM] + [VMEM] * 2, (zone_low, zone_high, zone_map, pressure_obs),
    )
    as_rows = lambda v: v.reshape(nx * ny, nz)
    ya, yb, pair = call(
        functools.partial(sides_kernel, g, 3), "sides", [ymsg(3)] * 2 + [own_shape],
        [SMEM] + [VMEM] * 7, (flags, xa, xb, own, table, as_rows(density), as_rows(slowness), as_rows(zone_map)),
    )
    ya, yb = exchange("gy", ya, yb)
    others = pair_totals(pair, px)
    ends = [flat, flat, sums_shape, own_shape, xa_shape(2), xb_shape(2)]
    outs = call(
        functools.partial(opening_step, g, zones), "opening",
        [ext, ext, trs_shape, xbound, xbound, ybound, ybound] + ends,
        [SMEM] * 3 + [VMEM] * (12 + len(others)),
        (flags, zone_low, zone_high, xa, xb, ya, yb, own, density, slowness, pressure_obs, q, time_obs, table, ztable, *others),
        core_scratch, 24,
    )
    rho_e, sig_e, trs, xlow, xhigh, ylow, yhigh, grho, gsig, sums, own, xa, xb = outs
    history = []
    for iteration in range(1, ITERS):
        last = iteration == ITERS - 1
        xa, xb = exchange("gx", xa, xb)
        sums = lax.all_to_all(sums, both, 0, 0, tiled=True)
        history.append(sums)
        ya, yb, pair = call(
            functools.partial(sides_kernel, g, 2), "sides", [ymsg(2)] * 2 + [own_shape],
            [SMEM] + [VMEM] * 6, (flags, xa, xb, own, sums, grho, gsig),
        )
        ya, yb = exchange("gy", ya, yb)
        others = pair_totals(pair, px)
        outs = call(
            functools.partial(later_step, g, last), "step", [ext, ext, trs_shape] + (ends[:3] if last else ends),
            [SMEM] + [VMEM] * (22 + len(others)),
            (flags, xa, xb, ya, yb, sums, own, grho, gsig, rho_e, sig_e, low, high, xlow, xhigh, ylow, yhigh, trs,
             pressure_obs, q, time_obs, table, ztable, *others),
            core_scratch, 24,
        )
        rho_e, sig_e, trs, grho, gsig, sums = outs[:6]
        if not last:
            own, xa, xb = outs[6:]
    sums = lax.all_to_all(sums, both, 0, 0, tiled=True)
    history.append(sums)
    rho, sigma, obj = call(
        functools.partial(closing_kernel, g), "closing", [block, block, ((8, nz), F32)],
        [VMEM] * 9, (*history, grho, gsig, rho_e, sig_e, low, high),
    )
    return rho, sigma, obj[0, :ITERS]


def solution(mesh):
    placed = (P("gx", "gy", None),) * 5 + (P(), P())
    return jax.shard_map(
        local,
        mesh=mesh,
        in_specs=placed,
        out_specs=(P("gx", "gy", None), P("gx", "gy", None), P()),
        check_vma=False,
    )
```

time: 226 us -> 121 us (0.54)
  local copies, waits for them, and re-layouts: 73.2 us -> 5.44 us
  Pallas kernels: 60.2 us -> 36.8 us
  blocking collectives: 55.4 us -> 43.1 us
  waiting for transfers between devices: 7.12 us -> 9.55 us
    unnamed x174 -> x20, local copies, waits for them, and re-layouts: 72.6 us -> 4.92 us
    pallas_call x9, Pallas kernels: 60.2 us -> 36.8 us  [call(): pl.pallas_call(body, name=name, out_shape=[jax.ShapeDtypeStruct(s, d) for...]
    ppermute x0 -> x9, starting transfers between devices: none -> 17.1 us  [pair_totals(): lax.ppermute(pair, 'gx', [(i, i ^ 2 * m) for i in range(size)])]
    all_to_all x3 -> x0, starting transfers between devices: 14.7 us -> none  [the longest x2 7.45 us: local(): tr = lax.all_to_all(tr, 'gx', 0, 0)]
    all_to_all x3, blocking collectives: 55.4 us -> 43.1 us  [local(): sums = lax.all_to_all(sums, both, 0, 0, tiled=True)]
    ppermute x0 -> x9, waiting for transfers between devices: none -> 9.43 us  [pair_totals(): lax.ppermute(pair, 'gx', [(i, i ^ 2 * m) for i in range(size)])]
    ppermute x12, waiting for transfers between devices: 7.12 us -> 0.11 us  [exchange(): return (lax.ppermute(a, axis, pa), lax.ppermute(b, axis, pb))]
    ppermute x12, starting transfers between devices: 12.5 us -> 7.84 us  [exchange(): return (lax.ppermute(a, axis, pa), lax.ppermute(b, axis, pb))]
  transfers between devices with their start and end apart: 15 -> 21, of which waited for: 5 -> 7; matrix products, arithmetic and copies ran while one was open for 0% -> 0% of each run, Pallas kernels for 2% -> 2%
where the time goes in v2:
time: 121 us
  blocking collectives  43.1 us (36%)
  Pallas kernels  36.8 us (30%)
  starting transfers between devices  25 us (21%)
  waiting for transfers between devices  9.55 us (8%)
  local copies, waits for them, and re-layouts  5.44 us (4%)
    all_to_all x3, blocking collectives, local(): sums = lax.all_to_all(sums, both, 0, 0, tiled=True)  43.1 us
    pallas_call x9, Pallas kernels, call(): pl.pallas_call(body, name=name, out_shape=[jax.ShapeDtypeStruct(s, d) for...  36.8 us
    ppermute x9, starting transfers between devices, pair_totals(): lax.ppermute(pair, 'gx', [(i, i ^ 2 * m) for i in range(size)])  17.1 us
    ppermute x9, waiting for transfers between devices, pair_totals(): lax.ppermute(pair, 'gx', [(i, i ^ 2 * m) for i in range(size)])  9.43 us
    ppermute x12, starting transfers between devices, exchange(): return (lax.ppermute(a, axis, pa), lax.ppermute(b, axis, pb))  7.84 us
    unnamed x20, local copies, waits for them, and re-layouts  4.92 us
  transfers between devices with their start and end apart: 21, of which 7 were waited for; matrix products, arithmetic and copies ran while one was open for 0% of the time, Pallas kernels for 2%

profile of v2, /device:TPU:0, one launch (start us, length us, event | category | flops | bytes accessed | tf_op | source)
XLA Modules:
  0.0 120.8 jit_solution(2659566894945342011)
XLA Ops:
  0.7 1.2 %copy-done = f32[64,32,128]{2,1,0:T(8,128)S(1)} copy-done((f32[64,32,128]{2,1,0:T(8,128)S(1)}, f32[64,32,128]{2,1,0:T(8,128)}, u32[]{:S(2)}) %copy-start) | copy-done | bytes 1048600
  1.9 1.2 %copy-done.3 = s32[64,32,128]{2,1,0:T(8,128)S(1)} copy-done((s32[64,32,128]{2,1,0:T(8,128)S(1)}, s32[64,32,128]{2,1,0:T(8,128)}, u32[]{:S(2)}) %copy-start.3) | copy-done | bytes 1048600
  4.4 1.2 %copy-done.6 = f32[64,32,128]{2,1,0:T(8,128)S(1)} copy-done((f32[64,32,128]{2,1,0:T(8,128)S(1)}, f32[64,32,128]{2,1,0:T(8,128)}, u32[]{:S(2)}) %copy-start.6) | copy-done | bytes 1048600
  5.6 3.8 %first.1 = (f32[64,128]{1,0:T(8,128)S(1)}, f32[256,128]{1,0:T(8,128)S(1)}, f32[192,128]{1,0:T(8,128)S(1)}) custom-call(s32[2]{0:T(128)S(1)} %pad_add_fusion.flags, f32[64,32,128]{2,1,0:T(8,128)S(1)} %copy-done.4, f32[64,32,128]{2,1,0:T(8,128)S(1)} %copy-done.6, s32[64,32,128]{2,1,0:T(8,128)S(1)} %copy-done.3, f32[64,32,128]{2,1,0:T(8,128)S(1)} %copy-done), custom_call_target="tpu_custom_call" | custom-call | tf_op jit(solution)/shard_map/first/pallas_call | solution.py:440
  9.4 3.0 %collective-permute-start = (f32[256,128]{1,0:T(8,128)S(1)}, f32[256,128]{1,0:T(8,128)S(1)}, u32[]{:S(2)}, u32[]{:S(2)}) collective-permute-start(f32[256,128]{1,0:T(8,128)S(1)} %get-tuple-element.50), channel_id=1, source_target_pairs={{0,4},{4,0},{8,12},{12,8},{16,20},{20,16},{24,28},{28,24},{1,5},{5... | collective-permute-start | bytes 393224 | tf_op jit(solution)/shard_map/ppermute | solution.py:427
  13.1 2.7 %spread.1 = (f32[64,32,128]{2,1,0:T(8,128)S(1)}, f32[64,32,128]{2,1,0:T(8,128)S(1)}, f32[64,32,128]{2,1,0:T(8,128)S(1)}, bf16[256,256]{1,0:T(8,128)(2,1)S(1)}, bf16[256,128]{1,0:T(8,128)(2,1)S(1)}) custom-call(f32[8]{0:T(128)S(1)} %copy-done.8, f32[8]{0:T(128)S(1)} %copy-done.9, s32[64,32,128]{2,1,0:T(8,128)S(1)} %copy-done.3, f32[64,32,128]{2,1,0:T(8,128)S(1)} %copy-done.2), custom_call_target="tpu_custom_call" | custom-call | tf_op jit(solution)/shard_map/spread/pallas_call | solution.py:440
  17.5 7.6 %collective-permute-start.6 = (f32[64,128]{1,0:T(8,128)S(1)}, f32[64,128]{1,0:T(8,128)S(1)}, u32[]{:S(2)}, u32[]{:S(2)}) collective-permute-start(f32[64,128]{1,0:T(8,128)S(1)} %get-tuple-element.58), channel_id=1, source_target_pairs={{0,24},{4,28},{8,16},{12,20},{16,8},{20,12},{24,0},{28,4},{1,25},{... | collective-permute-start | bytes 98312 | tf_op jit(solution)/shard_map/ppermute | solution.py:431
  25.7 1.3 %collective-permute-done.6.refs_2_ = f32[64,128]{1,0:T(8,128)S(1)} collective-permute-done((f32[64,128]{1,0:T(8,128)S(1)}, f32[64,128]{1,0:T(8,128)S(1)}, u32[]{:S(2)}, u32[]{:S(2)}) %collective-permute-start.6) | collective-permute-done | bytes 32800 | tf_op jit(solution)/shard_map/ppermute | solution.py:431
  27.0 2.9 %collective-permute-done.5.refs_1_ = f32[64,128]{1,0:T(8,128)S(1)} collective-permute-done((f32[64,128]{1,0:T(8,128)S(1)}, f32[64,128]{1,0:T(8,128)S(1)}, u32[]{:S(2)}, u32[]{:S(2)}) %collective-permute-start.5) | collective-permute-done | bytes 32800 | tf_op jit(solution)/shard_map/ppermute | solution.py:431
  29.9 8.7 %opening.1 = (f32[2880,128]{1,0:T(8,128)S(1)}, f32[2880,128]{1,0:T(8,128)S(1)}, f32[5,64,128]{2,1,0:T(8,128)S(1)}, f32[2,64,128]{2,1,0:T(8,128)S(1)}, f32[2,64,1...) custom-call(s32[2]{0:T(128)S(1)} %pad_add_fusion.flags, ...), custom_call_target="tpu_custom_call" | custom-call | tf_op jit(solution)/shard_map/opening/pallas_call | solution.py:440
  39.3 16.3 %all_to_all.33 = f32[32,1,128]{2,1,0:T(1,128)S(1)} all-to-all(f32[32,1,128]{2,1,0:T(1,128)S(1)} %bitcast.30), channel_id=1, replica_groups=mesh['gx'=8,'gy'=4] {'gx','gy'}, dimensions={0} | all-to-all | bytes 32768 | tf_op jit(solution)/shard_map/all_to_all | solution.py:506
  57.7 1.5 %collective-permute-start.12 = (f32[64,128]{1,0:T(8,128)S(1)}, f32[64,128]{1,0:T(8,128)S(1)}, u32[]{:S(2)}, u32[]{:S(2)}) collective-permute-start(f32[64,128]{1,0:T(8,128)S(1)} %get-tuple-element.76), channel_id=1, source_target_pairs={{0,16},{4,20},{8,24},{12,28},{16,0},{20,4},{24,8},{28,12},{1,17},{... | collective-permute-start | bytes 98312 | tf_op jit(solution)/shard_map/ppermute | solution.py:431
  59.2 2.4 %collective-permute-start.11 = (f32[64,128]{1,0:T(8,128)S(1)}, f32[64,128]{1,0:T(8,128)S(1)}, u32[]{:S(2)}, u32[]{:S(2)}) collective-permute-start(f32[64,128]{1,0:T(8,128)S(1)} %get-tuple-element.76), channel_id=1, source_target_pairs={{0,8},{4,12},{8,0},{12,4},{16,24},{20,28},{24,16},{28,20},{1,9},{5... | collective-permute-start | bytes 98312 | tf_op jit(solution)/shard_map/ppermute | solution.py:431
  61.5 1.3 %collective-permute-done.13.refs_2_ = f32[64,128]{1,0:T(8,128)S(1)} collective-permute-done((f32[64,128]{1,0:T(8,128)S(1)}, f32[64,128]{1,0:T(8,128)S(1)}, u32[]{:S(2)}, u32[]{:S(2)}) %collective-permute-start.13) | collective-permute-done | bytes 32800 | tf_op jit(solution)/shard_map/ppermute | solution.py:431
  62.9 1.3 %collective-permute-done.11.refs_0_ = f32[64,128]{1,0:T(8,128)S(1)} collective-permute-done((f32[64,128]{1,0:T(8,128)S(1)}, f32[64,128]{1,0:T(8,128)S(1)}, u32[]{:S(2)}, u32[]{:S(2)}) %collective-permute-start.11) | collective-permute-done | bytes 32800 | tf_op jit(solution)/shard_map/ppermute | solution.py:431
  64.1 8.6 %step.2 = (f32[2880,128]{1,0:T(8,128)S(1)}, f32[2880,128]{1,0:T(8,128)S(1)}, f32[5,64,128]{2,1,0:T(8,128)S(1)}, f32[2048,128]{1,0:T(8,128)S(1)}, f32[2048,128]{1...) custom-call(s32[2]{0:T(128)S(1)} %pad_add_fusion.flags, ...), custom_call_target="tpu_custom_call" | custom-call | tf_op jit(solution)/shard_map/step/pallas_call | solution.py:440
  74.0 15.0 %all_to_all.34 = f32[32,1,128]{2,1,0:T(1,128)S(1)} all-to-all(f32[32,1,128]{2,1,0:T(1,128)S(1)} %bitcast.29), channel_id=1, replica_groups=mesh['gx'=8,'gy'=4] {'gx','gy'}, dimensions={0} | all-to-all | bytes 32768 | tf_op jit(solution)/shard_map/all_to_all | solution.py:506
  91.1 1.5 %collective-permute-start.19 = (f32[64,128]{1,0:T(8,128)S(1)}, f32[64,128]{1,0:T(8,128)S(1)}, u32[]{:S(2)}, u32[]{:S(2)}) collective-permute-start(f32[64,128]{1,0:T(8,128)S(1)} %get-tuple-element.88), channel_id=1, source_target_pairs={{0,16},{4,20},{8,24},{12,28},{16,0},{20,4},{24,8},{28,12},{1,17},{... | collective-permute-start | bytes 98312 | tf_op jit(solution)/shard_map/ppermute | solution.py:431
  92.6 2.4 %collective-permute-start.18 = (f32[64,128]{1,0:T(8,128)S(1)}, f32[64,128]{1,0:T(8,128)S(1)}, u32[]{:S(2)}, u32[]{:S(2)}) collective-permute-start(f32[64,128]{1,0:T(8,128)S(1)} %get-tuple-element.88), channel_id=1, source_target_pairs={{0,8},{4,12},{8,0},{12,4},{16,24},{20,28},{24,16},{28,20},{1,9},{5... | collective-permute-start | bytes 98312 | tf_op jit(solution)/shard_map/ppermute | solution.py:431
  94.9 1.3 %collective-permute-done.20.refs_2_ = f32[64,128]{1,0:T(8,128)S(1)} collective-permute-done((f32[64,128]{1,0:T(8,128)S(1)}, f32[64,128]{1,0:T(8,128)S(1)}, u32[]{:S(2)}, u32[]{:S(2)}) %collective-permute-start.20) | collective-permute-done | bytes 32800 | tf_op jit(solution)/shard_map/ppermute | solution.py:431
  96.3 1.3 %collective-permute-done.18.refs_0_ = f32[64,128]{1,0:T(8,128)S(1)} collective-permute-done((f32[64,128]{1,0:T(8,128)S(1)}, f32[64,128]{1,0:T(8,128)S(1)}, u32[]{:S(2)}, u32[]{:S(2)}) %collective-permute-start.18) | collective-permute-done | bytes 32800 | tf_op jit(solution)/shard_map/ppermute | solution.py:431
  97.6 9.1 %step.3 = (f32[2880,128]{1,0:T(8,128)S(1)}, f32[2880,128]{1,0:T(8,128)S(1)}, f32[5,64,128]{2,1,0:T(8,128)}, f32[2048,128]{1,0:T(8,128)S(1)}, f32[2048,128]{1,0:T(8,128)S(1)}, /*index=5*/f32[32,128]{1,0:T(8,128)S(1)}) custom-call(s32[2]{0:T(128)S(1)} %pad_add_fusion.flags, f32[192,128]{1,0:T(8,128)S(1)} %collective-permute-done.14.xa, ...), custom_call_target="tpu_custom_call" | custom-call | tf_op jit(solution)/shard_map/step/pallas_call | solution.py:440
  106.7 11.8 %all_to_all.35 = f32[32,1,128]{2,1,0:T(1,128)S(1)} all-to-all(f32[32,1,128]{2,1,0:T(1,128)S(1)} %bitcast.31), channel_id=1, replica_groups=mesh['gx'=8,'gy'=4] {'gx','gy'}, dimensions={0} | all-to-all | bytes 32768 | tf_op jit(solution)/shard_map/all_to_all | solution.py:524
  118.5 1.8 %closing.1 = (f32[64,32,128]{2,1,0:T(8,128)}, f32[64,32,128]{2,1,0:T(8,128)}, f32[8,128]{1,0:T(8,128)S(1)}) custom-call(f32[32,128]{1,0:T(8,128)S(1)} %bitcast.24, f32[32,128]{1,0:T(8,128)S(1)} %bitcast.27, f32[32,128]{1,0:T(8,128)S(1)} %bitcast.28, f32[2048,128]{1,0:T(8,128)S(1)} %get-tuple-element.90.grho, f32[2048,128]{1,0:T(8,128)S(1)} %get-tuple-element.91.gsig, ...), custom_call_target="tpu_custom_call" | custom-call | tf_op jit(solution)/shard_map/closing/pallas_call | solution.py:440
  (52 shorter events, 10.9 us)
Async XLA Ops:
  5.6 7.5 %copy-start.8 = (f32[8]{0:T(128)S(1)}, f32[8]{0:T(128)}, u32[]{:S(2)}) copy-start(f32[8]{0:T(128)} %zlow.3) | copy-start | bytes 100
  5.6 7.5 %copy-start.9 = (f32[8]{0:T(128)S(1)}, f32[8]{0:T(128)}, u32[]{:S(2)}) copy-start(f32[8]{0:T(128)} %zhigh.3) | copy-start | bytes 100
  9.4 6.5 %collective-permute-start = (f32[256,128]{1,0:T(8,128)S(1)}, f32[256,128]{1,0:T(8,128)S(1)}, u32[]{:S(2)}, u32[]{:S(2)}) collective-permute-start(f32[256,128]{1,0:T(8,128)S(1)} %get-tuple-element.50), channel_id=1, source_target_pairs={{0,4},{4,0},{8,12},{12,8},{16,20},{20,16},{24,28},{28,24},{1,5},{5... | collective-permute-start | bytes 393224 | tf_op jit(solution)/shard_map/ppermute | solution.py:427
  12.4 3.4 %collective-permute-start.1 = (f32[192,128]{1,0:T(8,128)S(1)}, f32[192,128]{1,0:T(8,128)S(1)}, u32[]{:S(2)}, u32[]{:S(2)}) collective-permute-start(f32[192,128]{1,0:T(8,128)S(1)} %get-tuple-element.51), channel_id=1, source_target_pairs={{0,0},{4,8},{8,4},{12,16},{16,12},{20,24},{24,20},{28,28},{1,1},{5... | collective-permute-start | bytes 294920 | tf_op jit(solution)/shard_map/ppermute | solution.py:427
  15.9 14.0 %copy-start.1 = (f32[64,32,128]{2,1,0:T(8,128)S(1)}, f32[64,32,128]{2,1,0:T(8,128)}, u32[]{:S(2)}) copy-start(f32[64,32,128]{2,1,0:T(8,128)} %t.7) | copy-start | bytes 3145732
  16.7 13.2 %collective-permute-start.2 = (f32[432,128]{1,0:T(8,128)S(1)}, f32[432,128]{1,0:T(8,128)S(1)}, u32[]{:S(2)}, u32[]{:S(2)}) collective-permute-start(f32[432,128]{1,0:T(8,128)S(1)} %get-tuple-element.54), channel_id=1, source_target_pairs={{0,1},{1,0},{2,3},{3,2},{4,5},{5,4},{6,7},{7,6},{8,9},{9,8},{10,11... | collective-permute-start | bytes 663560 | tf_op jit(solution)/shard_map/ppermute | solution.py:427
  16.8 13.1 %collective-permute-start.3 = (f32[432,128]{1,0:T(8,128)S(1)}, f32[432,128]{1,0:T(8,128)S(1)}, u32[]{:S(2)}, u32[]{:S(2)}) collective-permute-start(f32[432,128]{1,0:T(8,128)S(1)} %get-tuple-element.55), channel_id=1, source_target_pairs={{0,0},{1,2},{2,1},{3,3},{4,4},{5,6},{6,5},{7,7},{8,8},{9,10},{10,9... | collective-permute-start | bytes 663560 | tf_op jit(solution)/shard_map/ppermute | solution.py:427
  17.5 9.5 %collective-permute-start.6 = (f32[64,128]{1,0:T(8,128)S(1)}, f32[64,128]{1,0:T(8,128)S(1)}, u32[]{:S(2)}, u32[]{:S(2)}) collective-permute-start(f32[64,128]{1,0:T(8,128)S(1)} %get-tuple-element.58), channel_id=1, source_target_pairs={{0,24},{4,28},{8,16},{12,20},{16,8},{20,12},{24,0},{28,4},{1,25},{... | collective-permute-start | bytes 98312 | tf_op jit(solution)/shard_map/ppermute | solution.py:431
  25.1 4.8 %collective-permute-start.5 = (f32[64,128]{1,0:T(8,128)S(1)}, f32[64,128]{1,0:T(8,128)S(1)}, u32[]{:S(2)}, u32[]{:S(2)}) collective-permute-start(f32[64,128]{1,0:T(8,128)S(1)} %get-tuple-element.58), channel_id=1, source_target_pairs={{0,16},{4,20},{8,24},{12,28},{16,0},{20,4},{24,8},{28,12},{1,17},{... | collective-permute-start | bytes 98312 | tf_op jit(solution)/shard_map/ppermute | solution.py:431
  25.1 4.8 %collective-permute-start.4 = (f32[64,128]{1,0:T(8,128)S(1)}, f32[64,128]{1,0:T(8,128)S(1)}, u32[]{:S(2)}, u32[]{:S(2)}) collective-permute-start(f32[64,128]{1,0:T(8,128)S(1)} %get-tuple-element.58), channel_id=1, source_target_pairs={{0,8},{4,12},{8,0},{12,4},{16,24},{20,28},{24,16},{28,20},{1,9},{5... | collective-permute-start | bytes 98312 | tf_op jit(solution)/shard_map/ppermute | solution.py:431
  38.6 17.0 %collective-permute-start.7 = (f32[192,128]{1,0:T(8,128)S(1)}, f32[192,128]{1,0:T(8,128)S(1)}, u32[]{:S(2)}, u32[]{:S(2)}) collective-permute-start(f32[192,128]{1,0:T(8,128)S(1)} %get-tuple-element.60), channel_id=1, source_target_pairs={{0,4},{4,0},{8,12},{12,8},{16,20},{20,16},{24,28},{28,24},{1,5},{5... | collective-permute-start | bytes 294920 | tf_op jit(solution)/shard_map/ppermute | solution.py:427
  38.6 17.0 %collective-permute-start.8 = (f32[128,128]{1,0:T(8,128)S(1)}, f32[128,128]{1,0:T(8,128)S(1)}, u32[]{:S(2)}, u32[]{:S(2)}) collective-permute-start(f32[128,128]{1,0:T(8,128)S(1)} %get-tuple-element.61), channel_id=1, source_target_pairs={{0,0},{4,8},{8,4},{12,16},{16,12},{20,24},{24,20},{28,28},{1,1},{5... | collective-permute-start | bytes 196616 | tf_op jit(solution)/shard_map/ppermute | solution.py:427
  56.3 7.8 %collective-permute-start.9 = (f32[288,128]{1,0:T(8,128)S(1)}, f32[288,128]{1,0:T(8,128)S(1)}, u32[]{:S(2)}, u32[]{:S(2)}) collective-permute-start(f32[288,128]{1,0:T(8,128)S(1)} %get-tuple-element.65), channel_id=1, source_target_pairs={{0,1},{1,0},{2,3},{3,2},{4,5},{5,4},{6,7},{7,6},{8,9},{9,8},{10,11... | collective-permute-start | bytes 442376 | tf_op jit(solution)/shard_map/ppermute | solution.py:427
  56.4 7.8 %collective-permute-start.10 = (f32[288,128]{1,0:T(8,128)S(1)}, f32[288,128]{1,0:T(8,128)S(1)}, u32[]{:S(2)}, u32[]{:S(2)}) collective-permute-start(f32[288,128]{1,0:T(8,128)S(1)} %get-tuple-element.66), channel_id=1, source_target_pairs={{0,0},{1,2},{2,1},{3,3},{4,4},{5,6},{6,5},{7,7},{8,8},{9,10},{10,9... | collective-permute-start | bytes 442376 | tf_op jit(solution)/shard_map/ppermute | solution.py:427
  57.0 5.8 %collective-permute-start.13 = (f32[64,128]{1,0:T(8,128)S(1)}, f32[64,128]{1,0:T(8,128)S(1)}, u32[]{:S(2)}, u32[]{:S(2)}) collective-permute-start(f32[64,128]{1,0:T(8,128)S(1)} %get-tuple-element.76), channel_id=1, source_target_pairs={{0,24},{4,28},{8,16},{12,20},{16,8},{20,12},{24,0},{28,4},{1,25},{... | collective-permute-start | bytes 98312 | tf_op jit(solution)/shard_map/ppermute | solution.py:431
  57.7 5.2 %collective-permute-start.12 = (f32[64,128]{1,0:T(8,128)S(1)}, f32[64,128]{1,0:T(8,128)S(1)}, u32[]{:S(2)}, u32[]{:S(2)}) collective-permute-start(f32[64,128]{1,0:T(8,128)S(1)} %get-tuple-element.76), channel_id=1, source_target_pairs={{0,16},{4,20},{8,24},{12,28},{16,0},{20,4},{24,8},{28,12},{1,17},{... | collective-permute-start | bytes 98312 | tf_op jit(solution)/shard_map/ppermute | solution.py:431
  59.2 5.0 %collective-permute-start.11 = (f32[64,128]{1,0:T(8,128)S(1)}, f32[64,128]{1,0:T(8,128)S(1)}, u32[]{:S(2)}, u32[]{:S(2)}) collective-permute-start(f32[64,128]{1,0:T(8,128)S(1)} %get-tuple-element.76), channel_id=1, source_target_pairs={{0,8},{4,12},{8,0},{12,4},{16,24},{20,28},{24,16},{28,20},{1,9},{5... | collective-permute-start | bytes 98312 | tf_op jit(solution)/shard_map/ppermute | solution.py:431
  72.8 16.3 %collective-permute-start.14 = (f32[192,128]{1,0:T(8,128)S(1)}, f32[192,128]{1,0:T(8,128)S(1)}, u32[]{:S(2)}, u32[]{:S(2)}) collective-permute-start(f32[192,128]{1,0:T(8,128)S(1)} %get-tuple-element.78), channel_id=1, source_target_pairs={{0,4},{4,0},{8,12},{12,8},{16,20},{20,16},{24,28},{28,24},{1,5},{5... | collective-permute-start | bytes 294920 | tf_op jit(solution)/shard_map/ppermute | solution.py:427
  73.3 15.7 %collective-permute-start.15 = (f32[128,128]{1,0:T(8,128)S(1)}, f32[128,128]{1,0:T(8,128)S(1)}, u32[]{:S(2)}, u32[]{:S(2)}) collective-permute-start(f32[128,128]{1,0:T(8,128)S(1)} %get-tuple-element.79), channel_id=1, source_target_pairs={{0,0},{4,8},{8,4},{12,16},{16,12},{20,24},{24,20},{28,28},{1,1},{5... | collective-permute-start | bytes 196616 | tf_op jit(solution)/shard_map/ppermute | solution.py:427
  89.7 7.8 %collective-permute-start.16 = (f32[288,128]{1,0:T(8,128)S(1)}, f32[288,128]{1,0:T(8,128)S(1)}, u32[]{:S(2)}, u32[]{:S(2)}) collective-permute-start(f32[288,128]{1,0:T(8,128)S(1)} %get-tuple-element.83), channel_id=1, source_target_pairs={{0,1},{1,0},{2,3},{3,2},{4,5},{5,4},{6,7},{7,6},{8,9},{9,8},{10,11... | collective-permute-start | bytes 442376 | tf_op jit(solution)/shard_map/ppermute | solution.py:427
  89.8 7.8 %collective-permute-start.17 = (f32[288,128]{1,0:T(8,128)S(1)}, f32[288,128]{1,0:T(8,128)S(1)}, u32[]{:S(2)}, u32[]{:S(2)}) collective-permute-start(f32[288,128]{1,0:T(8,128)S(1)} %get-tuple-element.84), channel_id=1, source_target_pairs={{0,0},{1,2},{2,1},{3,3},{4,4},{5,6},{6,5},{7,7},{8,8},{9,10},{10,9... | collective-permute-start | bytes 442376 | tf_op jit(solution)/shard_map/ppermute | solution.py:427
  90.5 5.8 %collective-permute-start.20 = (f32[64,128]{1,0:T(8,128)S(1)}, f32[64,128]{1,0:T(8,128)S(1)}, u32[]{:S(2)}, u32[]{:S(2)}) collective-permute-start(f32[64,128]{1,0:T(8,128)S(1)} %get-tuple-element.88), channel_id=1, source_target_pairs={{0,24},{4,28},{8,16},{12,20},{16,8},{20,12},{24,0},{28,4},{1,25},{... | collective-permute-start | bytes 98312 | tf_op jit(solution)/shard_map/ppermute | solution.py:431
  91.1 5.2 %collective-permute-start.19 = (f32[64,128]{1,0:T(8,128)S(1)}, f32[64,128]{1,0:T(8,128)S(1)}, u32[]{:S(2)}, u32[]{:S(2)}) collective-permute-start(f32[64,128]{1,0:T(8,128)S(1)} %get-tuple-element.88), channel_id=1, source_target_pairs={{0,16},{4,20},{8,24},{12,28},{16,0},{20,4},{24,8},{28,12},{1,17},{... | collective-permute-start | bytes 98312 | tf_op jit(solution)/shard_map/ppermute | solution.py:431
  92.6 5.0 %collective-permute-start.18 = (f32[64,128]{1,0:T(8,128)S(1)}, f32[64,128]{1,0:T(8,128)S(1)}, u32[]{:S(2)}, u32[]{:S(2)}) collective-permute-start(f32[64,128]{1,0:T(8,128)S(1)} %get-tuple-element.88), channel_id=1, source_target_pairs={{0,8},{4,12},{8,0},{12,4},{16,24},{20,28},{24,16},{28,20},{1,9},{5... | collective-permute-start | bytes 98312 | tf_op jit(solution)/shard_map/ppermute | solution.py:431
  (7 other events, 25.5 us)

commit v3 on v2

--- a/solution.py
+++ b/solution.py
@@ -265,7 +265,7 @@
         bz[at, :] = zdiff(sig_e[at, :])
         return run, acc
 
-    _, acc_t = lax.fori_loop(0, nx // step, fields, (before, zero8))
+    _, acc_t = lax.fori_loop(0, nx // step, fields, (before, zero8), unroll=True)
 
     rowid = lax.broadcasted_iota(jnp.int32, (w, nz), 0)
     mine = jnp.logical_and(rowid >= 1, rowid <= ny)
@@ -295,7 +295,7 @@
 
     cross_plane(0, None, False)
     cross_plane(nx + 1, None, False)
-    acc_c = lax.fori_loop(1, nx + 1, lambda xi, acc: cross_plane(xi, acc, True), zero8, unroll=2)
+    acc_c = lax.fori_loop(1, nx + 1, lambda xi, acc: cross_plane(xi, acc, True), zero8, unroll=4)
 
     def adjoints(c, carry):
         start = (1 + c * step) * w
@@ -305,7 +305,7 @@
             out[at, :] = along_y - zdiff(vz[at, :])
         return carry
 
-    lax.fori_loop(0, nx // step, adjoints, 0)
+    lax.fori_loop(0, nx // step, adjoints, 0, unroll=True)
 
     def gradients(i, carry):
         back, sum_t, sum_r, nr, ns, acc = carry
@@ -328,7 +328,7 @@
                 acc + fold8(miss * miss))
 
     start = (after, zero, zero, zero8, zero8, zero8)
-    _, sum_t, sum_r, nr, ns, acc_p = lax.fori_loop(0, nx, gradients, start, unroll=4)
+    _, sum_t, sum_r, nr, ns, acc_p = lax.fori_loop(0, nx, gradients, start, unroll=8)
 
     total = lambda v: jnp.sum(jnp.sum(v, axis=0, keepdims=True), axis=1, keepdims=True)
     lane = lax.broadcasted_iota(jnp.int32, sums.shape, 1)
@@ -408,12 +408,10 @@
         return carry
 
     lax.fori_loop(0, g.nx, body, 0, unroll=4)
-    lane = lax.broadcasted_iota(jnp.int32, obj.shape, 1)
-    total = jnp.zeros(obj.shape, F32)
     for k, sums in enumerate((sums0, sums1, sums2)):
         row = jnp.sum(sums[...], axis=0, keepdims=True)
-        total = jnp.where(lane == k, lane_value(row, 2) * (0.5 / g.cells), total)
-    obj[...] = total
+        lane = lax.broadcasted_iota(jnp.int32, row.shape, 1)
+        obj[k] = jnp.sum(jnp.where(lane == 2, row, 0.0)) * (0.5 / g.cells)
 
 
 def pairs_of(size):
@@ -436,13 +434,13 @@
 HBM = pl.BlockSpec(memory_space=pltpu.HBM)
 
 
-def call(body, name, shapes, specs, args, scratch=(), limit=12):
+def call(body, name, shapes, specs, args, scratch=(), limit=12, outs=None):
     return pl.pallas_call(
         body,
         name=name,
         out_shape=[jax.ShapeDtypeStruct(s, d) for s, d in shapes],
         in_specs=specs,
-        out_specs=[VMEM] * len(shapes),
+        out_specs=outs or [VMEM] * len(shapes),
         scratch_shapes=list(scratch),
         compiler_params=pltpu.CompilerParams(vmem_limit_bytes=limit * 1024 * 1024),
     )(*args)
@@ -473,7 +471,7 @@
 
     own, xa, xb = call(
         functools.partial(first_kernel, g), "first", [own_shape, xa_shape(3), xb_shape(3)],
-        [SMEM] + [HBM] * 4, (flags, density, slowness, zone_map, time_obs),
+        [SMEM] + [HBM] * 4, (flags, *(pltpu.with_memory_space_constraint(v, pltpu.HBM) for v in (density, slowness, zone_map, time_obs))),
         [pltpu.VMEM((2, 1, 2, ny, nz), F32), pltpu.VMEM((2, 2, ny, nz), jnp.int32),
          pltpu.VMEM((nx, ny, nz), F32), pltpu.VMEM((nx, ny, nz), F32), pltpu.SemaphoreType.DMA((4 + nx // 4,))],
     )
@@ -524,10 +522,10 @@
     sums = lax.all_to_all(sums, both, 0, 0, tiled=True)
     history.append(sums)
     rho, sigma, obj = call(
-        functools.partial(closing_kernel, g), "closing", [block, block, ((8, nz), F32)],
-        [VMEM] * 9, (*history, grho, gsig, rho_e, sig_e, low, high),
+        functools.partial(closing_kernel, g), "closing", [block, block, ((ITERS,), F32)],
+        [VMEM] * 9, (*history, grho, gsig, rho_e, sig_e, low, high), outs=[VMEM, VMEM, SMEM],
     )
-    return rho, sigma, obj[0, :ITERS]
+    return rho, sigma, obj
 
 
 def solution(mesh):

time: 121 us -> 106 us (0.88)
  Pallas kernels: 36.8 us -> 27.5 us
  local copies, waits for them, and re-layouts: 5.44 us -> 0.03 us
    pallas_call x9, Pallas kernels: 36.8 us -> 27.5 us  [call(): pl.pallas_call(body, name=name, out_shape=[jax.ShapeDtypeStruct(s, d) for...]
    unnamed x20 -> x14, local copies, waits for them, and re-layouts: 4.92 us -> 0.03 us
  transfers between devices with their start and end apart: 21 -> 21, of which waited for: 7 -> 7; matrix products, arithmetic and copies ran while one was open for 0% -> 0% of each run, Pallas kernels for 2% -> 3%
where the time goes in v3:
time: 106 us
  blocking collectives  43.1 us (41%)
  Pallas kernels  27.5 us (26%)
  starting transfers between devices  25 us (24%)
  waiting for transfers between devices  9.54 us (9%)
    all_to_all x3, blocking collectives, local(): sums = lax.all_to_all(sums, both, 0, 0, tiled=True)  43.1 us
    pallas_call x9, Pallas kernels, call(): pl.pallas_call(body, name=name, out_shape=[jax.ShapeDtypeStruct(s, d) for...  27.5 us
    ppermute x9, starting transfers between devices, pair_totals(): lax.ppermute(pair, 'gx', [(i, i ^ 2 * m) for i in range(size)])  17.1 us
    ppermute x9, waiting for transfers between devices, pair_totals(): lax.ppermute(pair, 'gx', [(i, i ^ 2 * m) for i in range(size)])  9.43 us
    ppermute x12, starting transfers between devices, exchange(): return (lax.ppermute(a, axis, pa), lax.ppermute(b, axis, pb))  7.85 us
  transfers between devices with their start and end apart: 21, of which 7 were waited for; matrix products, arithmetic and copies ran while one was open for 0% of the time, Pallas kernels for 3%

profile of v3, /device:TPU:0, one launch (start us, length us, event | category | flops | bytes accessed | tf_op | source)
XLA Modules:
  0.0 106.1 jit_solution(18194310379565224902)
XLA Ops:
  0.7 2.5 %first.1 = (f32[64,128]{1,0:T(8,128)S(1)}, f32[256,128]{1,0:T(8,128)S(1)}, f32[192,128]{1,0:T(8,128)S(1)}) custom-call(s32[2]{0:T(128)S(1)} %pad_add_fusion.flags, f32[64,32,128]{2,1,0:T(8,128)} %rho.3, f32[64,32,128]{2,1,0:T(8,128)} %sig.1, s32[64,32,128]{2,1,0:T(8,128)} %zone.3, f32[64,32,128]{2,1,0:T(8,128)} %t.7), custom_call_target="tpu_custom_call" | custom-call | tf_op jit(solution)/shard_map/first/pallas_call | solution.py:438
  3.2 3.0 %collective-permute-start = (f32[256,128]{1,0:T(8,128)S(1)}, f32[256,128]{1,0:T(8,128)S(1)}, u32[]{:S(2)}, u32[]{:S(2)}) collective-permute-start(f32[256,128]{1,0:T(8,128)S(1)} %get-tuple-element.47), channel_id=1, source_target_pairs={{0,4},{4,0},{8,12},{12,8},{16,20},{20,16},{24,28},{28,24},{1,5},{5... | collective-permute-start | bytes 393224 | tf_op jit(solution)/shard_map/ppermute | solution.py:425
  6.9 2.7 %spread.1 = (f32[64,32,128]{2,1,0:T(8,128)S(1)}, f32[64,32,128]{2,1,0:T(8,128)S(1)}, f32[64,32,128]{2,1,0:T(8,128)S(1)}, bf16[256,256]{1,0:T(8,128)(2,1)S(1)}, bf16[256,128]{1,0:T(8,128)(2,1)S(1)}) custom-call(f32[8]{0:T(128)S(1)} %copy-done.5, f32[8]{0:T(128)S(1)} %copy-done.6, s32[64,32,128]{2,1,0:T(8,128)S(1)} %copy-done.2, f32[64,32,128]{2,1,0:T(8,128)S(1)} %copy-done.1), custom_call_target="tpu_custom_call" | custom-call | tf_op jit(solution)/shard_map/spread/pallas_call | solution.py:438
  9.7 0.8 sides.3
  11.3 7.6 %collective-permute-start.6 = (f32[64,128]{1,0:T(8,128)S(1)}, f32[64,128]{1,0:T(8,128)S(1)}, u32[]{:S(2)}, u32[]{:S(2)}) collective-permute-start(f32[64,128]{1,0:T(8,128)S(1)} %get-tuple-element.55), channel_id=1, source_target_pairs={{0,24},{4,28},{8,16},{12,20},{16,8},{20,12},{24,0},{28,4},{1,25},{... | collective-permute-start | bytes 98312 | tf_op jit(solution)/shard_map/ppermute | solution.py:429
  19.5 1.3 %collective-permute-done.6.refs_2_ = f32[64,128]{1,0:T(8,128)S(1)} collective-permute-done((f32[64,128]{1,0:T(8,128)S(1)}, f32[64,128]{1,0:T(8,128)S(1)}, u32[]{:S(2)}, u32[]{:S(2)}) %collective-permute-start.6) | collective-permute-done | bytes 32800 | tf_op jit(solution)/shard_map/ppermute | solution.py:429
  20.8 2.9 %collective-permute-done.5.refs_1_ = f32[64,128]{1,0:T(8,128)S(1)} collective-permute-done((f32[64,128]{1,0:T(8,128)S(1)}, f32[64,128]{1,0:T(8,128)S(1)}, u32[]{:S(2)}, u32[]{:S(2)}) %collective-permute-start.5) | collective-permute-done | bytes 32800 | tf_op jit(solution)/shard_map/ppermute | solution.py:429
  23.7 5.9 %opening.1 = (f32[2880,128]{1,0:T(8,128)S(1)}, f32[2880,128]{1,0:T(8,128)S(1)}, f32[5,64,128]{2,1,0:T(8,128)S(1)}, f32[2,64,128]{2,1,0:T(8,128)S(1)}, f32[2,64,1...) custom-call(s32[2]{0:T(128)S(1)} %pad_add_fusion.flags, ...), custom_call_target="tpu_custom_call" | custom-call | tf_op jit(solution)/shard_map/opening/pallas_call | solution.py:438
  30.3 16.3 %all_to_all.33 = f32[32,1,128]{2,1,0:T(1,128)S(1)} all-to-all(f32[32,1,128]{2,1,0:T(1,128)S(1)} %bitcast.28), channel_id=1, replica_groups=mesh['gx'=8,'gy'=4] {'gx','gy'}, dimensions={0} | all-to-all | bytes 32768 | tf_op jit(solution)/shard_map/all_to_all | solution.py:504
  46.6 0.7 sides.4
  48.7 1.5 %collective-permute-start.12 = (f32[64,128]{1,0:T(8,128)S(1)}, f32[64,128]{1,0:T(8,128)S(1)}, u32[]{:S(2)}, u32[]{:S(2)}) collective-permute-start(f32[64,128]{1,0:T(8,128)S(1)} %get-tuple-element.73), channel_id=1, source_target_pairs={{0,16},{4,20},{8,24},{12,28},{16,0},{20,4},{24,8},{28,12},{1,17},{... | collective-permute-start | bytes 98312 | tf_op jit(solution)/shard_map/ppermute | solution.py:429
  50.2 2.4 %collective-permute-start.11 = (f32[64,128]{1,0:T(8,128)S(1)}, f32[64,128]{1,0:T(8,128)S(1)}, u32[]{:S(2)}, u32[]{:S(2)}) collective-permute-start(f32[64,128]{1,0:T(8,128)S(1)} %get-tuple-element.73), channel_id=1, source_target_pairs={{0,8},{4,12},{8,0},{12,4},{16,24},{20,28},{24,16},{28,20},{1,9},{5... | collective-permute-start | bytes 98312 | tf_op jit(solution)/shard_map/ppermute | solution.py:429
  52.6 1.3 %collective-permute-done.13.refs_2_ = f32[64,128]{1,0:T(8,128)S(1)} collective-permute-done((f32[64,128]{1,0:T(8,128)S(1)}, f32[64,128]{1,0:T(8,128)S(1)}, u32[]{:S(2)}, u32[]{:S(2)}) %collective-permute-start.13) | collective-permute-done | bytes 32800 | tf_op jit(solution)/shard_map/ppermute | solution.py:429
  53.9 1.3 %collective-permute-done.11.refs_0_ = f32[64,128]{1,0:T(8,128)S(1)} collective-permute-done((f32[64,128]{1,0:T(8,128)S(1)}, f32[64,128]{1,0:T(8,128)S(1)}, u32[]{:S(2)}, u32[]{:S(2)}) %collective-permute-start.11) | collective-permute-done | bytes 32800 | tf_op jit(solution)/shard_map/ppermute | solution.py:429
  55.2 6.1 %step.2 = (f32[2880,128]{1,0:T(8,128)S(1)}, f32[2880,128]{1,0:T(8,128)S(1)}, f32[5,64,128]{2,1,0:T(8,128)S(1)}, f32[2048,128]{1,0:T(8,128)S(1)}, f32[2048,128]{1...) custom-call(s32[2]{0:T(128)S(1)} %pad_add_fusion.flags, ...), custom_call_target="tpu_custom_call" | custom-call | tf_op jit(solution)/shard_map/step/pallas_call | solution.py:438
  62.5 15.0 %all_to_all.34 = f32[32,1,128]{2,1,0:T(1,128)S(1)} all-to-all(f32[32,1,128]{2,1,0:T(1,128)S(1)} %bitcast.27), channel_id=1, replica_groups=mesh['gx'=8,'gy'=4] {'gx','gy'}, dimensions={0} | all-to-all | bytes 32768 | tf_op jit(solution)/shard_map/all_to_all | solution.py:504
  77.5 0.7 sides.5
  79.6 1.5 %collective-permute-start.19 = (f32[64,128]{1,0:T(8,128)S(1)}, f32[64,128]{1,0:T(8,128)S(1)}, u32[]{:S(2)}, u32[]{:S(2)}) collective-permute-start(f32[64,128]{1,0:T(8,128)S(1)} %get-tuple-element.85), channel_id=1, source_target_pairs={{0,16},{4,20},{8,24},{12,28},{16,0},{20,4},{24,8},{28,12},{1,17},{... | collective-permute-start | bytes 98312 | tf_op jit(solution)/shard_map/ppermute | solution.py:429
  81.1 2.4 %collective-permute-start.18 = (f32[64,128]{1,0:T(8,128)S(1)}, f32[64,128]{1,0:T(8,128)S(1)}, u32[]{:S(2)}, u32[]{:S(2)}) collective-permute-start(f32[64,128]{1,0:T(8,128)S(1)} %get-tuple-element.85), channel_id=1, source_target_pairs={{0,8},{4,12},{8,0},{12,4},{16,24},{20,28},{24,16},{28,20},{1,9},{5... | collective-permute-start | bytes 98312 | tf_op jit(solution)/shard_map/ppermute | solution.py:429
  83.4 1.3 %collective-permute-done.20.refs_2_ = f32[64,128]{1,0:T(8,128)S(1)} collective-permute-done((f32[64,128]{1,0:T(8,128)S(1)}, f32[64,128]{1,0:T(8,128)S(1)}, u32[]{:S(2)}, u32[]{:S(2)}) %collective-permute-start.20) | collective-permute-done | bytes 32800 | tf_op jit(solution)/shard_map/ppermute | solution.py:429
  84.8 1.3 %collective-permute-done.18.refs_0_ = f32[64,128]{1,0:T(8,128)S(1)} collective-permute-done((f32[64,128]{1,0:T(8,128)S(1)}, f32[64,128]{1,0:T(8,128)S(1)}, u32[]{:S(2)}, u32[]{:S(2)}) %collective-permute-start.18) | collective-permute-done | bytes 32800 | tf_op jit(solution)/shard_map/ppermute | solution.py:429
  86.1 6.4 %step.3 = (f32[2880,128]{1,0:T(8,128)S(1)}, f32[2880,128]{1,0:T(8,128)S(1)}, f32[5,64,128]{2,1,0:T(8,128)}, f32[2048,128]{1,0:T(8,128)S(1)}, f32[2048,128]{1,0:T(8,128)S(1)}, /*index=5*/f32[32,128]{1,0:T(8,128)S(1)}) custom-call(s32[2]{0:T(128)S(1)} %pad_add_fusion.flags, f32[192,128]{1,0:T(8,128)S(1)} %collective-permute-done.14.xa, ...), custom_call_target="tpu_custom_call" | custom-call | tf_op jit(solution)/shard_map/step/pallas_call | solution.py:438
  92.5 11.8 %all_to_all.35 = f32[32,1,128]{2,1,0:T(1,128)S(1)} all-to-all(f32[32,1,128]{2,1,0:T(1,128)S(1)} %bitcast.29), channel_id=1, replica_groups=mesh['gx'=8,'gy'=4] {'gx','gy'}, dimensions={0} | all-to-all | bytes 32768 | tf_op jit(solution)/shard_map/all_to_all | solution.py:522
  104.3 1.8 %closing.1 = (f32[64,32,128]{2,1,0:T(8,128)}, f32[64,32,128]{2,1,0:T(8,128)}, f32[3]{0:T(128)}) custom-call(f32[32,128]{1,0:T(8,128)S(1)} %bitcast.22, f32[32,128]{1,0:T(8,128)S(1)} %bitcast.25, f32[32,128]{1,0:T(8,128)S(1)} %bitcast.26, f32[2048,128]{1,0:T(8,128)S(1)} %get-tuple-element.87.grho, f32[2048,128]{1,0:T(8,128)S(1)} %get-tuple-element.88.gsig, ...), custom_call_target="tpu_custom_call" | custom-call | tf_op jit(solution)/shard_map/closing/pallas_call | solution.py:438
  (45 shorter events, 6.9 us)
Async XLA Ops:
  3.2 6.6 %copy-start.3 = (f32[64,32,128]{2,1,0:T(8,128)S(1)}, f32[64,32,128]{2,1,0:T(8,128)}, u32[]{:S(2)}) copy-start(f32[64,32,128]{2,1,0:T(8,128)} %rho.3) | copy-start | bytes 3145732
  3.2 6.5 %copy-start.4 = (f32[64,32,128]{2,1,0:T(8,128)S(1)}, f32[64,32,128]{2,1,0:T(8,128)}, u32[]{:S(2)}) copy-start(f32[64,32,128]{2,1,0:T(8,128)} %sig.1) | copy-start | bytes 3145732
  3.2 6.5 %collective-permute-start = (f32[256,128]{1,0:T(8,128)S(1)}, f32[256,128]{1,0:T(8,128)S(1)}, u32[]{:S(2)}, u32[]{:S(2)}) collective-permute-start(f32[256,128]{1,0:T(8,128)S(1)} %get-tuple-element.47), channel_id=1, source_target_pairs={{0,4},{4,0},{8,12},{12,8},{16,20},{20,16},{24,28},{28,24},{1,5},{5... | collective-permute-start | bytes 393224 | tf_op jit(solution)/shard_map/ppermute | solution.py:425
  6.2 3.4 %collective-permute-start.1 = (f32[192,128]{1,0:T(8,128)S(1)}, f32[192,128]{1,0:T(8,128)S(1)}, u32[]{:S(2)}, u32[]{:S(2)}) collective-permute-start(f32[192,128]{1,0:T(8,128)S(1)} %get-tuple-element.48), channel_id=1, source_target_pairs={{0,0},{4,8},{8,4},{12,16},{16,12},{20,24},{24,20},{28,28},{1,1},{5... | collective-permute-start | bytes 294920 | tf_op jit(solution)/shard_map/ppermute | solution.py:425
  9.7 14.0 %copy-start = (f32[64,32,128]{2,1,0:T(8,128)S(1)}, f32[64,32,128]{2,1,0:T(8,128)}, u32[]{:S(2)}) copy-start(f32[64,32,128]{2,1,0:T(8,128)} %t.7) | copy-start | bytes 3145732
  10.5 13.2 %collective-permute-start.2 = (f32[432,128]{1,0:T(8,128)S(1)}, f32[432,128]{1,0:T(8,128)S(1)}, u32[]{:S(2)}, u32[]{:S(2)}) collective-permute-start(f32[432,128]{1,0:T(8,128)S(1)} %get-tuple-element.51), channel_id=1, source_target_pairs={{0,1},{1,0},{2,3},{3,2},{4,5},{5,4},{6,7},{7,6},{8,9},{9,8},{10,11... | collective-permute-start | bytes 663560 | tf_op jit(solution)/shard_map/ppermute | solution.py:425
  10.6 13.1 %collective-permute-start.3 = (f32[432,128]{1,0:T(8,128)S(1)}, f32[432,128]{1,0:T(8,128)S(1)}, u32[]{:S(2)}, u32[]{:S(2)}) collective-permute-start(f32[432,128]{1,0:T(8,128)S(1)} %get-tuple-element.52), channel_id=1, source_target_pairs={{0,0},{1,2},{2,1},{3,3},{4,4},{5,6},{6,5},{7,7},{8,8},{9,10},{10,9... | collective-permute-start | bytes 663560 | tf_op jit(solution)/shard_map/ppermute | solution.py:425
  11.3 9.5 %collective-permute-start.6 = (f32[64,128]{1,0:T(8,128)S(1)}, f32[64,128]{1,0:T(8,128)S(1)}, u32[]{:S(2)}, u32[]{:S(2)}) collective-permute-start(f32[64,128]{1,0:T(8,128)S(1)} %get-tuple-element.55), channel_id=1, source_target_pairs={{0,24},{4,28},{8,16},{12,20},{16,8},{20,12},{24,0},{28,4},{1,25},{... | collective-permute-start | bytes 98312 | tf_op jit(solution)/shard_map/ppermute | solution.py:429
  18.9 4.8 %collective-permute-start.5 = (f32[64,128]{1,0:T(8,128)S(1)}, f32[64,128]{1,0:T(8,128)S(1)}, u32[]{:S(2)}, u32[]{:S(2)}) collective-permute-start(f32[64,128]{1,0:T(8,128)S(1)} %get-tuple-element.55), channel_id=1, source_target_pairs={{0,16},{4,20},{8,24},{12,28},{16,0},{20,4},{24,8},{28,12},{1,17},{... | collective-permute-start | bytes 98312 | tf_op jit(solution)/shard_map/ppermute | solution.py:429
  18.9 4.8 %collective-permute-start.4 = (f32[64,128]{1,0:T(8,128)S(1)}, f32[64,128]{1,0:T(8,128)S(1)}, u32[]{:S(2)}, u32[]{:S(2)}) collective-permute-start(f32[64,128]{1,0:T(8,128)S(1)} %get-tuple-element.55), channel_id=1, source_target_pairs={{0,8},{4,12},{8,0},{12,4},{16,24},{20,28},{24,16},{28,20},{1,9},{5... | collective-permute-start | bytes 98312 | tf_op jit(solution)/shard_map/ppermute | solution.py:429
  29.6 17.0 %collective-permute-start.7 = (f32[192,128]{1,0:T(8,128)S(1)}, f32[192,128]{1,0:T(8,128)S(1)}, u32[]{:S(2)}, u32[]{:S(2)}) collective-permute-start(f32[192,128]{1,0:T(8,128)S(1)} %get-tuple-element.57), channel_id=1, source_target_pairs={{0,4},{4,0},{8,12},{12,8},{16,20},{20,16},{24,28},{28,24},{1,5},{5... | collective-permute-start | bytes 294920 | tf_op jit(solution)/shard_map/ppermute | solution.py:425
  29.7 17.0 %collective-permute-start.8 = (f32[128,128]{1,0:T(8,128)S(1)}, f32[128,128]{1,0:T(8,128)S(1)}, u32[]{:S(2)}, u32[]{:S(2)}) collective-permute-start(f32[128,128]{1,0:T(8,128)S(1)} %get-tuple-element.58), channel_id=1, source_target_pairs={{0,0},{4,8},{8,4},{12,16},{16,12},{20,24},{24,20},{28,28},{1,1},{5... | collective-permute-start | bytes 196616 | tf_op jit(solution)/shard_map/ppermute | solution.py:425
  47.4 7.8 %collective-permute-start.9 = (f32[288,128]{1,0:T(8,128)S(1)}, f32[288,128]{1,0:T(8,128)S(1)}, u32[]{:S(2)}, u32[]{:S(2)}) collective-permute-start(f32[288,128]{1,0:T(8,128)S(1)} %get-tuple-element.62), channel_id=1, source_target_pairs={{0,1},{1,0},{2,3},{3,2},{4,5},{5,4},{6,7},{7,6},{8,9},{9,8},{10,11... | collective-permute-start | bytes 442376 | tf_op jit(solution)/shard_map/ppermute | solution.py:425
  47.4 7.8 %collective-permute-start.10 = (f32[288,128]{1,0:T(8,128)S(1)}, f32[288,128]{1,0:T(8,128)S(1)}, u32[]{:S(2)}, u32[]{:S(2)}) collective-permute-start(f32[288,128]{1,0:T(8,128)S(1)} %get-tuple-element.63), channel_id=1, source_target_pairs={{0,0},{1,2},{2,1},{3,3},{4,4},{5,6},{6,5},{7,7},{8,8},{9,10},{10,9... | collective-permute-start | bytes 442376 | tf_op jit(solution)/shard_map/ppermute | solution.py:425
  48.1 5.8 %collective-permute-start.13 = (f32[64,128]{1,0:T(8,128)S(1)}, f32[64,128]{1,0:T(8,128)S(1)}, u32[]{:S(2)}, u32[]{:S(2)}) collective-permute-start(f32[64,128]{1,0:T(8,128)S(1)} %get-tuple-element.73), channel_id=1, source_target_pairs={{0,24},{4,28},{8,16},{12,20},{16,8},{20,12},{24,0},{28,4},{1,25},{... | collective-permute-start | bytes 98312 | tf_op jit(solution)/shard_map/ppermute | solution.py:429
  48.7 5.2 %collective-permute-start.12 = (f32[64,128]{1,0:T(8,128)S(1)}, f32[64,128]{1,0:T(8,128)S(1)}, u32[]{:S(2)}, u32[]{:S(2)}) collective-permute-start(f32[64,128]{1,0:T(8,128)S(1)} %get-tuple-element.73), channel_id=1, source_target_pairs={{0,16},{4,20},{8,24},{12,28},{16,0},{20,4},{24,8},{28,12},{1,17},{... | collective-permute-start | bytes 98312 | tf_op jit(solution)/shard_map/ppermute | solution.py:429
  50.2 5.0 %collective-permute-start.11 = (f32[64,128]{1,0:T(8,128)S(1)}, f32[64,128]{1,0:T(8,128)S(1)}, u32[]{:S(2)}, u32[]{:S(2)}) collective-permute-start(f32[64,128]{1,0:T(8,128)S(1)} %get-tuple-element.73), channel_id=1, source_target_pairs={{0,8},{4,12},{8,0},{12,4},{16,24},{20,28},{24,16},{28,20},{1,9},{5... | collective-permute-start | bytes 98312 | tf_op jit(solution)/shard_map/ppermute | solution.py:429
  61.3 16.3 %collective-permute-start.14 = (f32[192,128]{1,0:T(8,128)S(1)}, f32[192,128]{1,0:T(8,128)S(1)}, u32[]{:S(2)}, u32[]{:S(2)}) collective-permute-start(f32[192,128]{1,0:T(8,128)S(1)} %get-tuple-element.75), channel_id=1, source_target_pairs={{0,4},{4,0},{8,12},{12,8},{16,20},{20,16},{24,28},{28,24},{1,5},{5... | collective-permute-start | bytes 294920 | tf_op jit(solution)/shard_map/ppermute | solution.py:425
  61.9 15.7 %collective-permute-start.15 = (f32[128,128]{1,0:T(8,128)S(1)}, f32[128,128]{1,0:T(8,128)S(1)}, u32[]{:S(2)}, u32[]{:S(2)}) collective-permute-start(f32[128,128]{1,0:T(8,128)S(1)} %get-tuple-element.76), channel_id=1, source_target_pairs={{0,0},{4,8},{8,4},{12,16},{16,12},{20,24},{24,20},{28,28},{1,1},{5... | collective-permute-start | bytes 196616 | tf_op jit(solution)/shard_map/ppermute | solution.py:425
  78.2 7.8 %collective-permute-start.16 = (f32[288,128]{1,0:T(8,128)S(1)}, f32[288,128]{1,0:T(8,128)S(1)}, u32[]{:S(2)}, u32[]{:S(2)}) collective-permute-start(f32[288,128]{1,0:T(8,128)S(1)} %get-tuple-element.80), channel_id=1, source_target_pairs={{0,1},{1,0},{2,3},{3,2},{4,5},{5,4},{6,7},{7,6},{8,9},{9,8},{10,11... | collective-permute-start | bytes 442376 | tf_op jit(solution)/shard_map/ppermute | solution.py:425
  78.3 7.8 %collective-permute-start.17 = (f32[288,128]{1,0:T(8,128)S(1)}, f32[288,128]{1,0:T(8,128)S(1)}, u32[]{:S(2)}, u32[]{:S(2)}) collective-permute-start(f32[288,128]{1,0:T(8,128)S(1)} %get-tuple-element.81), channel_id=1, source_target_pairs={{0,0},{1,2},{2,1},{3,3},{4,4},{5,6},{6,5},{7,7},{8,8},{9,10},{10,9... | collective-permute-start | bytes 442376 | tf_op jit(solution)/shard_map/ppermute | solution.py:425
  79.0 5.8 %collective-permute-start.20 = (f32[64,128]{1,0:T(8,128)S(1)}, f32[64,128]{1,0:T(8,128)S(1)}, u32[]{:S(2)}, u32[]{:S(2)}) collective-permute-start(f32[64,128]{1,0:T(8,128)S(1)} %get-tuple-element.85), channel_id=1, source_target_pairs={{0,24},{4,28},{8,16},{12,20},{16,8},{20,12},{24,0},{28,4},{1,25},{... | collective-permute-start | bytes 98312 | tf_op jit(solution)/shard_map/ppermute | solution.py:429
  79.6 5.2 %collective-permute-start.19 = (f32[64,128]{1,0:T(8,128)S(1)}, f32[64,128]{1,0:T(8,128)S(1)}, u32[]{:S(2)}, u32[]{:S(2)}) collective-permute-start(f32[64,128]{1,0:T(8,128)S(1)} %get-tuple-element.85), channel_id=1, source_target_pairs={{0,16},{4,20},{8,24},{12,28},{16,0},{20,4},{24,8},{28,12},{1,17},{... | collective-permute-start | bytes 98312 | tf_op jit(solution)/shard_map/ppermute | solution.py:429
  81.1 5.0 %collective-permute-start.18 = (f32[64,128]{1,0:T(8,128)S(1)}, f32[64,128]{1,0:T(8,128)S(1)}, u32[]{:S(2)}, u32[]{:S(2)}) collective-permute-start(f32[64,128]{1,0:T(8,128)S(1)} %get-tuple-element.85), channel_id=1, source_target_pairs={{0,8},{4,12},{8,0},{12,4},{16,24},{20,28},{24,16},{28,20},{1,9},{5... | collective-permute-start | bytes 98312 | tf_op jit(solution)/shard_map/ppermute | solution.py:429
  (4 other events, 24.8 us)

commit v4 on v3

--- a/solution.py
+++ b/solution.py
@@ -8,6 +8,7 @@
 from jax.experimental.pallas import tpu as pltpu
 from jax.sharding import PartitionSpec as P
 
+
 ITERS = 3
 BETA = 1.0
 ETA = 0.5
@@ -15,6 +16,8 @@
 
 XO = 2
 YO = 4
+CHUNK = 4
+DIAGONALS = ((-1, -1), (-1, 1), (1, -1), (1, 1))
 F32 = jnp.float32
 BF16 = jnp.bfloat16
 
@@ -23,7 +26,6 @@
     def __init__(self, nx, ny, nz, px, py):
         self.nx, self.ny, self.nz, self.px, self.py = nx, ny, nz, px, py
         self.pl = ny + 2 * YO
-        self.planes = nx + 2 * XO
         self.ext = (nx + 8) * self.pl
         self.xp = nx + 8
         self.cells = float(nx * px * ny * py * nz)
@@ -147,7 +149,38 @@
     lax.fori_loop(0, g.nx // step, body, 0)
 
 
-def sides_kernel(g, fields, flags, xa, xb, own, order, *refs):
+def join_kernel(g, flags, xa, own, head, pair, sums):
+    (even, _, _), _ = flags_of(g, flags)
+    ny = g.ny
+    at = 4 * ny
+    join_pair(g, even, own, xa, at, pair)
+    n = sums.shape[0] // CHUNK
+    sums[...] = jnp.zeros(sums.shape, F32)
+    sums[pl.ds(0, n, stride=CHUNK), :] = jnp.broadcast_to(head[0:1, :], (n, g.nz))
+    for k, (dx, dy) in enumerate(DIAGONALS):
+        ok, there = diagonal(g, flags, dx, dy)
+
+        @pl.when(ok)
+        def _():
+            for f in range(2):
+                sums[pl.ds(there * CHUNK + 1 + f, 1), :] = head[8 + 2 * k + f : 9 + 2 * k + f, :]
+
+
+def diagonal(g, flags, dx, dy):
+    ix, iy = flags[0] + dx, flags[1] + dy
+    ok = jnp.logical_and(jnp.logical_and(ix >= 0, ix < g.px), jnp.logical_and(iy >= 0, iy < g.py))
+    return ok, jnp.where(ok, ix * g.py + iy, 0)
+
+
+def join_pair(g, even, own, xa, at, pair):
+    ny = g.ny
+    mine_t, mine_s = own[0:ny, :], own[ny : 2 * ny, :]
+    other_t, other_s = xa[at : at + ny, :], xa[at + ny : at + 2 * ny, :]
+    pair[0:ny, :] = mine_t + other_t
+    pair[ny : 2 * ny, :] = mine_s + other_s + jnp.where(even, mine_t, other_t) * (g.nx * g.xs)
+
+
+def sides_kernel(g, fields, flags, xa, xb, own, *refs):
     blocks, (ya, yb, pair) = refs[:fields], refs[fields:]
     (xeven, xfirst, xlast), (yeven, _, _) = flags_of(g, flags)
     n = g.xp
@@ -164,29 +197,26 @@
                 for r in range(2):
                     spot = (f * 2 + r) * n + plane
                     put_pair(yeven, value[r : r + 1], value[g.ny - 2 + r : g.ny - 1 + r], ya, yb, spot)
-    at = fields * 2 * g.ny
-    mine_t, mine_s = own[0 : g.ny, :], own[g.ny : 2 * g.ny, :]
-    other_t, other_s = xa[at : at + g.ny, :], xa[at + g.ny : at + 2 * g.ny, :]
-    pair[0 : g.ny, :] = mine_t + other_t
-    pair[g.ny : 2 * g.ny, :] = mine_s + other_s + jnp.where(xeven, mine_t, other_t) * (g.nx * g.xs)
-
-
-def halo_slots(g):
+    join_pair(g, xeven, own, xa, fields * 2 * g.ny, pair)
+
+
+def halo_slots(g, n, off):
     xs = []
     for r in range(2):
         xs.append((r * g.ny, pl.ds(r * g.pl + YO, g.ny), pl.ds((XO + g.nx + r) * g.pl + YO, g.ny)))
     ys = []
     for r in range(2):
-        ys.append((r * g.xp, pl.ds(YO - 2 + r, g.xp, stride=g.pl), pl.ds(YO + g.ny + r, g.xp, stride=g.pl)))
+        first = off * g.pl + r
+        ys.append((r * n, pl.ds(first + YO - 2, n, stride=g.pl), pl.ds(first + YO + g.ny, n, stride=g.pl)))
     return xs, ys
 
 
-def halo_values(g, flags, field, xa, xb, ya, yb):
+def halo_values(g, flags, field, xa, xb, ya, yb, yn, off):
     (xeven, xfirst, xlast), (yeven, yfirst, ylast) = flags_of(g, flags)
-    xs, ys = halo_slots(g)
+    xs, ys = halo_slots(g, yn, off)
     for axis, slots, n, a, b, even, first, last in (
         (0, xs, g.ny, xa, xb, xeven, xfirst, xlast),
-        (1, ys, g.xp, ya, yb, yeven, yfirst, ylast),
+        (1, ys, yn, ya, yb, yeven, yfirst, ylast),
     ):
         for at, low_rows, high_rows in slots:
             here = pl.ds(field * 2 * n + at, n)
@@ -200,8 +230,13 @@
     return jnp.sum(jnp.where(ids == lane, row, 0.0), axis=1, keepdims=True)
 
 
+def sum_row(g, sums):
+    n = g.px * g.py
+    return jnp.sum(sums[pl.ds(0, n, stride=sums.shape[0] // n), :], axis=0, keepdims=True)
+
+
 def alphas(g, sums):
-    row = jnp.sum(sums[...], axis=0, keepdims=True)
+    row = sum_row(g, sums)
     return tuple(ETA * lax.rsqrt(lane_value(row, k) / g.cells + EPSILON) for k in range(2))
 
 
@@ -226,10 +261,10 @@
 
 
 def step_core(g, flags, update, rho_e, sig_e, trs, p, q, t, table, ztable, outs, scratch):
-    grho, gsig, sums, own, xa, xb = outs
+    grho, gsig, sums, own, xa, xb, ya, yb = outs
     vxr, vxs, vyr, vys, vzr, vzs, gyr, gys, rt_s, az, bz, yu, ym = scratch
     nx, ny, nz, w = g.nx, g.ny, g.nz, g.pl
-    (even, _, _), _ = flags_of(g, flags)
+    (even, _, _), (yeven, _, _) = flags_of(g, flags)
     zero = jnp.zeros((ny, nz), F32)
     zero8 = jnp.zeros((8, nz), F32)
     before, after = ray_offsets(g, flags, trs)
@@ -331,9 +366,10 @@
     _, sum_t, sum_r, nr, ns, acc_p = lax.fori_loop(0, nx, gradients, start, unroll=8)
 
     total = lambda v: jnp.sum(jnp.sum(v, axis=0, keepdims=True), axis=1, keepdims=True)
-    lane = lax.broadcasted_iota(jnp.int32, sums.shape, 1)
+    spread = sums.shape[0] if own is None else 8
+    lane = lax.broadcasted_iota(jnp.int32, (spread, nz), 1)
     obj = acc_t + acc_p + acc_c * (BETA / 16.0)
-    sums[...] = jnp.where(lane == 0, total(nr), jnp.where(lane == 1, total(ns), jnp.where(lane == 2, total(obj), 0.0)))
+    sums[0:spread, :] = jnp.where(lane == 0, total(nr), jnp.where(lane == 1, total(ns), jnp.where(lane == 2, total(obj), 0.0)))
     if own is not None:
         rest = sum_r * g.xs
         pos = 0
@@ -344,6 +380,14 @@
         for ref, at in ((own, 0), (xa, pos)):
             ref[at : at + ny, :] = sum_t
             ref[at + ny : at + 2 * ny, :] = rest
+        for f, block in enumerate((grho, gsig)):
+            for r in range(2):
+                rows_low = block[pl.ds(r, nx, stride=ny), :]
+                rows_high = block[pl.ds(ny - 2 + r, nx, stride=ny), :]
+                put_pair(yeven, rows_low, rows_high, ya, yb, (f * 2 + r) * nx)
+            for k, (dx, dy) in enumerate(DIAGONALS):
+                cell = (0 if dx < 0 else nx - 1) * ny + (0 if dy < 0 else ny - 1)
+                sums[8 + 2 * k + f : 9 + 2 * k + f, :] = block[cell : cell + 1, :]
 
 
 def opening_step(g, zones, flags, zlow, zhigh, xa, xb, ya, yb, own, rho, sig, p, q, t, table, ztable, *refs):
@@ -351,9 +395,9 @@
     rho_e, sig_e, trs, xlow, xhigh, ylow, yhigh = rest[:7]
     ny = g.ny
     for f, ext in ((0, rho_e), (1, sig_e)):
-        for axis, side, at, spot, value in halo_values(g, flags, f, xa, xb, ya, yb):
+        for axis, side, at, spot, value in halo_values(g, flags, f, xa, xb, ya, yb, g.xp, 0):
             ext[spot, :] = value
-    for axis, side, at, spot, value in halo_values(g, flags, 2, xa, xb, ya, yb):
+    for axis, side, at, spot, value in halo_values(g, flags, 2, xa, xb, ya, yb, g.xp, 0):
         low, high = bounds_of(zones, value, zlow, zhigh)
         lows, highs = ((xlow, xhigh), (ylow, yhigh))[axis]
         lows[side, pl.ds(at, value.shape[0]), :] = low
@@ -363,7 +407,7 @@
     trs[1] = xa[pos : pos + 2 * ny, :]
     for m, other in enumerate(others):
         trs[2 + m] = other[...]
-    step_core(g, flags, lambda x, at: (rho[x], sig[x]), rho_e, sig_e, trs, p, q, t, table, ztable, rest[7:13], rest[13:])
+    step_core(g, flags, lambda x, at: (rho[x], sig[x]), rho_e, sig_e, trs, p, q, t, table, ztable, rest[7:15], rest[15:])
 
 
 def later_step(g, last, flags, xa, xb, ya, yb, sums_i, own_i, grho_i, gsig_i, rho_i, sig_i, low, high,
@@ -372,12 +416,24 @@
     rho_e, sig_e, trs = rest[:3]
     ny = g.ny
     ar, asig = alphas(g, sums_i)
-    for axis, side, at, spot, value in halo_values(g, flags, 0, xa, xb, ya, yb):
+    clip = lambda v, lows, highs: jnp.minimum(jnp.maximum(v, lows), highs)
+    for axis, side, at, spot, value in halo_values(g, flags, 0, xa, xb, ya, yb, g.nx, XO):
         lows, highs = ((xlow, xhigh), (ylow, yhigh))[axis]
+        if axis == 1:
+            at = at // g.nx * g.xp + XO
         here = pl.ds(at, value.shape[0])
-        moved = rho_i[spot, :] - ar * value
-        rho_e[spot, :] = jnp.minimum(jnp.maximum(moved, lows[side, here, :]), highs[side, here, :])
-    for axis, side, at, spot, value in halo_values(g, flags, 1, xa, xb, ya, yb):
+        rho_e[spot, :] = clip(rho_i[spot, :] - ar * value, lows[side, here, :], highs[side, here, :])
+    for axis, side, at, spot, value in halo_values(g, flags, 1, xa, xb, ya, yb, g.nx, XO):
+        sig_e[spot, :] = sig_i[spot, :] - asig * value
+    for dx, dy in DIAGONALS:
+        ok, there = diagonal(g, flags, dx, dy)
+        plane = XO - 1 if dx < 0 else XO + g.nx
+        side = 0 if dy < 0 else 1
+        here = pl.ds((1 - side) * g.xp + plane, 1)
+        spot = pl.ds(plane * g.pl + (YO - 1 if dy < 0 else YO + ny), 1)
+        value = jnp.where(ok, sums_i[pl.ds(there * CHUNK + 1, 1), :], 0.0)
+        rho_e[spot, :] = clip(rho_i[spot, :] - ar * value, ylow[side, here, :], yhigh[side, here, :])
+        value = jnp.where(ok, sums_i[pl.ds(there * CHUNK + 2, 1), :], 0.0)
         sig_e[spot, :] = sig_i[spot, :] - asig * value
     pos = 4 * ny
     trs[0] = trs_i[0] - asig * own_i[...]
@@ -388,12 +444,12 @@
     def update(x, at):
         here = pl.ds(pl.multiple_of(x * ny, 8), ny)
         moved = rho_i[at, :] - ar * grho_i[here, :]
-        return jnp.minimum(jnp.maximum(moved, low[x]), high[x]), sig_i[at, :] - asig * gsig_i[here, :]
+        return clip(moved, low[x], high[x]), sig_i[at, :] - asig * gsig_i[here, :]
 
     if last:
-        outs, scratch = (*rest[3:6], None, None, None), rest[6:]
+        outs, scratch = (*rest[3:6], None, None, None, None, None), rest[6:]
     else:
-        outs, scratch = rest[3:9], rest[9:]
+        outs, scratch = rest[3:11], rest[11:]
     step_core(g, flags, update, rho_e, sig_e, trs, p, q, t, table, ztable, outs, scratch)
 
 
@@ -409,7 +465,7 @@
 
     lax.fori_loop(0, g.nx, body, 0, unroll=4)
     for k, sums in enumerate((sums0, sums1, sums2)):
-        row = jnp.sum(sums[...], axis=0, keepdims=True)
+        row = sum_row(g, sums)
         lane = lax.broadcasted_iota(jnp.int32, row.shape, 1)
         obj[k] = jnp.sum(jnp.where(lane == 2, row, 0.0)) * (0.5 / g.cells)
 
@@ -422,11 +478,16 @@
 
 def exchange(axis, a, b):
     pa, pb = pairs_of(lax.axis_size(axis))
-    return lax.ppermute(a, axis, pa), lax.ppermute(b, axis, pb)
+    a = lax.ppermute(a, axis, pa)
+    b = lax.ppermute(b, axis, pb)
+    return a, b
 
 
 def pair_totals(pair, size):
-    return [lax.ppermute(pair, "gx", [(i, i ^ (2 * m)) for i in range(size)]) for m in range(1, size // 2)]
+    out = []
+    for m in range(1, size // 2):
+        out.append(lax.ppermute(pair, "gx", [(i, i ^ (2 * m)) for i in range(size)]))
+    return out
 
 
 SMEM = pl.BlockSpec(memory_space=pltpu.SMEM)
@@ -434,10 +495,9 @@
 HBM = pl.BlockSpec(memory_space=pltpu.HBM)
 
 
-def call(body, name, shapes, specs, args, scratch=(), limit=12, outs=None):
+def call(body, shapes, specs, args, scratch=(), limit=12, outs=None):
     return pl.pallas_call(
         body,
-        name=name,
         out_shape=[jax.ShapeDtypeStruct(s, d) for s, d in shapes],
         in_specs=specs,
         out_specs=outs or [VMEM] * len(shapes),
@@ -470,59 +530,60 @@
     core_scratch = [win] * 8 + [pltpu.VMEM((nx * ny, nz), F32)] + [ext_v] * 4
 
     own, xa, xb = call(
-        functools.partial(first_kernel, g), "first", [own_shape, xa_shape(3), xb_shape(3)],
+        functools.partial(first_kernel, g), [own_shape, xa_shape(3), xb_shape(3)],
         [SMEM] + [HBM] * 4, (flags, *(pltpu.with_memory_space_constraint(v, pltpu.HBM) for v in (density, slowness, zone_map, time_obs))),
         [pltpu.VMEM((2, 1, 2, ny, nz), F32), pltpu.VMEM((2, 2, ny, nz), jnp.int32),
          pltpu.VMEM((nx, ny, nz), F32), pltpu.VMEM((nx, ny, nz), F32), pltpu.SemaphoreType.DMA((4 + nx // 4,))],
     )
     xa, xb = exchange("gx", xa, xb)
     low, high, q, table, ztable = call(
-        functools.partial(spread_kernel, g, zones), "spread",
+        functools.partial(spread_kernel, g, zones),
         [block] * 3 + [((2 * nz, 2 * nz), BF16), ((2 * nz, nz), BF16)],
         [SMEM, SMEM] + [VMEM] * 2, (zone_low, zone_high, zone_map, pressure_obs),
     )
     as_rows = lambda v: v.reshape(nx * ny, nz)
     ya, yb, pair = call(
-        functools.partial(sides_kernel, g, 3), "sides", [ymsg(3)] * 2 + [own_shape],
-        [SMEM] + [VMEM] * 7, (flags, xa, xb, own, table, as_rows(density), as_rows(slowness), as_rows(zone_map)),
+        functools.partial(sides_kernel, g, 3), [ymsg(3)] * 2 + [own_shape],
+        [SMEM] + [VMEM] * 6, (flags, xa, xb, own, as_rows(density), as_rows(slowness), as_rows(zone_map)),
     )
     ya, yb = exchange("gy", ya, yb)
     others = pair_totals(pair, px)
-    ends = [flat, flat, sums_shape, own_shape, xa_shape(2), xb_shape(2)]
+    yown = ((4 * nx, nz), F32)
+    ends = [flat, flat, ((16, nz), F32), own_shape, xa_shape(2), xb_shape(2), yown, yown]
+    chunks = ((px * py * CHUNK, nz), F32)
     outs = call(
-        functools.partial(opening_step, g, zones), "opening",
+        functools.partial(opening_step, g, zones),
         [ext, ext, trs_shape, xbound, xbound, ybound, ybound] + ends,
         [SMEM] * 3 + [VMEM] * (12 + len(others)),
         (flags, zone_low, zone_high, xa, xb, ya, yb, own, density, slowness, pressure_obs, q, time_obs, table, ztable, *others),
         core_scratch, 24,
     )
-    rho_e, sig_e, trs, xlow, xhigh, ylow, yhigh, grho, gsig, sums, own, xa, xb = outs
+    rho_e, sig_e, trs, xlow, xhigh, ylow, yhigh, grho, gsig, head, own, xa, xb, ya, yb = outs
     history = []
     for iteration in range(1, ITERS):
         last = iteration == ITERS - 1
         xa, xb = exchange("gx", xa, xb)
+        ya, yb = exchange("gy", ya, yb)
+        pair, sums = call(
+            functools.partial(join_kernel, g), [own_shape, chunks], [SMEM] + [VMEM] * 3,
+            (flags, xa, own, head),
+        )
+        others = pair_totals(pair, px)
         sums = lax.all_to_all(sums, both, 0, 0, tiled=True)
         history.append(sums)
-        ya, yb, pair = call(
-            functools.partial(sides_kernel, g, 2), "sides", [ymsg(2)] * 2 + [own_shape],
-            [SMEM] + [VMEM] * 6, (flags, xa, xb, own, sums, grho, gsig),
-        )
-        ya, yb = exchange("gy", ya, yb)
-        others = pair_totals(pair, px)
         outs = call(
-            functools.partial(later_step, g, last), "step", [ext, ext, trs_shape] + (ends[:3] if last else ends),
+            functools.partial(later_step, g, last), [ext, ext, trs_shape] + ([flat, flat, sums_shape] if last else ends),
             [SMEM] + [VMEM] * (22 + len(others)),
             (flags, xa, xb, ya, yb, sums, own, grho, gsig, rho_e, sig_e, low, high, xlow, xhigh, ylow, yhigh, trs,
              pressure_obs, q, time_obs, table, ztable, *others),
             core_scratch, 24,
         )
-        rho_e, sig_e, trs, grho, gsig, sums = outs[:6]
+        rho_e, sig_e, trs, grho, gsig, head = outs[:6]
         if not last:
-            own, xa, xb = outs[6:]
-    sums = lax.all_to_all(sums, both, 0, 0, tiled=True)
-    history.append(sums)
+            own, xa, xb, ya, yb = outs[6:]
+    history.append(lax.all_to_all(head, both, 0, 0, tiled=True))
     rho, sigma, obj = call(
-        functools.partial(closing_kernel, g), "closing", [block, block, ((ITERS,), F32)],
+        functools.partial(closing_kernel, g), [block, block, ((ITERS,), F32)],
         [VMEM] * 9, (*history, grho, gsig, rho_e, sig_e, low, high), outs=[VMEM, VMEM, SMEM],
     )
     return rho, sigma, obj

time: 106 us -> 157 us (1.48); the launches traced: 106 us -> 155 us
  local copies, waits for them, and re-layouts: 0.03 us -> 54.4 us
  blocking collectives: 43.1 us -> 11 us
  starting transfers between devices: 25 us -> 49.1 us
  Pallas kernels: 27.5 us -> 30.1 us
    unnamed x14 -> x148, local copies, waits for them, and re-layouts: 0.03 us -> 54.4 us
    all_to_all x3 -> x1, blocking collectives: 43.1 us -> 11 us  [local(): history.append(lax.all_to_all(head, both, 0, 0, tiled=True))]
    ppermute x21, starting transfers between devices: 25 us -> 38.4 us  [the longest x9 23.4 us: pair_totals(): out.append(lax.ppermute(pair, 'gx', [(i, i ^ 2 * m) for i in range(size)]))]
    all_to_all x0 -> x2, starting transfers between devices: none -> 10.8 us  [local(): sums = lax.all_to_all(sums, both, 0, 0, tiled=True)]
    pallas_call x9, Pallas kernels: 27.5 us -> 30.1 us  [call(): pl.pallas_call(body, out_shape=[jax.ShapeDtypeStruct(s, d) for s, d in sh...]
  transfers between devices with their start and end apart: 21 -> 23, of which waited for: 7 -> 8; matrix products, arithmetic and copies ran while one was open for 0% -> 0% of each run, Pallas kernels for 3% -> 3%
where the time goes in v4:
time: 157 us; the launch traced here: 155 us
  local copies, waits for them, and re-layouts  54.4 us (35%)
  starting transfers between devices  49.1 us (31%)
  Pallas kernels  30.1 us (19%)
  blocking collectives  11 us (7%)
  waiting for transfers between devices  9.42 us (6%)
    unnamed x148, local copies, waits for them, and re-layouts  54.4 us
    pallas_call x9, Pallas kernels, call(): pl.pallas_call(body, out_shape=[jax.ShapeDtypeStruct(s, d) for s, d in sh...  30.1 us
    ppermute x9, starting transfers between devices, pair_totals(): out.append(lax.ppermute(pair, 'gx', [(i, i ^ 2 * m) for i in range(size)]))  23.4 us
    all_to_all x1, blocking collectives, local(): history.append(lax.all_to_all(head, both, 0, 0, tiled=True))  11 us
    all_to_all x2, starting transfers between devices, local(): sums = lax.all_to_all(sums, both, 0, 0, tiled=True)  10.8 us
    ppermute x6, starting transfers between devices, exchange(): b = lax.ppermute(b, axis, pb)  8.77 us
    ppermute x6, starting transfers between devices, exchange(): a = lax.ppermute(a, axis, pa)  6.15 us
    ppermute x6, waiting for transfers between devices, exchange(): a = lax.ppermute(a, axis, pa)  4.84 us
  transfers between devices with their start and end apart: 23, of which 8 were waited for; matrix products, arithmetic and copies ran while one was open for 0% of the time, Pallas kernels for 3%

profile of v4, /device:TPU:0, one launch (start us, length us, event | category | flops | bytes accessed | tf_op | source)
XLA Modules:
  0.0 155.0 jit_solution(2512755371739189944)
XLA Ops:
  0.7 2.6 %shard_map.94 = (f32[64,128]{1,0:T(8,128)S(1)}, f32[256,128]{1,0:T(8,128)S(1)}, f32[192,128]{1,0:T(8,128)S(1)}) custom-call(s32[2]{0:T(128)S(1)} %pad_add_fusion.flags, f32[64,32,128]{2,1,0:T(8,128)} %rho.3, f32[64,32,128]{2,1,0:T(8,128)} %sig.1, s32[64,32,128]{2,1,0:T(8,128)} %zone.3, f32[64,32,128]{2,1,0:T(8,128)} %t.7), custom_call_target="tpu_custom_call" | custom-call | tf_op jit(solution)/shard_map/pallas_call | solution.py:499
  3.3 3.0 %collective-permute-start = (f32[256,128]{1,0:T(8,128)S(1)}, f32[256,128]{1,0:T(8,128)S(1)}, u32[]{:S(2)}, u32[]{:S(2)}) collective-permute-start(f32[256,128]{1,0:T(8,128)S(1)} %get-tuple-element.49), channel_id=1, source_target_pairs={{0,4},{4,0},{8,12},{12,8},{16,20},{20,16},{24,28},{28,24},{1,5},{5... | collective-permute-start | bytes 393224 | tf_op jit(solution)/shard_map/ppermute | solution.py:481
  7.0 2.8 %collective-permute-done.xa = f32[256,128]{1,0:T(8,128)S(1)} collective-permute-done((f32[256,128]{1,0:T(8,128)S(1)}, f32[256,128]{1,0:T(8,128)S(1)}, u32[]{:S(2)}, u32[]{:S(2)}) %collective-permute-start) | collective-permute-done | bytes 131104 | tf_op jit(solution)/shard_map/ppermute | solution.py:481
  11.6 7.6 %collective-permute-start.6 = (f32[64,128]{1,0:T(8,128)S(1)}, f32[64,128]{1,0:T(8,128)S(1)}, u32[]{:S(2)}, u32[]{:S(2)}) collective-permute-start(f32[64,128]{1,0:T(8,128)S(1)} %get-tuple-element.57), channel_id=1, source_target_pairs={{0,24},{4,28},{8,16},{12,20},{16,8},{20,12},{24,0},{28,4},{1,25},{... | collective-permute-start | bytes 98312 | tf_op jit(solution)/shard_map/ppermute | solution.py:489
  19.8 2.7 %shard_map.96 = (f32[64,32,128]{2,1,0:T(8,128)S(1)}, f32[64,32,128]{2,1,0:T(8,128)S(1)}, f32[64,32,128]{2,1,0:T(8,128)S(1)}, bf16[256,256]{1,0:T(8,128)(2,1)S(1)}, bf16[256,128]{1,0:T(8,128)(2,1)S(1)}) custom-call(f32[8]{0:T(128)S(1)} %copy-done.68, f32[8]{0:T(128)S(1)} %copy-done.69, s32[64,32,128]{2,1,0:T(8,128)S(1)} %copy-done.5, f32[64,32,128]{2,1,0:T(8,128)S(1)} %copy-done.1), custom_call_target="tpu_custom_call" | custom-call | tf_op jit(solution)/shard_map/pallas_call | solution.py:499
  24.0 6.6 %shard_map.97 = (f32[2880,128]{1,0:T(8,128)S(1)}, f32[2880,128]{1,0:T(8,128)S(1)}, f32[5,64,128]{2,1,0:T(8,128)S(1)}, f32[2,64,128]{2,1,0:T(8,128)S(1)}, f32[2,6...) custom-call(s32[2]{0:T(128)S(1)} %pad_add_fusion.flags, ...), custom_call_target="tpu_custom_call" | custom-call | tf_op jit(solution)/shard_map/pallas_call | solution.py:499
  38.0 2.0 %collective-permute-start.9 = (f32[256,128]{1,0:T(8,128)}, f32[256,128]{1,0:T(8,128)}, u32[]{:S(2)}, u32[]{:S(2)}) collective-permute-start(f32[256,128]{1,0:T(8,128)} %get-tuple-element.63), channel_id=1, source_target_pairs={{0,1},{1,0},{2,3},{3,2},{4,5},{5,4},{6,7},{7,6},{8,9},{9,8},{10,11... | collective-permute-start | bytes 393224 | tf_op jit(solution)/shard_map/ppermute | solution.py:481
  40.0 2.2 %collective-permute-start.10 = (f32[256,128]{1,0:T(8,128)}, f32[256,128]{1,0:T(8,128)}, u32[]{:S(2)}, u32[]{:S(2)}) collective-permute-start(f32[256,128]{1,0:T(8,128)} %get-tuple-element.64), channel_id=1, source_target_pairs={{0,0},{1,2},{2,1},{3,3},{4,4},{5,6},{6,5},{7,7},{8,8},{9,10},{10,9... | collective-permute-start | bytes 393224 | tf_op jit(solution)/shard_map/ppermute | solution.py:482
  45.8 6.2 %all-to-all-start = ((f32[32,4,128]{2,1,0:T(4,128)}), f32[32,4,128]{2,1,0:T(4,128)S(1)}, u32[]{:S(2)}, u32[]{:S(2)}) async-start(f32[32,4,128]{2,1,0:T(4,128)} %bitcast.21), calls=%async_computation | async-start | bytes 131072 | tf_op jit(solution)/shard_map/all_to_all | solution.py:572
  52.0 1.5 collective-permute-start.8
  53.5 5.5 %collective-permute-start.13 = (f32[64,128]{1,0:T(8,128)}, f32[64,128]{1,0:T(8,128)S(1)}, u32[]{:S(2)}, u32[]{:S(2)}) collective-permute-start(f32[64,128]{1,0:T(8,128)} %copy-done.72), channel_id=1, source_target_pairs={{0,24},{4,28},{8,16},{12,20},{16,8},{20,12},{24,0},{28,4},{1,25},{... | collective-permute-start | bytes 98312 | tf_op jit(solution)/shard_map/ppermute | solution.py:489
  59.7 2.1 %collective-permute-start.11 = (f32[64,128]{1,0:T(8,128)}, f32[64,128]{1,0:T(8,128)S(1)}, u32[]{:S(2)}, u32[]{:S(2)}) collective-permute-start(f32[64,128]{1,0:T(8,128)} %copy-done.72), channel_id=1, source_target_pairs={{0,8},{4,12},{8,0},{12,4},{16,24},{20,28},{24,16},{28,20},{1,9},{5... | collective-permute-start | bytes 98312 | tf_op jit(solution)/shard_map/ppermute | solution.py:489
  69.2 1.4 copy-done.18
  82.0 7.2 %shard_map.99 = (f32[2880,128]{1,0:T(8,128)S(1)}, f32[2880,128]{1,0:T(8,128)S(1)}, f32[5,64,128]{2,1,0:T(8,128)S(1)}, f32[2048,128]{1,0:T(8,128)S(1)}, f32[2048,...) custom-call(s32[2]{0:T(128)S(1)} %copy-done.66, ...), custom_call_target="tpu_custom_call" | custom-call | tf_op jit(solution)/shard_map/pallas_call | solution.py:499
  95.0 2.2 %collective-permute-start.17 = (f32[256,128]{1,0:T(8,128)}, f32[256,128]{1,0:T(8,128)}, u32[]{:S(2)}, u32[]{:S(2)}) collective-permute-start(f32[256,128]{1,0:T(8,128)} %get-tuple-element.83), channel_id=1, source_target_pairs={{0,0},{1,2},{2,1},{3,3},{4,4},{5,6},{6,5},{7,7},{8,8},{9,10},{10,9... | collective-permute-start | bytes 393224 | tf_op jit(solution)/shard_map/ppermute | solution.py:482
  97.2 1.4 collective-permute-done.14.xa
  101.1 4.6 %all-to-all-start.1 = ((f32[32,4,128]{2,1,0:T(4,128)}), f32[32,4,128]{2,1,0:T(4,128)S(1)}, u32[]{:S(2)}, u32[]{:S(2)}) async-start(f32[32,4,128]{2,1,0:T(4,128)} %bitcast.7), calls=%async_computation.1 | async-start | bytes 131072 | tf_op jit(solution)/shard_map/all_to_all | solution.py:572
  105.7 1.5 collective-permute-start.15
  107.2 5.5 %collective-permute-start.20 = (f32[64,128]{1,0:T(8,128)}, f32[64,128]{1,0:T(8,128)S(1)}, u32[]{:S(2)}, u32[]{:S(2)}) collective-permute-start(f32[64,128]{1,0:T(8,128)} %copy-done.73), channel_id=1, source_target_pairs={{0,24},{4,28},{8,16},{12,20},{16,8},{20,12},{24,0},{28,4},{1,25},{... | collective-permute-start | bytes 98312 | tf_op jit(solution)/shard_map/ppermute | solution.py:489
  112.7 2.1 %collective-permute-start.18 = (f32[64,128]{1,0:T(8,128)}, f32[64,128]{1,0:T(8,128)S(1)}, u32[]{:S(2)}, u32[]{:S(2)}) collective-permute-start(f32[64,128]{1,0:T(8,128)} %copy-done.73), channel_id=1, source_target_pairs={{0,8},{4,12},{8,0},{12,4},{16,24},{20,28},{24,16},{28,20},{1,9},{5... | collective-permute-start | bytes 98312 | tf_op jit(solution)/shard_map/ppermute | solution.py:489
  121.4 1.4 copy-done.12
  135.6 6.6 %shard_map.101 = (f32[2880,128]{1,0:T(8,128)S(1)}, f32[2880,128]{1,0:T(8,128)S(1)}, f32[5,64,128]{2,1,0:T(8,128)}, f32[2048,128]{1,0:T(8,128)S(1)}, f32[2048,128]{1,0:T(8,128)S(1)}, /*index=5*/f32[32,128]{1,0:T(8,128)S(1)}) custom-call(s32[2]{0:T(128)S(1)} %copy-done.67, f32[192,128]{1,0:T(8,128)S(1)} %copy-done.33, ...), custom_call_target="tpu_custom_call" | custom-call | tf_op jit(solution)/shard_map/pallas_call | solution.py:499
  142.2 11.0 %all_to_all.33 = f32[32,1,128]{2,1,0:T(1,128)S(1)} all-to-all(f32[32,1,128]{2,1,0:T(1,128)S(1)} %bitcast.22), channel_id=1, replica_groups=mesh['gx'=8,'gy'=4] {'gx','gy'}, dimensions={0} | all-to-all | bytes 32768 | tf_op jit(solution)/shard_map/all_to_all | solution.py:584
  153.2 1.8 %shard_map.102 = (f32[64,32,128]{2,1,0:T(8,128)}, f32[64,32,128]{2,1,0:T(8,128)}, f32[3]{0:T(128)}) custom-call(f32[128,128]{1,0:T(8,128)S(1)} %bitcast.17, f32[128,128]{1,0:T(8,128)S(1)} %bitcast.19, f32[32,128]{1,0:T(8,128)S(1)} %bitcast.20, f32[2048,128]{1,0:T(8,128)S(1)} %get-tuple-element.91.grho, f32[2048,128]{1,0:T(8,128)S(1)} %get-tuple-element.92.gsig, ...), custom_call_target="tpu_custom_call" | custom-call | tf_op jit(solution)/shard_map/pallas_call | solution.py:499
  (181 shorter events, 62.8 us)
Async XLA Ops:
  3.3 6.5 %collective-permute-start = (f32[256,128]{1,0:T(8,128)S(1)}, f32[256,128]{1,0:T(8,128)S(1)}, u32[]{:S(2)}, u32[]{:S(2)}) collective-permute-start(f32[256,128]{1,0:T(8,128)S(1)} %get-tuple-element.49), channel_id=1, source_target_pairs={{0,4},{4,0},{8,12},{12,8},{16,20},{20,16},{24,28},{28,24},{1,5},{5... | collective-permute-start | bytes 393224 | tf_op jit(solution)/shard_map/ppermute | solution.py:481
  6.4 0.7 collective-permute-start.1
  10.7 13.3 %collective-permute-start.2 = (f32[432,128]{1,0:T(8,128)S(1)}, f32[432,128]{1,0:T(8,128)S(1)}, u32[]{:S(2)}, u32[]{:S(2)}) collective-permute-start(f32[432,128]{1,0:T(8,128)S(1)} %get-tuple-element.52), channel_id=1, source_target_pairs={{0,1},{1,0},{2,3},{3,2},{4,5},{5,4},{6,7},{7,6},{8,9},{9,8},{10,11... | collective-permute-start | bytes 663560 | tf_op jit(solution)/shard_map/ppermute | solution.py:481
  10.8 13.2 %collective-permute-start.3 = (f32[432,128]{1,0:T(8,128)S(1)}, f32[432,128]{1,0:T(8,128)S(1)}, u32[]{:S(2)}, u32[]{:S(2)}) collective-permute-start(f32[432,128]{1,0:T(8,128)S(1)} %get-tuple-element.53), channel_id=1, source_target_pairs={{0,0},{1,2},{2,1},{3,3},{4,4},{5,6},{6,5},{7,7},{8,8},{9,10},{10,9... | collective-permute-start | bytes 663560 | tf_op jit(solution)/shard_map/ppermute | solution.py:482
  11.6 11.9 %collective-permute-start.6 = (f32[64,128]{1,0:T(8,128)S(1)}, f32[64,128]{1,0:T(8,128)S(1)}, u32[]{:S(2)}, u32[]{:S(2)}) collective-permute-start(f32[64,128]{1,0:T(8,128)S(1)} %get-tuple-element.57), channel_id=1, source_target_pairs={{0,24},{4,28},{8,16},{12,20},{16,8},{20,12},{24,0},{28,4},{1,25},{... | collective-permute-start | bytes 98312 | tf_op jit(solution)/shard_map/ppermute | solution.py:489
  19.2 4.8 %collective-permute-start.5 = (f32[64,128]{1,0:T(8,128)S(1)}, f32[64,128]{1,0:T(8,128)S(1)}, u32[]{:S(2)}, u32[]{:S(2)}) collective-permute-start(f32[64,128]{1,0:T(8,128)S(1)} %get-tuple-element.57), channel_id=1, source_target_pairs={{0,16},{4,20},{8,24},{12,28},{16,0},{20,4},{24,8},{28,12},{1,17},{... | collective-permute-start | bytes 98312 | tf_op jit(solution)/shard_map/ppermute | solution.py:489
  19.2 4.8 %collective-permute-start.4 = (f32[64,128]{1,0:T(8,128)S(1)}, f32[64,128]{1,0:T(8,128)S(1)}, u32[]{:S(2)}, u32[]{:S(2)}) collective-permute-start(f32[64,128]{1,0:T(8,128)S(1)} %get-tuple-element.57), channel_id=1, source_target_pairs={{0,8},{4,12},{8,0},{12,4},{16,24},{20,28},{24,16},{28,20},{1,9},{5... | collective-permute-start | bytes 98312 | tf_op jit(solution)/shard_map/ppermute | solution.py:489
  38.0 51.2 %copy-start.27 = (f32[2,144,128]{2,1,0:T(8,128)}, f32[2,144,128]{2,1,0:T(8,128)S(1)}, u32[]{:S(2)}) copy-start(f32[2,144,128]{2,1,0:T(8,128)S(1)} %get-tuple-element.73.ylow) | copy-start | bytes 442372
  38.0 4.8 %collective-permute-start.7 = (f32[192,128]{1,0:T(8,128)S(1)}, f32[192,128]{1,0:T(8,128)S(1)}, u32[]{:S(2)}, u32[]{:S(2)}) collective-permute-start(f32[192,128]{1,0:T(8,128)S(1)} %get-tuple-element.58), channel_id=1, source_target_pairs={{0,4},{4,0},{8,12},{12,8},{16,20},{20,16},{24,28},{28,24},{1,5},{5... | collective-permute-start | bytes 294920 | tf_op jit(solution)/shard_map/ppermute | solution.py:481
  38.0 27.4 %collective-permute-start.9 = (f32[256,128]{1,0:T(8,128)}, f32[256,128]{1,0:T(8,128)}, u32[]{:S(2)}, u32[]{:S(2)}) collective-permute-start(f32[256,128]{1,0:T(8,128)} %get-tuple-element.63), channel_id=1, source_target_pairs={{0,1},{1,0},{2,3},{3,2},{4,5},{5,4},{6,7},{7,6},{8,9},{9,8},{10,11... | collective-permute-start | bytes 393224 | tf_op jit(solution)/shard_map/ppermute | solution.py:481
  40.0 25.4 %collective-permute-start.10 = (f32[256,128]{1,0:T(8,128)}, f32[256,128]{1,0:T(8,128)}, u32[]{:S(2)}, u32[]{:S(2)}) collective-permute-start(f32[256,128]{1,0:T(8,128)} %get-tuple-element.64), channel_id=1, source_target_pairs={{0,0},{1,2},{2,1},{3,3},{4,4},{5,6},{6,5},{7,7},{8,8},{9,10},{10,9... | collective-permute-start | bytes 393224 | tf_op jit(solution)/shard_map/ppermute | solution.py:482
  45.8 19.6 %all-to-all-start = ((f32[32,4,128]{2,1,0:T(4,128)}), f32[32,4,128]{2,1,0:T(4,128)S(1)}, u32[]{:S(2)}, u32[]{:S(2)}) async-start(f32[32,4,128]{2,1,0:T(4,128)} %bitcast.21), calls=%async_computation | async-start | bytes 131072 | tf_op jit(solution)/shard_map/all_to_all | solution.py:572
  52.0 7.0 %collective-permute-start.8 = (f32[128,128]{1,0:T(8,128)}, f32[128,128]{1,0:T(8,128)S(1)}, u32[]{:S(2)}, u32[]{:S(2)}) collective-permute-start(f32[128,128]{1,0:T(8,128)} %copy-done.71), channel_id=1, source_target_pairs={{0,0},{4,8},{8,4},{12,16},{16,12},{20,24},{24,20},{28,28},{1,1},{5... | collective-permute-start | bytes 196616 | tf_op jit(solution)/shard_map/ppermute | solution.py:482
  53.5 8.9 %collective-permute-start.13 = (f32[64,128]{1,0:T(8,128)}, f32[64,128]{1,0:T(8,128)S(1)}, u32[]{:S(2)}, u32[]{:S(2)}) collective-permute-start(f32[64,128]{1,0:T(8,128)} %copy-done.72), channel_id=1, source_target_pairs={{0,24},{4,28},{8,16},{12,20},{16,8},{20,12},{24,0},{28,4},{1,25},{... | collective-permute-start | bytes 98312 | tf_op jit(solution)/shard_map/ppermute | solution.py:489
  59.0 5.1 %collective-permute-start.12 = (f32[64,128]{1,0:T(8,128)}, f32[64,128]{1,0:T(8,128)S(1)}, u32[]{:S(2)}, u32[]{:S(2)}) collective-permute-start(f32[64,128]{1,0:T(8,128)} %copy-done.72), channel_id=1, source_target_pairs={{0,16},{4,20},{8,24},{12,28},{16,0},{20,4},{24,8},{28,12},{1,17},{... | collective-permute-start | bytes 98312 | tf_op jit(solution)/shard_map/ppermute | solution.py:489
  59.7 5.1 %collective-permute-start.11 = (f32[64,128]{1,0:T(8,128)}, f32[64,128]{1,0:T(8,128)S(1)}, u32[]{:S(2)}, u32[]{:S(2)}) collective-permute-start(f32[64,128]{1,0:T(8,128)} %copy-done.72), channel_id=1, source_target_pairs={{0,8},{4,12},{8,0},{12,4},{16,24},{20,28},{24,16},{28,20},{1,9},{5... | collective-permute-start | bytes 98312 | tf_op jit(solution)/shard_map/ppermute | solution.py:489
  94.0 4.6 %collective-permute-start.14 = (f32[192,128]{1,0:T(8,128)S(1)}, f32[192,128]{1,0:T(8,128)S(1)}, u32[]{:S(2)}, u32[]{:S(2)}) collective-permute-start(f32[192,128]{1,0:T(8,128)S(1)} %get-tuple-element.77), channel_id=1, source_target_pairs={{0,4},{4,0},{8,12},{12,8},{16,20},{20,16},{24,28},{28,24},{1,5},{5... | collective-permute-start | bytes 294920 | tf_op jit(solution)/shard_map/ppermute | solution.py:481
  95.0 23.9 %collective-permute-start.16 = (f32[256,128]{1,0:T(8,128)}, f32[256,128]{1,0:T(8,128)}, u32[]{:S(2)}, u32[]{:S(2)}) collective-permute-start(f32[256,128]{1,0:T(8,128)} %get-tuple-element.82), channel_id=1, source_target_pairs={{0,1},{1,0},{2,3},{3,2},{4,5},{5,4},{6,7},{7,6},{8,9},{9,8},{10,11... | collective-permute-start | bytes 393224 | tf_op jit(solution)/shard_map/ppermute | solution.py:481
  95.0 23.9 %collective-permute-start.17 = (f32[256,128]{1,0:T(8,128)}, f32[256,128]{1,0:T(8,128)}, u32[]{:S(2)}, u32[]{:S(2)}) collective-permute-start(f32[256,128]{1,0:T(8,128)} %get-tuple-element.83), channel_id=1, source_target_pairs={{0,0},{1,2},{2,1},{3,3},{4,4},{5,6},{6,5},{7,7},{8,8},{9,10},{10,9... | collective-permute-start | bytes 393224 | tf_op jit(solution)/shard_map/ppermute | solution.py:482
  101.1 17.9 %all-to-all-start.1 = ((f32[32,4,128]{2,1,0:T(4,128)}), f32[32,4,128]{2,1,0:T(4,128)S(1)}, u32[]{:S(2)}, u32[]{:S(2)}) async-start(f32[32,4,128]{2,1,0:T(4,128)} %bitcast.7), calls=%async_computation.1 | async-start | bytes 131072 | tf_op jit(solution)/shard_map/all_to_all | solution.py:572
  105.7 7.0 %collective-permute-start.15 = (f32[128,128]{1,0:T(8,128)}, f32[128,128]{1,0:T(8,128)S(1)}, u32[]{:S(2)}, u32[]{:S(2)}) collective-permute-start(f32[128,128]{1,0:T(8,128)} %copy-done.70), channel_id=1, source_target_pairs={{0,0},{4,8},{8,4},{12,16},{16,12},{20,24},{24,20},{28,28},{1,1},{5... | collective-permute-start | bytes 196616 | tf_op jit(solution)/shard_map/ppermute | solution.py:482
  107.2 8.8 %collective-permute-start.20 = (f32[64,128]{1,0:T(8,128)}, f32[64,128]{1,0:T(8,128)S(1)}, u32[]{:S(2)}, u32[]{:S(2)}) collective-permute-start(f32[64,128]{1,0:T(8,128)} %copy-done.73), channel_id=1, source_target_pairs={{0,24},{4,28},{8,16},{12,20},{16,8},{20,12},{24,0},{28,4},{1,25},{... | collective-permute-start | bytes 98312 | tf_op jit(solution)/shard_map/ppermute | solution.py:489
  112.7 5.0 %collective-permute-start.19 = (f32[64,128]{1,0:T(8,128)}, f32[64,128]{1,0:T(8,128)S(1)}, u32[]{:S(2)}, u32[]{:S(2)}) collective-permute-start(f32[64,128]{1,0:T(8,128)} %copy-done.73), channel_id=1, source_target_pairs={{0,16},{4,20},{8,24},{12,28},{16,0},{20,4},{24,8},{28,12},{1,17},{... | collective-permute-start | bytes 98312 | tf_op jit(solution)/shard_map/ppermute | solution.py:489
  112.7 5.6 %collective-permute-start.18 = (f32[64,128]{1,0:T(8,128)}, f32[64,128]{1,0:T(8,128)S(1)}, u32[]{:S(2)}, u32[]{:S(2)}) collective-permute-start(f32[64,128]{1,0:T(8,128)} %copy-done.73), channel_id=1, source_target_pairs={{0,8},{4,12},{8,0},{12,4},{16,24},{20,28},{24,16},{28,20},{1,9},{5... | collective-permute-start | bytes 98312 | tf_op jit(solution)/shard_map/ppermute | solution.py:489
  (73 other events, 187.0 us)

commit v5 on v4

--- a/solution.py
+++ b/solution.py
@@ -15,8 +15,12 @@
 EPSILON = 1e-06
 
 XO = 2
-YO = 4
+YO = 8
 CHUNK = 4
+STEP = 16
+UNROLL_FIELDS = 4
+UNROLL_MAIN = 2
+SCALE = 16.0 / BETA
 DIAGONALS = ((-1, -1), (-1, 1), (1, -1), (1, 1))
 F32 = jnp.float32
 BF16 = jnp.bfloat16
@@ -25,13 +29,13 @@
 class Geo:
     def __init__(self, nx, ny, nz, px, py):
         self.nx, self.ny, self.nz, self.px, self.py = nx, ny, nz, px, py
-        self.pl = ny + 2 * YO
-        self.ext = (nx + 8) * self.pl
+        self.pl = ny + YO
+        self.ext = (nx + 9) * self.pl
         self.xp = nx + 8
         self.cells = float(nx * px * ny * py * nz)
         self.zs = 1.0 / math.sqrt(nz)
         self.xs = 1.0 / math.sqrt(nx * px)
-        self.win = (nx + 2) * self.pl + 8
+        self.win = (nx + 2) * ny
         self.pairs = px // 2
 
     def own(self, x):
@@ -107,7 +111,7 @@
             total = total + run
             seen = seen + t_v[c * step + k]
     own[0 : g.ny, :] = run
-    own[g.ny : 2 * g.ny, :] = total * g.xs - seen
+    own[g.ny : 2 * g.ny, :] = total - seen * (1.0 / g.xs)
     for copy in small:
         copy.wait()
     at = 0
@@ -121,32 +125,40 @@
         put_pair(even, zrims[0, r].astype(F32), zrims[1, r].astype(F32), xa, xb, at)
         at += g.ny
     xa[at : at + g.ny, :] = run
-    xa[at + g.ny : at + 2 * g.ny, :] = total * g.xs - seen
-
-
-def spread_kernel(g, zones, zlow, zhigh, zone, p, low_o, high_o, q, table, ztable):
+    xa[at + g.ny : at + 2 * g.ny, :] = total - seen * (1.0 / g.xs)
+
+
+def bounds_kernel(g, zones, zlow, zhigh, zone, t, low_o, high_o, t_o):
+    def body(x, carry):
+        low_o[x], high_o[x] = bounds_of(zones, zone[x], zlow, zhigh)
+        t_o[x] = t[x] * (1.0 / g.xs)
+        return carry
+
+    lax.fori_loop(0, g.nx, body, 0, unroll=8)
+
+
+def spread_kernel(g, p, q, p_o, table, ztable):
     nz = g.nz
     row = lax.broadcasted_iota(jnp.int32, (2 * nz, 2 * nz), 0) % nz
     col = lax.broadcasted_iota(jnp.int32, (2 * nz, 2 * nz), 1)
     first = (row <= col).astype(F32)
-    second = (nz - jnp.maximum(row, col - nz)).astype(F32)
+    second = (nz - jnp.maximum(row, col - nz)).astype(F32) * (SCALE / nz)
     table[...] = jnp.where(col < nz, first, second).astype(BF16)
     r2 = lax.broadcasted_iota(jnp.int32, (2 * nz, nz), 0) % nz
     c2 = lax.broadcasted_iota(jnp.int32, (2 * nz, nz), 1)
     back = (r2 >= c2).astype(F32).astype(BF16)
     ztable[...] = ((r2 == c2 + 1).astype(F32) - (r2 == c2 - 1).astype(F32)).astype(BF16)
-    step = 8
+    step = 16
 
     def body(c, carry):
-        for k in range(step):
-            x = c * step + k
-            low_o[x], high_o[x] = bounds_of(zones, zone[x], zlow, zhigh)
-        rows = p[pl.ds(c * step, step)].reshape(step * g.ny, nz)
-        out = jnp.dot(split2(rows), back, preferred_element_type=F32) * g.zs
-        q[pl.ds(c * step, step)] = out.reshape(step, g.ny, nz)
+        here = pl.ds(c * step, step)
+        values = p[here]
+        p_o[here] = values * (1.0 / g.zs)
+        out = jnp.dot(split2(values.reshape(step * g.ny, nz)), back, preferred_element_type=F32) * (g.zs * SCALE)
+        q[here] = out.reshape(step, g.ny, nz)
         return carry
 
-    lax.fori_loop(0, g.nx // step, body, 0)
+    lax.fori_loop(0, g.nx // step, body, 0, unroll=True)
 
 
 def join_kernel(g, flags, xa, own, head, pair, sums):
@@ -177,10 +189,10 @@
     mine_t, mine_s = own[0:ny, :], own[ny : 2 * ny, :]
     other_t, other_s = xa[at : at + ny, :], xa[at + ny : at + 2 * ny, :]
     pair[0:ny, :] = mine_t + other_t
-    pair[ny : 2 * ny, :] = mine_s + other_s + jnp.where(even, mine_t, other_t) * (g.nx * g.xs)
-
-
-def sides_kernel(g, fields, flags, xa, xb, own, *refs):
+    pair[ny : 2 * ny, :] = mine_s + other_s + jnp.where(even, mine_t, other_t) * float(g.nx)
+
+
+def sides_kernel(g, fields, flags, xa, xb, own, order, *refs):
     blocks, (ya, yb, pair) = refs[:fields], refs[fields:]
     (xeven, xfirst, xlast), (yeven, _, _) = flags_of(g, flags)
     n = g.xp
@@ -237,7 +249,9 @@
 
 def alphas(g, sums):
     row = sum_row(g, sums)
-    return tuple(ETA * lax.rsqrt(lane_value(row, k) / g.cells + EPSILON) for k in range(2))
+    return tuple(
+        ETA / SCALE * lax.rsqrt(lane_value(row, k) * (1.0 / (g.cells * SCALE * SCALE)) + EPSILON) for k in range(2)
+    )
 
 
 def ray_offsets(g, flags, trs):
@@ -246,7 +260,7 @@
     even = (ix % 2) == 0
     ny = g.ny
     mine, other = trs[0, 0:ny, :], trs[1, 0:ny, :]
-    reach = float(g.nx * g.xs)
+    reach = float(g.nx)
     before = jnp.where(even, 0.0, other)
     sums = jnp.zeros_like(mine)
     spread = (mine + other) * (g.pairs - 1 - q).astype(F32)
@@ -260,118 +274,162 @@
     return before, near + sums + spread * (2.0 * reach)
 
 
+def cross(a, b):
+    return a[1] * b[2] - a[2] * b[1], a[2] * b[0] - a[0] * b[2], a[0] * b[1] - a[1] * b[0]
+
+
 def step_core(g, flags, update, rho_e, sig_e, trs, p, q, t, table, ztable, outs, scratch):
     grho, gsig, sums, own, xa, xb, ya, yb = outs
-    vxr, vxs, vyr, vys, vzr, vzs, gyr, gys, rt_s, az, bz, yu, ym = scratch
+    vxr, vxs, vyr, vys, vzr, vzs, rt_s, az, bz, yu, ym = scratch
     nx, ny, nz, w = g.nx, g.ny, g.nz, g.pl
     (even, _, _), (yeven, _, _) = flags_of(g, flags)
     zero = jnp.zeros((ny, nz), F32)
     zero8 = jnp.zeros((8, nz), F32)
     before, after = ray_offsets(g, flags, trs)
-    step = 8
-    rows = step * w
+    step = STEP
+    rows = step * ny
+    ext = ((rho_e, az), (sig_e, bz))
+
+    def span(start, size, tile=8):
+        return pl.ds(start if isinstance(start, int) or tile == 1 else pl.multiple_of(start, tile), size)
+
+    def plane(x):
+        return span((x + 1) * ny, ny)
 
     def zdiff(v):
         return jnp.dot(split2(v), ztable[...], preferred_element_type=F32)
 
-    edge = [ref[pl.ds(k * w, w), :] for ref in (rho_e, sig_e) for k in (1, XO + nx)]
-    out = zdiff(jnp.concatenate(edge, axis=0))
-    for i, (ref, k) in enumerate(((az, 1), (az, XO + nx), (bz, 1), (bz, XO + nx))):
-        ref[pl.ds(k * w, w), :] = out[i * w : (i + 1) * w]
-
-    def fields(c, carry):
+    def slopes(ref, z, x):
+        at = g.own(x)
+        sx = ref[pl.ds(at + w, ny), :] - ref[pl.ds(at - w, ny), :]
+        sy = ref[pl.ds(at + 1, ny), :] - ref[pl.ds(at - 1, ny), :]
+        return sx, sy, z[plane(x), :]
+
+    def cross_plane(x, acc, inside):
+        a = slopes(*ext[0], x)
+        b = slopes(*ext[1], x)
+        c = cross(a, b)
+        vxr[plane(x), :] = b[1] * c[2] - b[2] * c[1]
+        vxs[plane(x), :] = c[1] * a[2] - c[2] * a[1]
+        if not inside:
+            return acc
+        at = pl.ds(g.own(x), ny)
+        vyr[at, :] = b[2] * c[0] - b[0] * c[2]
+        vys[at, :] = c[2] * a[0] - c[0] * a[2]
+        vzr[plane(x), :] = b[0] * c[1] - b[1] * c[0]
+        vzs[plane(x), :] = c[0] * a[1] - c[1] * a[0]
+        return acc + fold8(c[0] * c[0] + c[1] * c[1] + c[2] * c[2])
+
+    def fields_chunk(c, carry):
         run, acc = carry
+        values = ([], [])
         for k in range(step):
             x = c * step + k
             at = pl.ds(g.own(x), ny)
             rho, sig = update(x, at)
             rho_e[at, :] = rho
             sig_e[at, :] = sig
+            values[0].append(rho)
+            values[1].append(sig)
             run = run + sig
-            miss = run * g.xs - t[x]
-            rt_s[pl.ds(x * ny, ny), :] = miss
+            miss = run - t[x]
+            rt_s[span(x * ny, ny), :] = miss
             acc = acc + fold8(miss * miss)
-        at = pl.ds((c * step + XO) * w, rows)
-        pieces = split2(rho_e[at, :])
-        az[at, :] = jnp.dot(pieces, ztable[...], preferred_element_type=F32)
-        y = jnp.dot(pieces, table[...], preferred_element_type=F32)
+        at = span(c * rows + ny, rows)
+        pieces = split2(jnp.concatenate(values[0] + values[1], axis=0))
+        y = jnp.dot(pieces[:rows], table[...], preferred_element_type=F32)
         yu[at, :] = y[:, :nz]
         ym[at, :] = y[:, nz:]
-        bz[at, :] = zdiff(sig_e[at, :])
+        z = jnp.dot(pieces, ztable[...], preferred_element_type=F32)
+        az[at, :] = z[:rows]
+        bz[at, :] = z[rows:]
         return run, acc
 
-    _, acc_t = lax.fori_loop(0, nx // step, fields, (before, zero8), unroll=True)
-
-    rowid = lax.broadcasted_iota(jnp.int32, (w, nz), 0)
-    mine = jnp.logical_and(rowid >= 1, rowid <= ny)
-
-    def slopes(ref, z, base):
-        sx = ref[pl.ds(base + w, w), :] - ref[pl.ds(base - w, w), :]
-        sy = ref[pl.ds(base + 1, w), :] - ref[pl.ds(base - 1, w), :]
-        return sx, sy, z[pl.ds(base, w), :]
-
-    def cross_plane(xi, acc, inside):
-        base = (xi + XO - 1) * w + YO - 1
-        a0, a1, a2 = slopes(rho_e, az, base)
-        b0, b1, b2 = slopes(sig_e, bz, base)
-        c0 = a1 * b2 - a2 * b1
-        c1 = a2 * b0 - a0 * b2
-        c2 = a0 * b1 - a1 * b0
-        at = pl.ds(pl.multiple_of(xi * w, 8), w)
-        vxr[at, :] = b1 * c2 - b2 * c1
-        vxs[at, :] = c1 * a2 - c2 * a1
-        if not inside:
-            return acc
-        vyr[at, :] = b2 * c0 - b0 * c2
-        vys[at, :] = c2 * a0 - c0 * a2
-        vzr[at, :] = b0 * c1 - b1 * c0
-        vzs[at, :] = c0 * a1 - c1 * a0
-        return acc + fold8(jnp.where(mine, c0 * c0 + c1 * c1 + c2 * c2, 0.0))
-
-    cross_plane(0, None, False)
-    cross_plane(nx + 1, None, False)
-    acc_c = lax.fori_loop(1, nx + 1, lambda xi, acc: cross_plane(xi, acc, True), zero8, unroll=4)
-
-    def adjoints(c, carry):
-        start = (1 + c * step) * w
-        at = pl.ds(pl.multiple_of(start, 8), rows)
-        for vy, vz, out in ((vyr, vzr, gyr), (vys, vzs, gys)):
-            along_y = vy[pl.ds(start - 1, rows), :] - vy[pl.ds(start + 1, rows), :]
-            out[at, :] = along_y - zdiff(vz[at, :])
+    chunks = nx // step
+    _, acc_t = lax.fori_loop(0, chunks, fields_chunk, (before, zero8), unroll=UNROLL_FIELDS)
+
+    lines = (-1, ny)
+    line = lambda ref, x, y: ref[pl.ds((XO + x) * w + YO + y, nx, stride=w), :]
+    flat = lambda ref, x: ref[g.own(x) : g.own(x) + ny, :]
+    pieces = [line(ref, 0, y) for ref, _ in ext for y in lines] + [flat(ref, x) for ref, _ in ext for x in (-1, nx)]
+    deep = zdiff(jnp.concatenate(pieces, axis=0))
+    for k, y in enumerate(lines):
+        fields = []
+        for f, (ref, _) in enumerate(ext):
+            at = (2 * f + k) * nx
+            fields.append((line(ref, 1, y) - line(ref, -1, y), line(ref, 0, y + 1) - line(ref, 0, y - 1), deep[at : at + nx]))
+        a, b = fields
+        c = cross(a, b)
+        spot = pl.ds(XO * w + YO + y, nx, stride=w)
+        vyr[spot, :] = b[2] * c[0] - b[0] * c[2]
+        vys[spot, :] = c[2] * a[0] - c[0] * a[2]
+    base = 4 * nx
+    for k, x in enumerate((-1, nx)):
+        for f, (_, z) in enumerate(ext):
+            at = base + (2 * f + k) * ny
+            z[plane(x), :] = deep[at : at + ny]
+
+    def gradient_plane(x, carry):
+        back, sum_t, sum_r, nr, ns, acc = carry
+        at = g.own(x)
+        here = plane(x)
+        flat_at = span(x * ny, ny)
+
+        def term(vx, vy, vz):
+            along_x = vx[plane(x - 1), :] - vx[plane(x + 1), :]
+            along_y = vy[pl.ds(at - 1, ny), :] - vy[pl.ds(at + 1, ny), :]
+            return along_x + along_y - vz[here, :]
+
+        back = back + rt_s[flat_at, :]
+        miss = yu[here, :] - p[x]
+        gr = ym[here, :] - q[x] + term(vxr, vyr, vzr)
+        gs = back * (SCALE * g.xs * g.xs) + term(vxs, vys, vzs)
+        grho[flat_at, :] = gr
+        gsig[flat_at, :] = gs
+        sum_t = sum_t + gs
+        return back, sum_t, sum_r + sum_t, nr + fold8(gr * gr), ns + fold8(gs * gs), acc + fold8(miss * miss)
+
+    def crosses(c, acc):
+        for k in range(step):
+            acc = cross_plane(c * step + step - 1 - k, acc, True)
+        return acc
+
+    def adjoint(c):
+        at = span(c * rows + ny, rows)
+        z = zdiff(jnp.concatenate([vzr[at, :], vzs[at, :]], axis=0))
+        vzr[at, :] = z[:rows]
+        vzs[at, :] = z[rows:]
+
+    def gradients(c, carry):
+        for k in range(step):
+            carry = gradient_plane(c * step + step - 1 - k, carry)
         return carry
 
-    lax.fori_loop(0, nx // step, adjoints, 0, unroll=True)
-
-    def gradients(i, carry):
-        back, sum_t, sum_r, nr, ns, acc = carry
-        x = nx - 1 - i
-        lower = pl.ds(x * w + 1, ny)
-        here = pl.ds((x + 1) * w + 1, ny)
-        upper = pl.ds((x + 2) * w + 1, ny)
-        at = pl.ds(g.own(x), ny)
-        cr = (vxr[lower, :] - vxr[upper, :] + gyr[here, :]) * (BETA / 16.0)
-        cs = (vxs[lower, :] - vxs[upper, :] + gys[here, :]) * (BETA / 16.0)
-        back = back + rt_s[pl.ds(x * ny, ny), :]
-        miss = yu[at, :] * g.zs - p[x]
-        gr = ym[at, :] * (g.zs * g.zs) - q[x] + cr
-        gs = back * g.xs + cs
-        out = pl.ds(pl.multiple_of(x * ny, 8), ny)
-        grho[out, :] = gr
-        gsig[out, :] = gs
-        weight = (i + 1).astype(F32)
-        return (back, sum_t + gs, sum_r + gs * weight, nr + fold8(gr * gr), ns + fold8(gs * gs),
-                acc + fold8(miss * miss))
-
-    start = (after, zero, zero, zero8, zero8, zero8)
-    _, sum_t, sum_r, nr, ns, acc_p = lax.fori_loop(0, nx, gradients, start, unroll=8)
+    carry = (after, zero, zero, zero8, zero8, zero8)
+    cross_plane(-1, None, False)
+    cross_plane(nx, None, False)
+    acc_c = crosses(chunks - 1, zero8)
+    acc_c = crosses(chunks - 2, acc_c)
+    adjoint(chunks - 1)
+
+    def main(i, carry):
+        c = chunks - 3 - i
+        acc = crosses(c, carry[0])
+        adjoint(c + 1)
+        return acc, gradients(c + 2, carry[1])
+
+    acc_c, carry = lax.fori_loop(0, chunks - 2, main, (acc_c, carry), unroll=UNROLL_MAIN)
+    adjoint(0)
+    carry = gradients(1, carry)
+    _, sum_t, sum_r, nr, ns, acc_p = gradients(0, carry)
 
     total = lambda v: jnp.sum(jnp.sum(v, axis=0, keepdims=True), axis=1, keepdims=True)
     spread = sums.shape[0] if own is None else 8
     lane = lax.broadcasted_iota(jnp.int32, (spread, nz), 1)
-    obj = acc_t + acc_p + acc_c * (BETA / 16.0)
+    obj = acc_t * (g.xs * g.xs) + acc_p * (g.zs * g.zs) + acc_c * (BETA / 16.0)
     sums[0:spread, :] = jnp.where(lane == 0, total(nr), jnp.where(lane == 1, total(ns), jnp.where(lane == 2, total(obj), 0.0)))
     if own is not None:
-        rest = sum_r * g.xs
+        rest = sum_t * (nx + 1.0) - sum_r
         pos = 0
         for block in (grho, gsig):
             for r in range(2):
@@ -453,21 +511,31 @@
     step_core(g, flags, update, rho_e, sig_e, trs, p, q, t, table, ztable, outs, scratch)
 
 
-def closing_kernel(g, sums0, sums1, sums2, grho, gsig, rho_e, sig_e, low, high, rho_o, sig_o, obj):
+def closing_kernel(g, sums0, sums1, sums2, grho, gsig, rho_e, sig_e, low, high, rho_o, sig_o, obj, rho_v, sig_v, sems):
     ar, asig = alphas(g, sums2)
-
-    def body(x, carry):
-        at = pl.ds(g.own(x), g.ny)
-        here = pl.ds(pl.multiple_of(x * g.ny, 8), g.ny)
-        rho_o[x] = jnp.minimum(jnp.maximum(rho_e[at, :] - ar * grho[here, :], low[x]), high[x])
-        sig_o[x] = sig_e[at, :] - asig * gsig[here, :]
-        return carry
-
-    lax.fori_loop(0, g.nx, body, 0, unroll=4)
+    step = 8
+    copies = []
+    for c in range(g.nx // step):
+
+        def body(k, carry):
+            x = c * step + k
+            at = pl.ds(g.own(x), g.ny)
+            here = pl.ds(pl.multiple_of(x * g.ny, 8), g.ny)
+            rho_v[x] = jnp.minimum(jnp.maximum(rho_e[at, :] - ar * grho[here, :], low[x]), high[x])
+            sig_v[x] = sig_e[at, :] - asig * gsig[here, :]
+            return carry
+
+        lax.fori_loop(0, step, body, 0, unroll=True)
+        here = pl.ds(c * step, step)
+        for k, (v, o) in enumerate(((rho_v, rho_o), (sig_v, sig_o))):
+            copies.append(pltpu.make_async_copy(v.at[here], o.at[here], sems.at[2 * c + k]))
+            copies[-1].start()
     for k, sums in enumerate((sums0, sums1, sums2)):
         row = sum_row(g, sums)
         lane = lax.broadcasted_iota(jnp.int32, row.shape, 1)
         obj[k] = jnp.sum(jnp.where(lane == 2, row, 0.0)) * (0.5 / g.cells)
+    for copy in copies:
+        copy.wait()
 
 
 def pairs_of(size):
@@ -527,7 +595,7 @@
     ybound = ((2, 2 * g.xp, nz), F32)
     win = pltpu.VMEM((g.win, nz), F32)
     ext_v = pltpu.VMEM((g.ext, nz), F32)
-    core_scratch = [win] * 8 + [pltpu.VMEM((nx * ny, nz), F32)] + [ext_v] * 4
+    core_scratch = [win] * 2 + [ext_v] * 2 + [win] * 2 + [pltpu.VMEM((nx * ny, nz), F32)] + [win] * 4
 
     own, xa, xb = call(
         functools.partial(first_kernel, g), [own_shape, xa_shape(3), xb_shape(3)],
@@ -536,15 +604,18 @@
          pltpu.VMEM((nx, ny, nz), F32), pltpu.VMEM((nx, ny, nz), F32), pltpu.SemaphoreType.DMA((4 + nx // 4,))],
     )
     xa, xb = exchange("gx", xa, xb)
-    low, high, q, table, ztable = call(
-        functools.partial(spread_kernel, g, zones),
-        [block] * 3 + [((2 * nz, 2 * nz), BF16), ((2 * nz, nz), BF16)],
-        [SMEM, SMEM] + [VMEM] * 2, (zone_low, zone_high, zone_map, pressure_obs),
+    low, high, t = call(
+        functools.partial(bounds_kernel, g, zones), [block] * 3,
+        [SMEM, SMEM] + [VMEM] * 2, (zone_low, zone_high, zone_map, time_obs),
+    )
+    q, p, table, ztable = call(
+        functools.partial(spread_kernel, g),
+        [block] * 2 + [((2 * nz, 2 * nz), BF16), ((2 * nz, nz), BF16)], [VMEM], (pressure_obs,),
     )
     as_rows = lambda v: v.reshape(nx * ny, nz)
     ya, yb, pair = call(
         functools.partial(sides_kernel, g, 3), [ymsg(3)] * 2 + [own_shape],
-        [SMEM] + [VMEM] * 6, (flags, xa, xb, own, as_rows(density), as_rows(slowness), as_rows(zone_map)),
+        [SMEM] + [VMEM] * 7, (flags, xa, xb, own, low, as_rows(density), as_rows(slowness), as_rows(zone_map)),
     )
     ya, yb = exchange("gy", ya, yb)
     others = pair_totals(pair, px)
@@ -555,7 +626,7 @@
         functools.partial(opening_step, g, zones),
         [ext, ext, trs_shape, xbound, xbound, ybound, ybound] + ends,
         [SMEM] * 3 + [VMEM] * (12 + len(others)),
-        (flags, zone_low, zone_high, xa, xb, ya, yb, own, density, slowness, pressure_obs, q, time_obs, table, ztable, *others),
+        (flags, zone_low, zone_high, xa, xb, ya, yb, own, density, slowness, p, q, t, table, ztable, *others),
         core_scratch, 24,
     )
     rho_e, sig_e, trs, xlow, xhigh, ylow, yhigh, grho, gsig, head, own, xa, xb, ya, yb = outs
@@ -575,7 +646,7 @@
             functools.partial(later_step, g, last), [ext, ext, trs_shape] + ([flat, flat, sums_shape] if last else ends),
             [SMEM] + [VMEM] * (22 + len(others)),
             (flags, xa, xb, ya, yb, sums, own, grho, gsig, rho_e, sig_e, low, high, xlow, xhigh, ylow, yhigh, trs,
-             pressure_obs, q, time_obs, table, ztable, *others),
+             p, q, t, table, ztable, *others),
             core_scratch, 24,
         )
         rho_e, sig_e, trs, grho, gsig, head = outs[:6]
@@ -584,7 +655,8 @@
     history.append(lax.all_to_all(head, both, 0, 0, tiled=True))
     rho, sigma, obj = call(
         functools.partial(closing_kernel, g), [block, block, ((ITERS,), F32)],
-        [VMEM] * 9, (*history, grho, gsig, rho_e, sig_e, low, high), outs=[VMEM, VMEM, SMEM],
+        [VMEM] * 9, (*history, grho, gsig, rho_e, sig_e, low, high),
+        [pltpu.VMEM((nx, ny, nz), F32)] * 2 + [pltpu.SemaphoreType.DMA((nx // 4,))], outs=[HBM, HBM, SMEM],
     )
     return rho, sigma, obj
 

time: 157 us -> 153 us (0.975)
  Pallas kernels: 30.1 us -> 26.9 us
  waiting for transfers between devices: 9.42 us -> 12.4 us
  starting transfers between devices: 49.1 us -> 46.8 us
    ppermute x9, waiting for transfers between devices: 4.55 us -> 7.96 us  [pair_totals(): out.append(lax.ppermute(pair, 'gx', [(i, i ^ 2 * m) for i in range(size)]))]
    pallas_call x9 -> x10, Pallas kernels: 30.1 us -> 26.9 us  [call(): pl.pallas_call(body, out_shape=[jax.ShapeDtypeStruct(s, d) for s, d in sh...]
    all_to_all x2, starting transfers between devices: 10.8 us -> 9.12 us  [local(): sums = lax.all_to_all(sums, both, 0, 0, tiled=True)]
  transfers between devices with their start and end apart: 23 -> 23, of which waited for: 8 -> 9; matrix products, arithmetic and copies ran while one was open for 0% -> 0% of each run, Pallas kernels for 3% -> 2%
where the time goes in v5:
time: 153 us; the launch traced here: 151 us
  local copies, waits for them, and re-layouts  53.4 us (35%)
  starting transfers between devices  46.8 us (31%)
  Pallas kernels  26.9 us (18%)
  waiting for transfers between devices  12.4 us (8%)
  blocking collectives  10.7 us (7%)
    unnamed x148, local copies, waits for them, and re-layouts  53.4 us
    pallas_call x10, Pallas kernels, call(): pl.pallas_call(body, out_shape=[jax.ShapeDtypeStruct(s, d) for s, d in sh...  26.9 us
    ppermute x9, starting transfers between devices, pair_totals(): out.append(lax.ppermute(pair, 'gx', [(i, i ^ 2 * m) for i in range(size)]))  23.5 us
    all_to_all x1, blocking collectives, local(): history.append(lax.all_to_all(head, both, 0, 0, tiled=True))  10.7 us
    all_to_all x2, starting transfers between devices, local(): sums = lax.all_to_all(sums, both, 0, 0, tiled=True)  9.12 us
    ppermute x6, starting transfers between devices, exchange(): b = lax.ppermute(b, axis, pb)  8.61 us
    ppermute x9, waiting for transfers between devices, pair_totals(): out.append(lax.ppermute(pair, 'gx', [(i, i ^ 2 * m) for i in range(size)]))  7.96 us
    ppermute x6, starting transfers between devices, exchange(): a = lax.ppermute(a, axis, pa)  5.58 us
  transfers between devices with their start and end apart: 23, of which 9 were waited for; matrix products, arithmetic and copies ran while one was open for 0% of the time, Pallas kernels for 2%

profile of v5, /device:TPU:0, one launch (start us, length us, event | category | flops | bytes accessed | tf_op | source)
XLA Modules:
  0.0 151.3 jit_solution(12182330037492530263)
XLA Ops:
  0.7 2.4 %shard_map.94 = (f32[64,128]{1,0:T(8,128)S(1)}, f32[256,128]{1,0:T(8,128)S(1)}, f32[192,128]{1,0:T(8,128)S(1)}) custom-call(s32[2]{0:T(128)S(1)} %pad_add_fusion.flags, f32[64,32,128]{2,1,0:T(8,128)} %rho.3, f32[64,32,128]{2,1,0:T(8,128)} %sig.1, s32[64,32,128]{2,1,0:T(8,128)} %zone.3, f32[64,32,128]{2,1,0:T(8,128)} %t.3), custom_call_target="tpu_custom_call" | custom-call | tf_op jit(solution)/shard_map/pallas_call | solution.py:567
  3.2 3.0 %collective-permute-start = (f32[256,128]{1,0:T(8,128)S(1)}, f32[256,128]{1,0:T(8,128)S(1)}, u32[]{:S(2)}, u32[]{:S(2)}) collective-permute-start(f32[256,128]{1,0:T(8,128)S(1)} %get-tuple-element.51), channel_id=1, source_target_pairs={{0,4},{4,0},{8,12},{12,8},{16,20},{20,16},{24,28},{28,24},{1,5},{5... | collective-permute-start | bytes 393224 | tf_op jit(solution)/shard_map/ppermute | solution.py:549
  6.9 1.5 shard_map.95
  11.3 7.6 %collective-permute-start.6 = (f32[64,128]{1,0:T(8,128)S(1)}, f32[64,128]{1,0:T(8,128)S(1)}, u32[]{:S(2)}, u32[]{:S(2)}) collective-permute-start(f32[64,128]{1,0:T(8,128)S(1)} %get-tuple-element.62), channel_id=1, source_target_pairs={{0,24},{4,28},{8,16},{12,20},{16,8},{20,12},{24,0},{28,4},{1,25},{... | collective-permute-start | bytes 98312 | tf_op jit(solution)/shard_map/ppermute | solution.py:557
  20.8 2.9 %collective-permute-done.5.refs_1_ = f32[64,128]{1,0:T(8,128)S(1)} collective-permute-done((f32[64,128]{1,0:T(8,128)S(1)}, f32[64,128]{1,0:T(8,128)S(1)}, u32[]{:S(2)}, u32[]{:S(2)}) %collective-permute-start.5) | collective-permute-done | bytes 32800 | tf_op jit(solution)/shard_map/ppermute | solution.py:557
  23.7 5.8 %shard_map.98 = (f32[2920,128]{1,0:T(8,128)S(1)}, f32[2920,128]{1,0:T(8,128)S(1)}, f32[5,64,128]{2,1,0:T(8,128)S(1)}, f32[2,64,128]{2,1,0:T(8,128)S(1)}, f32[2,6...) custom-call(s32[2]{0:T(128)S(1)} %pad_add_fusion.flags, ...), custom_call_target="tpu_custom_call" | custom-call | tf_op jit(solution)/shard_map/pallas_call | solution.py:567
  36.9 1.4 collective-permute-start.9
  38.4 2.1 %collective-permute-start.10 = (f32[256,128]{1,0:T(8,128)}, f32[256,128]{1,0:T(8,128)}, u32[]{:S(2)}, u32[]{:S(2)}) collective-permute-start(f32[256,128]{1,0:T(8,128)} %get-tuple-element.69), channel_id=1, source_target_pairs={{0,0},{1,2},{2,1},{3,3},{4,4},{5,6},{6,5},{7,7},{8,8},{9,10},{10,9... | collective-permute-start | bytes 393224 | tf_op jit(solution)/shard_map/ppermute | solution.py:550
  40.5 1.6 %collective-permute-done.7.xa = f32[192,128]{1,0:T(8,128)S(1)} collective-permute-done((f32[192,128]{1,0:T(8,128)S(1)}, f32[192,128]{1,0:T(8,128)S(1)}, u32[]{:S(2)}, u32[]{:S(2)}) %collective-permute-start.7) | collective-permute-done | bytes 98336 | tf_op jit(solution)/shard_map/ppermute | solution.py:549
  45.2 4.5 %all-to-all-start = ((f32[32,4,128]{2,1,0:T(4,128)}), f32[32,4,128]{2,1,0:T(4,128)S(1)}, u32[]{:S(2)}, u32[]{:S(2)}) async-start(f32[32,4,128]{2,1,0:T(4,128)} %bitcast.21), calls=%async_computation | async-start | bytes 131072 | tf_op jit(solution)/shard_map/all_to_all | solution.py:643
  49.7 1.5 collective-permute-start.8
  51.2 5.5 %collective-permute-start.13 = (f32[64,128]{1,0:T(8,128)}, f32[64,128]{1,0:T(8,128)S(1)}, u32[]{:S(2)}, u32[]{:S(2)}) collective-permute-start(f32[64,128]{1,0:T(8,128)} %copy-done.72), channel_id=1, source_target_pairs={{0,24},{4,28},{8,16},{12,20},{16,8},{20,12},{24,0},{28,4},{1,25},{... | collective-permute-start | bytes 98312 | tf_op jit(solution)/shard_map/ppermute | solution.py:557
  57.4 2.1 %collective-permute-start.11 = (f32[64,128]{1,0:T(8,128)}, f32[64,128]{1,0:T(8,128)S(1)}, u32[]{:S(2)}, u32[]{:S(2)}) collective-permute-start(f32[64,128]{1,0:T(8,128)} %copy-done.72), channel_id=1, source_target_pairs={{0,8},{4,12},{8,0},{12,4},{16,24},{20,28},{24,16},{28,20},{1,9},{5... | collective-permute-start | bytes 98312 | tf_op jit(solution)/shard_map/ppermute | solution.py:557
  65.6 1.4 copy-done.15
  79.7 6.3 %shard_map.100 = (f32[2920,128]{1,0:T(8,128)S(1)}, f32[2920,128]{1,0:T(8,128)S(1)}, f32[5,64,128]{2,1,0:T(8,128)S(1)}, f32[2048,128]{1,0:T(8,128)S(1)}, f32[2048...) custom-call(s32[2]{0:T(128)S(1)} %copy-done.66, ...), custom_call_target="tpu_custom_call" | custom-call | tf_op jit(solution)/shard_map/pallas_call | solution.py:567
  92.0 2.1 %collective-permute-start.17 = (f32[256,128]{1,0:T(8,128)}, f32[256,128]{1,0:T(8,128)}, u32[]{:S(2)}, u32[]{:S(2)}) collective-permute-start(f32[256,128]{1,0:T(8,128)} %get-tuple-element.87), channel_id=1, source_target_pairs={{0,0},{1,2},{2,1},{3,3},{4,4},{5,6},{6,5},{7,7},{8,8},{9,10},{10,9... | collective-permute-start | bytes 393224 | tf_op jit(solution)/shard_map/ppermute | solution.py:550
  94.1 1.4 collective-permute-done.14.xa
  98.0 4.6 %all-to-all-start.1 = ((f32[32,4,128]{2,1,0:T(4,128)}), f32[32,4,128]{2,1,0:T(4,128)S(1)}, u32[]{:S(2)}, u32[]{:S(2)}) async-start(f32[32,4,128]{2,1,0:T(4,128)} %bitcast.7), calls=%async_computation.1 | async-start | bytes 131072 | tf_op jit(solution)/shard_map/all_to_all | solution.py:643
  102.6 1.5 collective-permute-start.15
  104.1 5.7 %collective-permute-start.20 = (f32[64,128]{1,0:T(8,128)}, f32[64,128]{1,0:T(8,128)S(1)}, u32[]{:S(2)}, u32[]{:S(2)}) collective-permute-start(f32[64,128]{1,0:T(8,128)} %copy-done.73), channel_id=1, source_target_pairs={{0,24},{4,28},{8,16},{12,20},{16,8},{20,12},{24,0},{28,4},{1,25},{... | collective-permute-start | bytes 98312 | tf_op jit(solution)/shard_map/ppermute | solution.py:557
  109.8 1.9 %collective-permute-start.18 = (f32[64,128]{1,0:T(8,128)}, f32[64,128]{1,0:T(8,128)S(1)}, u32[]{:S(2)}, u32[]{:S(2)}) collective-permute-start(f32[64,128]{1,0:T(8,128)} %copy-done.73), channel_id=1, source_target_pairs={{0,8},{4,12},{8,0},{12,4},{16,24},{20,28},{24,16},{28,20},{1,9},{5... | collective-permute-start | bytes 98312 | tf_op jit(solution)/shard_map/ppermute | solution.py:557
  132.7 5.7 %shard_map.102 = (f32[2920,128]{1,0:T(8,128)S(1)}, f32[2920,128]{1,0:T(8,128)S(1)}, f32[5,64,128]{2,1,0:T(8,128)}, f32[2048,128]{1,0:T(8,128)S(1)}, f32[2048,128]{1,0:T(8,128)S(1)}, /*index=5*/f32[32,128]{1,0:T(8,128)S(1)}) custom-call(s32[2]{0:T(128)S(1)} %copy-done.67, f32[192,128]{1,0:T(8,128)S(1)} %copy-done.33, ...), custom_call_target="tpu_custom_call" | custom-call | tf_op jit(solution)/shard_map/pallas_call | solution.py:567
  138.4 10.7 %all_to_all.33 = f32[32,1,128]{2,1,0:T(1,128)S(1)} all-to-all(f32[32,1,128]{2,1,0:T(1,128)S(1)} %bitcast.22), channel_id=1, replica_groups=mesh['gx'=8,'gy'=4] {'gx','gy'}, dimensions={0} | all-to-all | bytes 32768 | tf_op jit(solution)/shard_map/all_to_all | solution.py:655
  149.1 2.1 %shard_map.103 = (f32[64,32,128]{2,1,0:T(8,128)}, f32[64,32,128]{2,1,0:T(8,128)}, f32[3]{0:T(128)}) custom-call(f32[128,128]{1,0:T(8,128)S(1)} %bitcast.17, f32[128,128]{1,0:T(8,128)S(1)} %bitcast.19, f32[32,128]{1,0:T(8,128)S(1)} %bitcast.20, f32[2048,128]{1,0:T(8,128)S(1)} %get-tuple-element.95.grho, f32[2048,128]{1,0:T(8,128)S(1)} %get-tuple-element.96.gsig, ...), custom_call_target="tpu_custom_call" | custom-call | tf_op jit(solution)/shard_map/pallas_call | solution.py:567
  (182 shorter events, 64.7 us)
Async XLA Ops:
  3.2 6.5 %collective-permute-start = (f32[256,128]{1,0:T(8,128)S(1)}, f32[256,128]{1,0:T(8,128)S(1)}, u32[]{:S(2)}, u32[]{:S(2)}) collective-permute-start(f32[256,128]{1,0:T(8,128)S(1)} %get-tuple-element.51), channel_id=1, source_target_pairs={{0,4},{4,0},{8,12},{12,8},{16,20},{20,16},{24,28},{28,24},{1,5},{5... | collective-permute-start | bytes 393224 | tf_op jit(solution)/shard_map/ppermute | solution.py:549
  6.2 2.2 %collective-permute-start.1 = (f32[192,128]{1,0:T(8,128)S(1)}, f32[192,128]{1,0:T(8,128)S(1)}, u32[]{:S(2)}, u32[]{:S(2)}) collective-permute-start(f32[192,128]{1,0:T(8,128)S(1)} %get-tuple-element.52), channel_id=1, source_target_pairs={{0,0},{4,8},{8,4},{12,16},{16,12},{20,24},{24,20},{28,28},{1,1},{5... | collective-permute-start | bytes 294920 | tf_op jit(solution)/shard_map/ppermute | solution.py:550
  10.5 13.2 %collective-permute-start.2 = (f32[432,128]{1,0:T(8,128)S(1)}, f32[432,128]{1,0:T(8,128)S(1)}, u32[]{:S(2)}, u32[]{:S(2)}) collective-permute-start(f32[432,128]{1,0:T(8,128)S(1)} %get-tuple-element.55), channel_id=1, source_target_pairs={{0,1},{1,0},{2,3},{3,2},{4,5},{5,4},{6,7},{7,6},{8,9},{9,8},{10,11... | collective-permute-start | bytes 663560 | tf_op jit(solution)/shard_map/ppermute | solution.py:549
  10.6 13.1 %collective-permute-start.3 = (f32[432,128]{1,0:T(8,128)S(1)}, f32[432,128]{1,0:T(8,128)S(1)}, u32[]{:S(2)}, u32[]{:S(2)}) collective-permute-start(f32[432,128]{1,0:T(8,128)S(1)} %get-tuple-element.56), channel_id=1, source_target_pairs={{0,0},{1,2},{2,1},{3,3},{4,4},{5,6},{6,5},{7,7},{8,8},{9,10},{10,9... | collective-permute-start | bytes 663560 | tf_op jit(solution)/shard_map/ppermute | solution.py:550
  11.3 9.5 %collective-permute-start.6 = (f32[64,128]{1,0:T(8,128)S(1)}, f32[64,128]{1,0:T(8,128)S(1)}, u32[]{:S(2)}, u32[]{:S(2)}) collective-permute-start(f32[64,128]{1,0:T(8,128)S(1)} %get-tuple-element.62), channel_id=1, source_target_pairs={{0,24},{4,28},{8,16},{12,20},{16,8},{20,12},{24,0},{28,4},{1,25},{... | collective-permute-start | bytes 98312 | tf_op jit(solution)/shard_map/ppermute | solution.py:557
  18.9 4.8 %collective-permute-start.5 = (f32[64,128]{1,0:T(8,128)S(1)}, f32[64,128]{1,0:T(8,128)S(1)}, u32[]{:S(2)}, u32[]{:S(2)}) collective-permute-start(f32[64,128]{1,0:T(8,128)S(1)} %get-tuple-element.62), channel_id=1, source_target_pairs={{0,16},{4,20},{8,24},{12,28},{16,0},{20,4},{24,8},{28,12},{1,17},{... | collective-permute-start | bytes 98312 | tf_op jit(solution)/shard_map/ppermute | solution.py:557
  18.9 4.8 %collective-permute-start.4 = (f32[64,128]{1,0:T(8,128)S(1)}, f32[64,128]{1,0:T(8,128)S(1)}, u32[]{:S(2)}, u32[]{:S(2)}) collective-permute-start(f32[64,128]{1,0:T(8,128)S(1)} %get-tuple-element.62), channel_id=1, source_target_pairs={{0,8},{4,12},{8,0},{12,4},{16,24},{20,28},{24,16},{28,20},{1,9},{5... | collective-permute-start | bytes 98312 | tf_op jit(solution)/shard_map/ppermute | solution.py:557
  36.9 49.1 %copy-start.27 = (f32[2,144,128]{2,1,0:T(8,128)}, f32[2,144,128]{2,1,0:T(8,128)S(1)}, u32[]{:S(2)}) copy-start(f32[2,144,128]{2,1,0:T(8,128)S(1)} %get-tuple-element.77.ylow) | copy-start | bytes 442372
  36.9 5.2 %collective-permute-start.7 = (f32[192,128]{1,0:T(8,128)S(1)}, f32[192,128]{1,0:T(8,128)S(1)}, u32[]{:S(2)}, u32[]{:S(2)}) collective-permute-start(f32[192,128]{1,0:T(8,128)S(1)} %get-tuple-element.63), channel_id=1, source_target_pairs={{0,4},{4,0},{8,12},{12,8},{16,20},{20,16},{24,28},{28,24},{1,5},{5... | collective-permute-start | bytes 294920 | tf_op jit(solution)/shard_map/ppermute | solution.py:549
  36.9 26.2 %collective-permute-start.9 = (f32[256,128]{1,0:T(8,128)}, f32[256,128]{1,0:T(8,128)}, u32[]{:S(2)}, u32[]{:S(2)}) collective-permute-start(f32[256,128]{1,0:T(8,128)} %get-tuple-element.68), channel_id=1, source_target_pairs={{0,1},{1,0},{2,3},{3,2},{4,5},{5,4},{6,7},{7,6},{8,9},{9,8},{10,11... | collective-permute-start | bytes 393224 | tf_op jit(solution)/shard_map/ppermute | solution.py:549
  38.4 24.7 %collective-permute-start.10 = (f32[256,128]{1,0:T(8,128)}, f32[256,128]{1,0:T(8,128)}, u32[]{:S(2)}, u32[]{:S(2)}) collective-permute-start(f32[256,128]{1,0:T(8,128)} %get-tuple-element.69), channel_id=1, source_target_pairs={{0,0},{1,2},{2,1},{3,3},{4,4},{5,6},{6,5},{7,7},{8,8},{9,10},{10,9... | collective-permute-start | bytes 393224 | tf_op jit(solution)/shard_map/ppermute | solution.py:550
  45.2 17.9 %all-to-all-start = ((f32[32,4,128]{2,1,0:T(4,128)}), f32[32,4,128]{2,1,0:T(4,128)S(1)}, u32[]{:S(2)}, u32[]{:S(2)}) async-start(f32[32,4,128]{2,1,0:T(4,128)} %bitcast.21), calls=%async_computation | async-start | bytes 131072 | tf_op jit(solution)/shard_map/all_to_all | solution.py:643
  49.7 7.0 %collective-permute-start.8 = (f32[128,128]{1,0:T(8,128)}, f32[128,128]{1,0:T(8,128)S(1)}, u32[]{:S(2)}, u32[]{:S(2)}) collective-permute-start(f32[128,128]{1,0:T(8,128)} %copy-done.71), channel_id=1, source_target_pairs={{0,0},{4,8},{8,4},{12,16},{16,12},{20,24},{24,20},{28,28},{1,1},{5... | collective-permute-start | bytes 196616 | tf_op jit(solution)/shard_map/ppermute | solution.py:550
  51.2 8.9 %collective-permute-start.13 = (f32[64,128]{1,0:T(8,128)}, f32[64,128]{1,0:T(8,128)S(1)}, u32[]{:S(2)}, u32[]{:S(2)}) collective-permute-start(f32[64,128]{1,0:T(8,128)} %copy-done.72), channel_id=1, source_target_pairs={{0,24},{4,28},{8,16},{12,20},{16,8},{20,12},{24,0},{28,4},{1,25},{... | collective-permute-start | bytes 98312 | tf_op jit(solution)/shard_map/ppermute | solution.py:557
  56.8 5.1 %collective-permute-start.12 = (f32[64,128]{1,0:T(8,128)}, f32[64,128]{1,0:T(8,128)S(1)}, u32[]{:S(2)}, u32[]{:S(2)}) collective-permute-start(f32[64,128]{1,0:T(8,128)} %copy-done.72), channel_id=1, source_target_pairs={{0,16},{4,20},{8,24},{12,28},{16,0},{20,4},{24,8},{28,12},{1,17},{... | collective-permute-start | bytes 98312 | tf_op jit(solution)/shard_map/ppermute | solution.py:557
  57.4 5.1 %collective-permute-start.11 = (f32[64,128]{1,0:T(8,128)}, f32[64,128]{1,0:T(8,128)S(1)}, u32[]{:S(2)}, u32[]{:S(2)}) collective-permute-start(f32[64,128]{1,0:T(8,128)} %copy-done.72), channel_id=1, source_target_pairs={{0,8},{4,12},{8,0},{12,4},{16,24},{20,28},{24,16},{28,20},{1,9},{5... | collective-permute-start | bytes 98312 | tf_op jit(solution)/shard_map/ppermute | solution.py:557
  90.9 4.6 %collective-permute-start.14 = (f32[192,128]{1,0:T(8,128)S(1)}, f32[192,128]{1,0:T(8,128)S(1)}, u32[]{:S(2)}, u32[]{:S(2)}) collective-permute-start(f32[192,128]{1,0:T(8,128)S(1)} %get-tuple-element.81), channel_id=1, source_target_pairs={{0,4},{4,0},{8,12},{12,8},{16,20},{20,16},{24,28},{28,24},{1,5},{5... | collective-permute-start | bytes 294920 | tf_op jit(solution)/shard_map/ppermute | solution.py:549
  92.0 24.1 %collective-permute-start.16 = (f32[256,128]{1,0:T(8,128)}, f32[256,128]{1,0:T(8,128)}, u32[]{:S(2)}, u32[]{:S(2)}) collective-permute-start(f32[256,128]{1,0:T(8,128)} %get-tuple-element.86), channel_id=1, source_target_pairs={{0,1},{1,0},{2,3},{3,2},{4,5},{5,4},{6,7},{7,6},{8,9},{9,8},{10,11... | collective-permute-start | bytes 393224 | tf_op jit(solution)/shard_map/ppermute | solution.py:549
  92.0 24.1 %collective-permute-start.17 = (f32[256,128]{1,0:T(8,128)}, f32[256,128]{1,0:T(8,128)}, u32[]{:S(2)}, u32[]{:S(2)}) collective-permute-start(f32[256,128]{1,0:T(8,128)} %get-tuple-element.87), channel_id=1, source_target_pairs={{0,0},{1,2},{2,1},{3,3},{4,4},{5,6},{6,5},{7,7},{8,8},{9,10},{10,9... | collective-permute-start | bytes 393224 | tf_op jit(solution)/shard_map/ppermute | solution.py:550
  98.0 18.0 %all-to-all-start.1 = ((f32[32,4,128]{2,1,0:T(4,128)}), f32[32,4,128]{2,1,0:T(4,128)S(1)}, u32[]{:S(2)}, u32[]{:S(2)}) async-start(f32[32,4,128]{2,1,0:T(4,128)} %bitcast.7), calls=%async_computation.1 | async-start | bytes 131072 | tf_op jit(solution)/shard_map/all_to_all | solution.py:643
  102.6 7.2 %collective-permute-start.15 = (f32[128,128]{1,0:T(8,128)}, f32[128,128]{1,0:T(8,128)S(1)}, u32[]{:S(2)}, u32[]{:S(2)}) collective-permute-start(f32[128,128]{1,0:T(8,128)} %copy-done.70), channel_id=1, source_target_pairs={{0,0},{4,8},{8,4},{12,16},{16,12},{20,24},{24,20},{28,28},{1,1},{5... | collective-permute-start | bytes 196616 | tf_op jit(solution)/shard_map/ppermute | solution.py:550
  104.1 8.8 %collective-permute-start.20 = (f32[64,128]{1,0:T(8,128)}, f32[64,128]{1,0:T(8,128)S(1)}, u32[]{:S(2)}, u32[]{:S(2)}) collective-permute-start(f32[64,128]{1,0:T(8,128)} %copy-done.73), channel_id=1, source_target_pairs={{0,24},{4,28},{8,16},{12,20},{16,8},{20,12},{24,0},{28,4},{1,25},{... | collective-permute-start | bytes 98312 | tf_op jit(solution)/shard_map/ppermute | solution.py:557
  109.8 5.0 %collective-permute-start.19 = (f32[64,128]{1,0:T(8,128)}, f32[64,128]{1,0:T(8,128)S(1)}, u32[]{:S(2)}, u32[]{:S(2)}) collective-permute-start(f32[64,128]{1,0:T(8,128)} %copy-done.73), channel_id=1, source_target_pairs={{0,16},{4,20},{8,24},{12,28},{16,0},{20,4},{24,8},{28,12},{1,17},{... | collective-permute-start | bytes 98312 | tf_op jit(solution)/shard_map/ppermute | solution.py:557
  109.8 5.6 %collective-permute-start.18 = (f32[64,128]{1,0:T(8,128)}, f32[64,128]{1,0:T(8,128)S(1)}, u32[]{:S(2)}, u32[]{:S(2)}) collective-permute-start(f32[64,128]{1,0:T(8,128)} %copy-done.73), channel_id=1, source_target_pairs={{0,8},{4,12},{8,0},{12,4},{16,24},{20,28},{24,16},{28,20},{1,9},{5... | collective-permute-start | bytes 98312 | tf_op jit(solution)/shard_map/ppermute | solution.py:557
  (73 other events, 174.5 us)

commit v6 on v5

--- a/solution.py
+++ b/solution.py
@@ -192,24 +192,26 @@
     pair[ny : 2 * ny, :] = mine_s + other_s + jnp.where(even, mine_t, other_t) * float(g.nx)
 
 
-def sides_kernel(g, fields, flags, xa, xb, own, order, *refs):
-    blocks, (ya, yb, pair) = refs[:fields], refs[fields:]
-    (xeven, xfirst, xlast), (yeven, _, _) = flags_of(g, flags)
-    n = g.xp
+def sides_kernel(g, fields, flags, order, *refs):
+    blocks, (ya, yb) = refs[:fields], refs[fields:]
+    _, (even, _, _) = flags_of(g, flags)
     for f in range(fields):
         for r in range(2):
             low = blocks[f][pl.ds(r, g.nx, stride=g.ny), :].astype(F32)
             high = blocks[f][pl.ds(g.ny - 2 + r, g.nx, stride=g.ny), :].astype(F32)
-            put_pair(yeven, low, high, ya, yb, (f * 2 + r) * n + XO)
+            put_pair(even, low, high, ya, yb, (f * 2 + r) * g.nx)
+
+
+def corners_kernel(g, fields, flags, xa, xb, own, order, ca, cb, pair):
+    (even, first, last), (yeven, _, _) = flags_of(g, flags)
+    ca[...] = jnp.zeros(ca.shape, F32)
+    cb[...] = jnp.zeros(cb.shape, F32)
     for f in range(fields):
-        for px in range(2):
+        for side, px in ((0, 1), (1, 0)):
             at = (f * 2 + px) * g.ny
-            sides = pick_sides(xeven, xfirst, xlast, xa[at : at + g.ny, :], xb[at : at + g.ny, :])
-            for plane, value in zip((px, XO + g.nx + px), sides):
-                for r in range(2):
-                    spot = (f * 2 + r) * n + plane
-                    put_pair(yeven, value[r : r + 1], value[g.ny - 2 + r : g.ny - 1 + r], ya, yb, spot)
-    join_pair(g, xeven, own, xa, fields * 2 * g.ny, pair)
+            value = pick_sides(even, first, last, xa[at : at + g.ny, :], xb[at : at + g.ny, :])[side]
+            put_pair(yeven, value[0:1], value[g.ny - 1 : g.ny], ca, cb, 2 * f + side)
+    join_pair(g, even, own, xa, fields * 2 * g.ny, pair)
 
 
 def halo_slots(g, n, off):
@@ -448,18 +450,31 @@
                 sums[8 + 2 * k + f : 9 + 2 * k + f, :] = block[cell : cell + 1, :]
 
 
-def opening_step(g, zones, flags, zlow, zhigh, xa, xb, ya, yb, own, rho, sig, p, q, t, table, ztable, *refs):
+def opening_step(g, zones, flags, zlow, zhigh, xa, xb, ya, yb, ca, cb, own, rho, sig, p, q, t, table, ztable, *refs):
     others, rest = refs[: g.pairs - 1], refs[g.pairs - 1 :]
     rho_e, sig_e, trs, xlow, xhigh, ylow, yhigh = rest[:7]
     ny = g.ny
+    _, (yeven, yfirst, ylast) = flags_of(g, flags)
     for f, ext in ((0, rho_e), (1, sig_e)):
-        for axis, side, at, spot, value in halo_values(g, flags, f, xa, xb, ya, yb, g.xp, 0):
+        for axis, side, at, spot, value in halo_values(g, flags, f, xa, xb, ya, yb, g.nx, XO):
             ext[spot, :] = value
-    for axis, side, at, spot, value in halo_values(g, flags, 2, xa, xb, ya, yb, g.xp, 0):
+    for axis, side, at, spot, value in halo_values(g, flags, 2, xa, xb, ya, yb, g.nx, XO):
         low, high = bounds_of(zones, value, zlow, zhigh)
         lows, highs = ((xlow, xhigh), (ylow, yhigh))[axis]
+        if axis == 1:
+            at = at // g.nx * g.xp + XO
         lows[side, pl.ds(at, value.shape[0]), :] = low
         highs[side, pl.ds(at, value.shape[0]), :] = high
+    cells = pick_sides(yeven, yfirst, ylast, ca[...], cb[...])
+    limits = [bounds_of(zones, values, zlow, zhigh) for values in cells]
+    for side, row in ((0, YO - 1), (1, YO + ny)):
+        for k, plane in enumerate((XO - 1, XO + g.nx)):
+            at = plane * g.pl + row
+            rho_e[at : at + 1, :] = cells[side][k : k + 1]
+            sig_e[at : at + 1, :] = cells[side][2 + k : 3 + k]
+            at = (1 - side) * g.xp + plane
+            ylow[side, at : at + 1, :] = limits[side][0][4 + k : 5 + k]
+            yhigh[side, at : at + 1, :] = limits[side][1][4 + k : 5 + k]
     pos = 6 * ny
     trs[0] = own[...]
     trs[1] = xa[pos : pos + 2 * ny, :]
@@ -511,31 +526,21 @@
     step_core(g, flags, update, rho_e, sig_e, trs, p, q, t, table, ztable, outs, scratch)
 
 
-def closing_kernel(g, sums0, sums1, sums2, grho, gsig, rho_e, sig_e, low, high, rho_o, sig_o, obj, rho_v, sig_v, sems):
+def closing_kernel(g, sums0, sums1, sums2, grho, gsig, rho_e, sig_e, low, high, rho_o, sig_o, obj):
     ar, asig = alphas(g, sums2)
-    step = 8
-    copies = []
-    for c in range(g.nx // step):
-
-        def body(k, carry):
-            x = c * step + k
-            at = pl.ds(g.own(x), g.ny)
-            here = pl.ds(pl.multiple_of(x * g.ny, 8), g.ny)
-            rho_v[x] = jnp.minimum(jnp.maximum(rho_e[at, :] - ar * grho[here, :], low[x]), high[x])
-            sig_v[x] = sig_e[at, :] - asig * gsig[here, :]
-            return carry
-
-        lax.fori_loop(0, step, body, 0, unroll=True)
-        here = pl.ds(c * step, step)
-        for k, (v, o) in enumerate(((rho_v, rho_o), (sig_v, sig_o))):
-            copies.append(pltpu.make_async_copy(v.at[here], o.at[here], sems.at[2 * c + k]))
-            copies[-1].start()
+
+    def body(x, carry):
+        at = pl.ds(g.own(x), g.ny)
+        here = pl.ds(pl.multiple_of(x * g.ny, 8), g.ny)
+        rho_o[x] = jnp.minimum(jnp.maximum(rho_e[at, :] - ar * grho[here, :], low[x]), high[x])
+        sig_o[x] = sig_e[at, :] - asig * gsig[here, :]
+        return carry
+
+    lax.fori_loop(0, g.nx, body, 0, unroll=8)
     for k, sums in enumerate((sums0, sums1, sums2)):
         row = sum_row(g, sums)
         lane = lax.broadcasted_iota(jnp.int32, row.shape, 1)
         obj[k] = jnp.sum(jnp.where(lane == 2, row, 0.0)) * (0.5 / g.cells)
-    for copy in copies:
-        copy.wait()
 
 
 def pairs_of(size):
@@ -590,7 +595,7 @@
     flat = ((nx * ny, nz), F32)
     xa_shape = lambda f: (((f + 1) * 2 * ny, nz), F32)
     xb_shape = lambda f: ((f * 2 * ny, nz), F32)
-    ymsg = lambda f: ((f * 2 * g.xp, nz), F32)
+    ymsg = lambda f: ((f * 2 * nx, nz), F32)
     xbound = ((2, 2 * ny, nz), F32)
     ybound = ((2, 2 * g.xp, nz), F32)
     win = pltpu.VMEM((g.win, nz), F32)
@@ -613,20 +618,24 @@
         [block] * 2 + [((2 * nz, 2 * nz), BF16), ((2 * nz, nz), BF16)], [VMEM], (pressure_obs,),
     )
     as_rows = lambda v: v.reshape(nx * ny, nz)
-    ya, yb, pair = call(
-        functools.partial(sides_kernel, g, 3), [ymsg(3)] * 2 + [own_shape],
-        [SMEM] + [VMEM] * 7, (flags, xa, xb, own, low, as_rows(density), as_rows(slowness), as_rows(zone_map)),
+    ya, yb = call(
+        functools.partial(sides_kernel, g, 3), [ymsg(3)] * 2,
+        [SMEM] + [VMEM] * 4, (flags, own, as_rows(density), as_rows(slowness), as_rows(zone_map)),
     )
     ya, yb = exchange("gy", ya, yb)
+    ca, cb, pair = call(
+        functools.partial(corners_kernel, g, 3), [((8, nz), F32)] * 2 + [own_shape],
+        [SMEM] + [VMEM] * 4, (flags, xa, xb, own, low),
+    )
+    ca, cb = exchange("gy", ca, cb)
     others = pair_totals(pair, px)
-    yown = ((4 * nx, nz), F32)
-    ends = [flat, flat, ((16, nz), F32), own_shape, xa_shape(2), xb_shape(2), yown, yown]
+    ends = [flat, flat, ((16, nz), F32), own_shape, xa_shape(2), xb_shape(2), ymsg(2), ymsg(2)]
     chunks = ((px * py * CHUNK, nz), F32)
     outs = call(
         functools.partial(opening_step, g, zones),
         [ext, ext, trs_shape, xbound, xbound, ybound, ybound] + ends,
-        [SMEM] * 3 + [VMEM] * (12 + len(others)),
-        (flags, zone_low, zone_high, xa, xb, ya, yb, own, density, slowness, p, q, t, table, ztable, *others),
+        [SMEM] * 3 + [VMEM] * (14 + len(others)),
+        (flags, zone_low, zone_high, xa, xb, ya, yb, ca, cb, own, density, slowness, p, q, t, table, ztable, *others),
         core_scratch, 24,
     )
     rho_e, sig_e, trs, xlow, xhigh, ylow, yhigh, grho, gsig, head, own, xa, xb, ya, yb = outs
@@ -655,8 +664,7 @@
     history.append(lax.all_to_all(head, both, 0, 0, tiled=True))
     rho, sigma, obj = call(
         functools.partial(closing_kernel, g), [block, block, ((ITERS,), F32)],
-        [VMEM] * 9, (*history, grho, gsig, rho_e, sig_e, low, high),
-        [pltpu.VMEM((nx, ny, nz), F32)] * 2 + [pltpu.SemaphoreType.DMA((nx // 4,))], outs=[HBM, HBM, SMEM],
+        [VMEM] * 9, (*history, grho, gsig, rho_e, sig_e, low, high), outs=[VMEM, VMEM, SMEM],
     )
     return rho, sigma, obj
 

time: 153 us -> 156 us (1.020)
  starting transfers between devices: 46.8 us -> 50.5 us
  waiting for transfers between devices: 12.4 us -> 10.7 us
    ppermute x6 -> x7, starting transfers between devices: 5.58 us -> 8.28 us  [exchange(): a = lax.ppermute(a, axis, pa)]
    ppermute x6 -> x7, waiting for transfers between devices: 4.37 us -> 2.91 us  [exchange(): a = lax.ppermute(a, axis, pa)]
    ppermute x6 -> x7, starting transfers between devices: 8.61 us -> 9.59 us  [exchange(): b = lax.ppermute(b, axis, pb)]
    pallas_call x10 -> x11, Pallas kernels: 26.9 us -> 27.3 us  [call(): pl.pallas_call(body, out_shape=[jax.ShapeDtypeStruct(s, d) for s, d in sh...]
  transfers between devices with their start and end apart: 23 -> 25, of which waited for: 9 -> 9; matrix products, arithmetic and copies ran while one was open for 0% -> 0% of each run, Pallas kernels for 2% -> 3%
where the time goes in v6:
time: 156 us; the launch traced here: 154 us
  local copies, waits for them, and re-layouts  53.6 us (34%)
  starting transfers between devices  50.5 us (32%)
  Pallas kernels  27.3 us (18%)
  blocking collectives  11 us (7%)
  waiting for transfers between devices  10.7 us (7%)
    unnamed x148, local copies, waits for them, and re-layouts  53.6 us
    pallas_call x11, Pallas kernels, call(): pl.pallas_call(body, out_shape=[jax.ShapeDtypeStruct(s, d) for s, d in sh...  27.3 us
    ppermute x9, starting transfers between devices, pair_totals(): out.append(lax.ppermute(pair, 'gx', [(i, i ^ 2 * m) for i in range(size)]))  23.3 us
    all_to_all x1, blocking collectives, local(): history.append(lax.all_to_all(head, both, 0, 0, tiled=True))  11 us
    ppermute x7, starting transfers between devices, exchange(): b = lax.ppermute(b, axis, pb)  9.59 us
    all_to_all x2, starting transfers between devices, local(): sums = lax.all_to_all(sums, both, 0, 0, tiled=True)  9.29 us
    ppermute x7, starting transfers between devices, exchange(): a = lax.ppermute(a, axis, pa)  8.28 us
    ppermute x9, waiting for transfers between devices, pair_totals(): out.append(lax.ppermute(pair, 'gx', [(i, i ^ 2 * m) for i in range(size)]))  7.78 us
  transfers between devices with their start and end apart: 25, of which 9 were waited for; matrix products, arithmetic and copies ran while one was open for 0% of the time, Pallas kernels for 3%

profile of v6, /device:TPU:0, one launch (start us, length us, event | category | flops | bytes accessed | tf_op | source)
XLA Modules:
  0.0 154.3 jit_solution(9581448089974004199)
XLA Ops:
  0.7 2.6 %shard_map.94 = (f32[64,128]{1,0:T(8,128)S(1)}, f32[256,128]{1,0:T(8,128)S(1)}, f32[192,128]{1,0:T(8,128)S(1)}) custom-call(s32[2]{0:T(128)S(1)} %pad_add_fusion.flags, f32[64,32,128]{2,1,0:T(8,128)} %rho.3, f32[64,32,128]{2,1,0:T(8,128)} %sig.1, s32[64,32,128]{2,1,0:T(8,128)} %zone.3, f32[64,32,128]{2,1,0:T(8,128)} %t.3), custom_call_target="tpu_custom_call" | custom-call | tf_op jit(solution)/shard_map/pallas_call | solution.py:572
  5.4 2.6 %collective-permute-start = (f32[256,128]{1,0:T(8,128)S(1)}, f32[256,128]{1,0:T(8,128)S(1)}, u32[]{:S(2)}, u32[]{:S(2)}) collective-permute-start(f32[256,128]{1,0:T(8,128)S(1)} %get-tuple-element.53), channel_id=1, source_target_pairs={{0,4},{4,0},{8,12},{12,8},{16,20},{20,16},{24,28},{28,24},{1,5},{5... | collective-permute-start | bytes 393224 | tf_op jit(solution)/shard_map/ppermute | solution.py:554
  8.8 1.5 shard_map.96
  11.5 2.3 %collective-permute-start.4 = (f32[8,128]{1,0:T(8,128)S(1)}, f32[8,128]{1,0:T(8,128)S(1)}, u32[]{:S(2)}, u32[]{:S(2)}) collective-permute-start(f32[8,128]{1,0:T(8,128)S(1)} %get-tuple-element.59), channel_id=1, source_target_pairs={{0,1},{1,0},{2,3},{3,2},{4,5},{5,4},{6,7},{7,6},{8,9},{9,8},{10,11... | collective-permute-start | bytes 12296 | tf_op jit(solution)/shard_map/ppermute | solution.py:554
  14.5 7.4 %collective-permute-start.8 = (f32[64,128]{1,0:T(8,128)S(1)}, f32[64,128]{1,0:T(8,128)S(1)}, u32[]{:S(2)}, u32[]{:S(2)}) collective-permute-start(f32[64,128]{1,0:T(8,128)S(1)} %get-tuple-element.66), channel_id=1, source_target_pairs={{0,24},{4,28},{8,16},{12,20},{16,8},{20,12},{24,0},{28,4},{1,25},{... | collective-permute-start | bytes 98312 | tf_op jit(solution)/shard_map/ppermute | solution.py:562
  23.8 3.0 %collective-permute-done.7.refs_1_ = f32[64,128]{1,0:T(8,128)S(1)} collective-permute-done((f32[64,128]{1,0:T(8,128)S(1)}, f32[64,128]{1,0:T(8,128)S(1)}, u32[]{:S(2)}, u32[]{:S(2)}) %collective-permute-start.7) | collective-permute-done | bytes 32800 | tf_op jit(solution)/shard_map/ppermute | solution.py:562
  26.8 5.7 %shard_map.99 = (f32[2920,128]{1,0:T(8,128)S(1)}, f32[2920,128]{1,0:T(8,128)S(1)}, f32[5,64,128]{2,1,0:T(8,128)S(1)}, f32[2,64,128]{2,1,0:T(8,128)S(1)}, f32[2,6...) custom-call(s32[2]{0:T(128)S(1)} %pad_add_fusion.flags, ...), custom_call_target="tpu_custom_call" | custom-call | tf_op jit(solution)/shard_map/pallas_call | solution.py:572
  39.9 1.8 %collective-permute-start.11 = (f32[256,128]{1,0:T(8,128)}, f32[256,128]{1,0:T(8,128)}, u32[]{:S(2)}, u32[]{:S(2)}) collective-permute-start(f32[256,128]{1,0:T(8,128)} %get-tuple-element.72), channel_id=1, source_target_pairs={{0,1},{1,0},{2,3},{3,2},{4,5},{5,4},{6,7},{7,6},{8,9},{9,8},{10,11... | collective-permute-start | bytes 393224 | tf_op jit(solution)/shard_map/ppermute | solution.py:554
  41.7 2.2 %collective-permute-start.12 = (f32[256,128]{1,0:T(8,128)}, f32[256,128]{1,0:T(8,128)}, u32[]{:S(2)}, u32[]{:S(2)}) collective-permute-start(f32[256,128]{1,0:T(8,128)} %get-tuple-element.73), channel_id=1, source_target_pairs={{0,0},{1,2},{2,1},{3,3},{4,4},{5,6},{6,5},{7,7},{8,8},{9,10},{10,9... | collective-permute-start | bytes 393224 | tf_op jit(solution)/shard_map/ppermute | solution.py:555
  47.8 4.7 %all-to-all-start = ((f32[32,4,128]{2,1,0:T(4,128)}), f32[32,4,128]{2,1,0:T(4,128)S(1)}, u32[]{:S(2)}, u32[]{:S(2)}) async-start(f32[32,4,128]{2,1,0:T(4,128)} %bitcast.21), calls=%async_computation | async-start | bytes 131072 | tf_op jit(solution)/shard_map/all_to_all | solution.py:652
  52.6 1.5 collective-permute-start.10
  54.0 5.5 %collective-permute-start.15 = (f32[64,128]{1,0:T(8,128)}, f32[64,128]{1,0:T(8,128)S(1)}, u32[]{:S(2)}, u32[]{:S(2)}) collective-permute-start(f32[64,128]{1,0:T(8,128)} %copy-done.72), channel_id=1, source_target_pairs={{0,24},{4,28},{8,16},{12,20},{16,8},{20,12},{24,0},{28,4},{1,25},{... | collective-permute-start | bytes 98312 | tf_op jit(solution)/shard_map/ppermute | solution.py:562
  60.2 2.1 %collective-permute-start.13 = (f32[64,128]{1,0:T(8,128)}, f32[64,128]{1,0:T(8,128)S(1)}, u32[]{:S(2)}, u32[]{:S(2)}) collective-permute-start(f32[64,128]{1,0:T(8,128)} %copy-done.72), channel_id=1, source_target_pairs={{0,8},{4,12},{8,0},{12,4},{16,24},{20,28},{24,16},{28,20},{1,9},{5... | collective-permute-start | bytes 98312 | tf_op jit(solution)/shard_map/ppermute | solution.py:562
  68.4 1.4 copy-done.15
  82.5 6.3 %shard_map.101 = (f32[2920,128]{1,0:T(8,128)S(1)}, f32[2920,128]{1,0:T(8,128)S(1)}, f32[5,64,128]{2,1,0:T(8,128)S(1)}, f32[2048,128]{1,0:T(8,128)S(1)}, f32[2048...) custom-call(s32[2]{0:T(128)S(1)} %copy-done.66, ...), custom_call_target="tpu_custom_call" | custom-call | tf_op jit(solution)/shard_map/pallas_call | solution.py:572
  94.8 2.2 %collective-permute-start.19 = (f32[256,128]{1,0:T(8,128)}, f32[256,128]{1,0:T(8,128)}, u32[]{:S(2)}, u32[]{:S(2)}) collective-permute-start(f32[256,128]{1,0:T(8,128)} %get-tuple-element.91), channel_id=1, source_target_pairs={{0,0},{1,2},{2,1},{3,3},{4,4},{5,6},{6,5},{7,7},{8,8},{9,10},{10,9... | collective-permute-start | bytes 393224 | tf_op jit(solution)/shard_map/ppermute | solution.py:555
  96.9 1.4 collective-permute-done.16.xa
  100.8 4.6 %all-to-all-start.1 = ((f32[32,4,128]{2,1,0:T(4,128)}), f32[32,4,128]{2,1,0:T(4,128)S(1)}, u32[]{:S(2)}, u32[]{:S(2)}) async-start(f32[32,4,128]{2,1,0:T(4,128)} %bitcast.7), calls=%async_computation.1 | async-start | bytes 131072 | tf_op jit(solution)/shard_map/all_to_all | solution.py:652
  105.4 1.7 %collective-permute-start.17 = (f32[128,128]{1,0:T(8,128)}, f32[128,128]{1,0:T(8,128)S(1)}, u32[]{:S(2)}, u32[]{:S(2)}) collective-permute-start(f32[128,128]{1,0:T(8,128)} %copy-done.71), channel_id=1, source_target_pairs={{0,0},{4,8},{8,4},{12,16},{16,12},{20,24},{24,20},{28,28},{1,1},{5... | collective-permute-start | bytes 196616 | tf_op jit(solution)/shard_map/ppermute | solution.py:555
  107.1 5.5 %collective-permute-start.22 = (f32[64,128]{1,0:T(8,128)}, f32[64,128]{1,0:T(8,128)S(1)}, u32[]{:S(2)}, u32[]{:S(2)}) collective-permute-start(f32[64,128]{1,0:T(8,128)} %copy-done.73), channel_id=1, source_target_pairs={{0,24},{4,28},{8,16},{12,20},{16,8},{20,12},{24,0},{28,4},{1,25},{... | collective-permute-start | bytes 98312 | tf_op jit(solution)/shard_map/ppermute | solution.py:562
  112.6 2.1 %collective-permute-start.20 = (f32[64,128]{1,0:T(8,128)}, f32[64,128]{1,0:T(8,128)S(1)}, u32[]{:S(2)}, u32[]{:S(2)}) collective-permute-start(f32[64,128]{1,0:T(8,128)} %copy-done.73), channel_id=1, source_target_pairs={{0,8},{4,12},{8,0},{12,4},{16,24},{20,28},{24,16},{28,20},{1,9},{5... | collective-permute-start | bytes 98312 | tf_op jit(solution)/shard_map/ppermute | solution.py:562
  135.5 5.7 %shard_map.103 = (f32[2920,128]{1,0:T(8,128)S(1)}, f32[2920,128]{1,0:T(8,128)S(1)}, f32[5,64,128]{2,1,0:T(8,128)}, f32[2048,128]{1,0:T(8,128)S(1)}, f32[2048,128]{1,0:T(8,128)S(1)}, /*index=5*/f32[32,128]{1,0:T(8,128)S(1)}) custom-call(s32[2]{0:T(128)S(1)} %copy-done.67, f32[192,128]{1,0:T(8,128)S(1)} %copy-done.33, ...), custom_call_target="tpu_custom_call" | custom-call | tf_op jit(solution)/shard_map/pallas_call | solution.py:572
  141.2 11.0 %all_to_all.33 = f32[32,1,128]{2,1,0:T(1,128)S(1)} all-to-all(f32[32,1,128]{2,1,0:T(1,128)S(1)} %bitcast.22), channel_id=1, replica_groups=mesh['gx'=8,'gy'=4] {'gx','gy'}, dimensions={0} | all-to-all | bytes 32768 | tf_op jit(solution)/shard_map/all_to_all | solution.py:664
  152.2 1.9 %shard_map.104 = (f32[64,32,128]{2,1,0:T(8,128)}, f32[64,32,128]{2,1,0:T(8,128)}, f32[3]{0:T(128)}) custom-call(f32[128,128]{1,0:T(8,128)S(1)} %bitcast.17, f32[128,128]{1,0:T(8,128)S(1)} %bitcast.19, f32[32,128]{1,0:T(8,128)S(1)} %bitcast.20, f32[2048,128]{1,0:T(8,128)S(1)} %get-tuple-element.99.grho, f32[2048,128]{1,0:T(8,128)S(1)} %get-tuple-element.100.gsig, ...), custom_call_target="tpu_custom_call" | custom-call | tf_op jit(solution)/shard_map/pallas_call | solution.py:572
  (187 shorter events, 66.5 us)
Async XLA Ops:
  4.2 22.6 %collective-permute-start.2 = (f32[384,128]{1,0:T(8,128)S(1)}, f32[384,128]{1,0:T(8,128)S(1)}, u32[]{:S(2)}, u32[]{:S(2)}) collective-permute-start(f32[384,128]{1,0:T(8,128)S(1)} %get-tuple-element.56), channel_id=1, source_target_pairs={{0,1},{1,0},{2,3},{3,2},{4,5},{5,4},{6,7},{7,6},{8,9},{9,8},{10,11... | collective-permute-start | bytes 589832 | tf_op jit(solution)/shard_map/ppermute | solution.py:554
  4.7 22.0 %collective-permute-start.3 = (f32[384,128]{1,0:T(8,128)S(1)}, f32[384,128]{1,0:T(8,128)S(1)}, u32[]{:S(2)}, u32[]{:S(2)}) collective-permute-start(f32[384,128]{1,0:T(8,128)S(1)} %get-tuple-element.57), channel_id=1, source_target_pairs={{0,0},{1,2},{2,1},{3,3},{4,4},{5,6},{6,5},{7,7},{8,8},{9,10},{10,9... | collective-permute-start | bytes 589832 | tf_op jit(solution)/shard_map/ppermute | solution.py:555
  5.4 5.5 %collective-permute-start = (f32[256,128]{1,0:T(8,128)S(1)}, f32[256,128]{1,0:T(8,128)S(1)}, u32[]{:S(2)}, u32[]{:S(2)}) collective-permute-start(f32[256,128]{1,0:T(8,128)S(1)} %get-tuple-element.53), channel_id=1, source_target_pairs={{0,4},{4,0},{8,12},{12,8},{16,20},{20,16},{24,28},{28,24},{1,5},{5... | collective-permute-start | bytes 393224 | tf_op jit(solution)/shard_map/ppermute | solution.py:554
  11.5 10.4 %collective-permute-start.4 = (f32[8,128]{1,0:T(8,128)S(1)}, f32[8,128]{1,0:T(8,128)S(1)}, u32[]{:S(2)}, u32[]{:S(2)}) collective-permute-start(f32[8,128]{1,0:T(8,128)S(1)} %get-tuple-element.59), channel_id=1, source_target_pairs={{0,1},{1,0},{2,3},{3,2},{4,5},{5,4},{6,7},{7,6},{8,9},{9,8},{10,11... | collective-permute-start | bytes 12296 | tf_op jit(solution)/shard_map/ppermute | solution.py:554
  13.8 8.1 %collective-permute-start.5 = (f32[8,128]{1,0:T(8,128)S(1)}, f32[8,128]{1,0:T(8,128)S(1)}, u32[]{:S(2)}, u32[]{:S(2)}) collective-permute-start(f32[8,128]{1,0:T(8,128)S(1)} %get-tuple-element.60), channel_id=1, source_target_pairs={{0,0},{1,2},{2,1},{3,3},{4,4},{5,6},{6,5},{7,7},{8,8},{9,10},{10,9... | collective-permute-start | bytes 12296 | tf_op jit(solution)/shard_map/ppermute | solution.py:555
  14.5 9.3 %collective-permute-start.8 = (f32[64,128]{1,0:T(8,128)S(1)}, f32[64,128]{1,0:T(8,128)S(1)}, u32[]{:S(2)}, u32[]{:S(2)}) collective-permute-start(f32[64,128]{1,0:T(8,128)S(1)} %get-tuple-element.66), channel_id=1, source_target_pairs={{0,24},{4,28},{8,16},{12,20},{16,8},{20,12},{24,0},{28,4},{1,25},{... | collective-permute-start | bytes 98312 | tf_op jit(solution)/shard_map/ppermute | solution.py:562
  21.9 4.8 %collective-permute-start.7 = (f32[64,128]{1,0:T(8,128)S(1)}, f32[64,128]{1,0:T(8,128)S(1)}, u32[]{:S(2)}, u32[]{:S(2)}) collective-permute-start(f32[64,128]{1,0:T(8,128)S(1)} %get-tuple-element.66), channel_id=1, source_target_pairs={{0,16},{4,20},{8,24},{12,28},{16,0},{20,4},{24,8},{28,12},{1,17},{... | collective-permute-start | bytes 98312 | tf_op jit(solution)/shard_map/ppermute | solution.py:562
  21.9 4.8 %collective-permute-start.6 = (f32[64,128]{1,0:T(8,128)S(1)}, f32[64,128]{1,0:T(8,128)S(1)}, u32[]{:S(2)}, u32[]{:S(2)}) collective-permute-start(f32[64,128]{1,0:T(8,128)S(1)} %get-tuple-element.66), channel_id=1, source_target_pairs={{0,8},{4,12},{8,0},{12,4},{16,24},{20,28},{24,16},{28,20},{1,9},{5... | collective-permute-start | bytes 98312 | tf_op jit(solution)/shard_map/ppermute | solution.py:562
  39.9 4.8 %collective-permute-start.9 = (f32[192,128]{1,0:T(8,128)S(1)}, f32[192,128]{1,0:T(8,128)S(1)}, u32[]{:S(2)}, u32[]{:S(2)}) collective-permute-start(f32[192,128]{1,0:T(8,128)S(1)} %get-tuple-element.67), channel_id=1, source_target_pairs={{0,4},{4,0},{8,12},{12,8},{16,20},{20,16},{24,28},{28,24},{1,5},{5... | collective-permute-start | bytes 294920 | tf_op jit(solution)/shard_map/ppermute | solution.py:554
  39.9 26.0 %collective-permute-start.11 = (f32[256,128]{1,0:T(8,128)}, f32[256,128]{1,0:T(8,128)}, u32[]{:S(2)}, u32[]{:S(2)}) collective-permute-start(f32[256,128]{1,0:T(8,128)} %get-tuple-element.72), channel_id=1, source_target_pairs={{0,1},{1,0},{2,3},{3,2},{4,5},{5,4},{6,7},{7,6},{8,9},{9,8},{10,11... | collective-permute-start | bytes 393224 | tf_op jit(solution)/shard_map/ppermute | solution.py:554
  41.7 24.2 %collective-permute-start.12 = (f32[256,128]{1,0:T(8,128)}, f32[256,128]{1,0:T(8,128)}, u32[]{:S(2)}, u32[]{:S(2)}) collective-permute-start(f32[256,128]{1,0:T(8,128)} %get-tuple-element.73), channel_id=1, source_target_pairs={{0,0},{1,2},{2,1},{3,3},{4,4},{5,6},{6,5},{7,7},{8,8},{9,10},{10,9... | collective-permute-start | bytes 393224 | tf_op jit(solution)/shard_map/ppermute | solution.py:555
  47.8 18.1 %all-to-all-start = ((f32[32,4,128]{2,1,0:T(4,128)}), f32[32,4,128]{2,1,0:T(4,128)S(1)}, u32[]{:S(2)}, u32[]{:S(2)}) async-start(f32[32,4,128]{2,1,0:T(4,128)} %bitcast.21), calls=%async_computation | async-start | bytes 131072 | tf_op jit(solution)/shard_map/all_to_all | solution.py:652
  52.6 7.0 %collective-permute-start.10 = (f32[128,128]{1,0:T(8,128)}, f32[128,128]{1,0:T(8,128)S(1)}, u32[]{:S(2)}, u32[]{:S(2)}) collective-permute-start(f32[128,128]{1,0:T(8,128)} %copy-done.70), channel_id=1, source_target_pairs={{0,0},{4,8},{8,4},{12,16},{16,12},{20,24},{24,20},{28,28},{1,1},{5... | collective-permute-start | bytes 196616 | tf_op jit(solution)/shard_map/ppermute | solution.py:555
  54.0 8.9 %collective-permute-start.15 = (f32[64,128]{1,0:T(8,128)}, f32[64,128]{1,0:T(8,128)S(1)}, u32[]{:S(2)}, u32[]{:S(2)}) collective-permute-start(f32[64,128]{1,0:T(8,128)} %copy-done.72), channel_id=1, source_target_pairs={{0,24},{4,28},{8,16},{12,20},{16,8},{20,12},{24,0},{28,4},{1,25},{... | collective-permute-start | bytes 98312 | tf_op jit(solution)/shard_map/ppermute | solution.py:562
  59.6 5.1 %collective-permute-start.14 = (f32[64,128]{1,0:T(8,128)}, f32[64,128]{1,0:T(8,128)S(1)}, u32[]{:S(2)}, u32[]{:S(2)}) collective-permute-start(f32[64,128]{1,0:T(8,128)} %copy-done.72), channel_id=1, source_target_pairs={{0,16},{4,20},{8,24},{12,28},{16,0},{20,4},{24,8},{28,12},{1,17},{... | collective-permute-start | bytes 98312 | tf_op jit(solution)/shard_map/ppermute | solution.py:562
  60.2 5.1 %collective-permute-start.13 = (f32[64,128]{1,0:T(8,128)}, f32[64,128]{1,0:T(8,128)S(1)}, u32[]{:S(2)}, u32[]{:S(2)}) collective-permute-start(f32[64,128]{1,0:T(8,128)} %copy-done.72), channel_id=1, source_target_pairs={{0,8},{4,12},{8,0},{12,4},{16,24},{20,28},{24,16},{28,20},{1,9},{5... | collective-permute-start | bytes 98312 | tf_op jit(solution)/shard_map/ppermute | solution.py:562
  93.7 4.6 %collective-permute-start.16 = (f32[192,128]{1,0:T(8,128)S(1)}, f32[192,128]{1,0:T(8,128)S(1)}, u32[]{:S(2)}, u32[]{:S(2)}) collective-permute-start(f32[192,128]{1,0:T(8,128)S(1)} %get-tuple-element.85), channel_id=1, source_target_pairs={{0,4},{4,0},{8,12},{12,8},{16,20},{20,16},{24,28},{28,24},{1,5},{5... | collective-permute-start | bytes 294920 | tf_op jit(solution)/shard_map/ppermute | solution.py:554
  94.7 24.1 %collective-permute-start.18 = (f32[256,128]{1,0:T(8,128)}, f32[256,128]{1,0:T(8,128)}, u32[]{:S(2)}, u32[]{:S(2)}) collective-permute-start(f32[256,128]{1,0:T(8,128)} %get-tuple-element.90), channel_id=1, source_target_pairs={{0,1},{1,0},{2,3},{3,2},{4,5},{5,4},{6,7},{7,6},{8,9},{9,8},{10,11... | collective-permute-start | bytes 393224 | tf_op jit(solution)/shard_map/ppermute | solution.py:554
  94.8 24.1 %collective-permute-start.19 = (f32[256,128]{1,0:T(8,128)}, f32[256,128]{1,0:T(8,128)}, u32[]{:S(2)}, u32[]{:S(2)}) collective-permute-start(f32[256,128]{1,0:T(8,128)} %get-tuple-element.91), channel_id=1, source_target_pairs={{0,0},{1,2},{2,1},{3,3},{4,4},{5,6},{6,5},{7,7},{8,8},{9,10},{10,9... | collective-permute-start | bytes 393224 | tf_op jit(solution)/shard_map/ppermute | solution.py:555
  100.8 18.0 %all-to-all-start.1 = ((f32[32,4,128]{2,1,0:T(4,128)}), f32[32,4,128]{2,1,0:T(4,128)S(1)}, u32[]{:S(2)}, u32[]{:S(2)}) async-start(f32[32,4,128]{2,1,0:T(4,128)} %bitcast.7), calls=%async_computation.1 | async-start | bytes 131072 | tf_op jit(solution)/shard_map/all_to_all | solution.py:652
  105.4 7.2 %collective-permute-start.17 = (f32[128,128]{1,0:T(8,128)}, f32[128,128]{1,0:T(8,128)S(1)}, u32[]{:S(2)}, u32[]{:S(2)}) collective-permute-start(f32[128,128]{1,0:T(8,128)} %copy-done.71), channel_id=1, source_target_pairs={{0,0},{4,8},{8,4},{12,16},{16,12},{20,24},{24,20},{28,28},{1,1},{5... | collective-permute-start | bytes 196616 | tf_op jit(solution)/shard_map/ppermute | solution.py:555
  107.1 8.8 %collective-permute-start.22 = (f32[64,128]{1,0:T(8,128)}, f32[64,128]{1,0:T(8,128)S(1)}, u32[]{:S(2)}, u32[]{:S(2)}) collective-permute-start(f32[64,128]{1,0:T(8,128)} %copy-done.73), channel_id=1, source_target_pairs={{0,24},{4,28},{8,16},{12,20},{16,8},{20,12},{24,0},{28,4},{1,25},{... | collective-permute-start | bytes 98312 | tf_op jit(solution)/shard_map/ppermute | solution.py:562
  112.6 5.0 %collective-permute-start.21 = (f32[64,128]{1,0:T(8,128)}, f32[64,128]{1,0:T(8,128)S(1)}, u32[]{:S(2)}, u32[]{:S(2)}) collective-permute-start(f32[64,128]{1,0:T(8,128)} %copy-done.73), channel_id=1, source_target_pairs={{0,16},{4,20},{8,24},{12,28},{16,0},{20,4},{24,8},{28,12},{1,17},{... | collective-permute-start | bytes 98312 | tf_op jit(solution)/shard_map/ppermute | solution.py:562
  112.6 5.6 %collective-permute-start.20 = (f32[64,128]{1,0:T(8,128)}, f32[64,128]{1,0:T(8,128)S(1)}, u32[]{:S(2)}, u32[]{:S(2)}) collective-permute-start(f32[64,128]{1,0:T(8,128)} %copy-done.73), channel_id=1, source_target_pairs={{0,8},{4,12},{8,0},{12,4},{16,24},{20,28},{24,16},{28,20},{1,9},{5... | collective-permute-start | bytes 98312 | tf_op jit(solution)/shard_map/ppermute | solution.py:562
  (75 other events, 219.3 us)

commit v7 on v6

--- a/solution.py
+++ b/solution.py
@@ -29,7 +29,8 @@
 class Geo:
     def __init__(self, nx, ny, nz, px, py):
         self.nx, self.ny, self.nz, self.px, self.py = nx, ny, nz, px, py
-        self.pl = ny + YO
+        self.pl = ny + YO + 1
+        self.gp = ny + 1
         self.ext = (nx + 9) * self.pl
         self.xp = nx + 8
         self.cells = float(nx * px * ny * py * nz)
@@ -202,7 +203,7 @@
             put_pair(even, low, high, ya, yb, (f * 2 + r) * g.nx)
 
 
-def corners_kernel(g, fields, flags, xa, xb, own, order, ca, cb, pair):
+def corners_kernel(g, fields, flags, xa, xb, own, ca, cb, pair):
     (even, first, last), (yeven, _, _) = flags_of(g, flags)
     ca[...] = jnp.zeros(ca.shape, F32)
     cb[...] = jnp.zeros(cb.shape, F32)
@@ -386,8 +387,9 @@
         miss = yu[here, :] - p[x]
         gr = ym[here, :] - q[x] + term(vxr, vyr, vzr)
         gs = back * (SCALE * g.xs * g.xs) + term(vxs, vys, vzs)
-        grho[flat_at, :] = gr
-        gsig[flat_at, :] = gs
+        out = pl.ds(x * g.gp, ny)
+        grho[out, :] = gr
+        gsig[out, :] = gs
         sum_t = sum_t + gs
         return back, sum_t, sum_r + sum_t, nr + fold8(gr * gr), ns + fold8(gs * gs), acc + fold8(miss * miss)
 
@@ -435,18 +437,18 @@
         pos = 0
         for block in (grho, gsig):
             for r in range(2):
-                put_pair(even, block[pl.ds(r * ny, ny), :], block[pl.ds((nx - 2 + r) * ny, ny), :], xa, xb, pos)
+                put_pair(even, block[pl.ds(r * g.gp, ny), :], block[pl.ds((nx - 2 + r) * g.gp, ny), :], xa, xb, pos)
                 pos += ny
         for ref, at in ((own, 0), (xa, pos)):
             ref[at : at + ny, :] = sum_t
             ref[at + ny : at + 2 * ny, :] = rest
         for f, block in enumerate((grho, gsig)):
             for r in range(2):
-                rows_low = block[pl.ds(r, nx, stride=ny), :]
-                rows_high = block[pl.ds(ny - 2 + r, nx, stride=ny), :]
+                rows_low = block[pl.ds(r, nx, stride=g.gp), :]
+                rows_high = block[pl.ds(ny - 2 + r, nx, stride=g.gp), :]
                 put_pair(yeven, rows_low, rows_high, ya, yb, (f * 2 + r) * nx)
             for k, (dx, dy) in enumerate(DIAGONALS):
-                cell = (0 if dx < 0 else nx - 1) * ny + (0 if dy < 0 else ny - 1)
+                cell = (0 if dx < 0 else nx - 1) * g.gp + (0 if dy < 0 else ny - 1)
                 sums[8 + 2 * k + f : 9 + 2 * k + f, :] = block[cell : cell + 1, :]
 
 
@@ -515,7 +517,7 @@
         trs[2 + m] = trs_i[2 + m] - asig * other[...]
 
     def update(x, at):
-        here = pl.ds(pl.multiple_of(x * ny, 8), ny)
+        here = pl.ds(x * g.gp, ny)
         moved = rho_i[at, :] - ar * grho_i[here, :]
         return clip(moved, low[x], high[x]), sig_i[at, :] - asig * gsig_i[here, :]
 
@@ -531,7 +533,7 @@
 
     def body(x, carry):
         at = pl.ds(g.own(x), g.ny)
-        here = pl.ds(pl.multiple_of(x * g.ny, 8), g.ny)
+        here = pl.ds(x * g.gp, g.ny)
         rho_o[x] = jnp.minimum(jnp.maximum(rho_e[at, :] - ar * grho[here, :], low[x]), high[x])
         sig_o[x] = sig_e[at, :] - asig * gsig[here, :]
         return carry
@@ -592,7 +594,7 @@
     trs_shape = ((g.pairs + 1, 2 * ny, nz), F32)
     sums_shape = ((px * py, nz), F32)
     block = ((nx, ny, nz), F32)
-    flat = ((nx * ny, nz), F32)
+    flat = ((nx * g.gp, nz), F32)
     xa_shape = lambda f: (((f + 1) * 2 * ny, nz), F32)
     xb_shape = lambda f: ((f * 2 * ny, nz), F32)
     ymsg = lambda f: ((f * 2 * nx, nz), F32)
@@ -625,7 +627,7 @@
     ya, yb = exchange("gy", ya, yb)
     ca, cb, pair = call(
         functools.partial(corners_kernel, g, 3), [((8, nz), F32)] * 2 + [own_shape],
-        [SMEM] + [VMEM] * 4, (flags, xa, xb, own, low),
+        [SMEM] + [VMEM] * 3, (flags, xa, xb, own),
     )
     ca, cb = exchange("gy", ca, cb)
     others = pair_totals(pair, px)

time: 156 us -> 156 us (level)
    ppermute x7, waiting for transfers between devices: 2.91 us -> 4.5 us  [exchange(): a = lax.ppermute(a, axis, pa)]
  transfers between devices with their start and end apart: 25 -> 25, of which waited for: 9 -> 8; matrix products, arithmetic and copies ran while one was open for 0% -> 0% of each run, Pallas kernels for 3% -> 3%
where the time goes in v7:
time: 156 us; the launch traced here: 154 us
  local copies, waits for them, and re-layouts  53.9 us (35%)
  starting transfers between devices  50.1 us (32%)
  Pallas kernels  26.9 us (17%)
  waiting for transfers between devices  10.9 us (7%)
  blocking collectives  10.7 us (7%)
    unnamed x148, local copies, waits for them, and re-layouts  53.9 us
    pallas_call x11, Pallas kernels, call(): pl.pallas_call(body, out_shape=[jax.ShapeDtypeStruct(s, d) for s, d in sh...  26.9 us
    ppermute x9, starting transfers between devices, pair_totals(): out.append(lax.ppermute(pair, 'gx', [(i, i ^ 2 * m) for i in range(size)]))  22.8 us
    all_to_all x1, blocking collectives, local(): history.append(lax.all_to_all(head, both, 0, 0, tiled=True))  10.7 us
    all_to_all x2, starting transfers between devices, local(): sums = lax.all_to_all(sums, both, 0, 0, tiled=True)  9.35 us
    ppermute x7, starting transfers between devices, exchange(): b = lax.ppermute(b, axis, pb)  9.27 us
    ppermute x7, starting transfers between devices, exchange(): a = lax.ppermute(a, axis, pa)  8.69 us
    ppermute x9, waiting for transfers between devices, pair_totals(): out.append(lax.ppermute(pair, 'gx', [(i, i ^ 2 * m) for i in range(size)]))  6.41 us
  transfers between devices with their start and end apart: 25, of which 8 were waited for; matrix products, arithmetic and copies ran while one was open for 0% of the time, Pallas kernels for 3%

profile of v7, /device:TPU:0, one launch (start us, length us, event | category | flops | bytes accessed | tf_op | source)
XLA Modules:
  0.0 153.8 jit_solution(8710635491190213195)
XLA Ops:
  0.7 2.6 %shard_map.94 = (f32[64,128]{1,0:T(8,128)S(1)}, f32[256,128]{1,0:T(8,128)S(1)}, f32[192,128]{1,0:T(8,128)S(1)}) custom-call(s32[2]{0:T(128)S(1)} %pad_add_fusion.flags, f32[64,32,128]{2,1,0:T(8,128)} %rho.3, f32[64,32,128]{2,1,0:T(8,128)} %sig.1, s32[64,32,128]{2,1,0:T(8,128)} %zone.3, f32[64,32,128]{2,1,0:T(8,128)} %t.3), custom_call_target="tpu_custom_call" | custom-call | tf_op jit(solution)/shard_map/pallas_call | solution.py:574
  5.4 2.6 %collective-permute-start = (f32[256,128]{1,0:T(8,128)S(1)}, f32[256,128]{1,0:T(8,128)S(1)}, u32[]{:S(2)}, u32[]{:S(2)}) collective-permute-start(f32[256,128]{1,0:T(8,128)S(1)} %get-tuple-element.53), channel_id=1, source_target_pairs={{0,4},{4,0},{8,12},{12,8},{16,20},{20,16},{24,28},{28,24},{1,5},{5... | collective-permute-start | bytes 393224 | tf_op jit(solution)/shard_map/ppermute | solution.py:556
  8.7 2.3 %collective-permute-done.xa = f32[256,128]{1,0:T(8,128)S(1)} collective-permute-done((f32[256,128]{1,0:T(8,128)S(1)}, f32[256,128]{1,0:T(8,128)S(1)}, u32[]{:S(2)}, u32[]{:S(2)}) %collective-permute-start) | collective-permute-done | bytes 131104 | tf_op jit(solution)/shard_map/ppermute | solution.py:556
  11.5 2.7 %collective-permute-start.4 = (f32[8,128]{1,0:T(8,128)S(1)}, f32[8,128]{1,0:T(8,128)S(1)}, u32[]{:S(2)}, u32[]{:S(2)}) collective-permute-start(f32[8,128]{1,0:T(8,128)S(1)} %get-tuple-element.58), channel_id=1, source_target_pairs={{0,1},{1,0},{2,3},{3,2},{4,5},{5,4},{6,7},{7,6},{8,9},{9,8},{10,11... | collective-permute-start | bytes 12296 | tf_op jit(solution)/shard_map/ppermute | solution.py:556
  14.8 7.0 %collective-permute-start.8 = (f32[64,128]{1,0:T(8,128)S(1)}, f32[64,128]{1,0:T(8,128)S(1)}, u32[]{:S(2)}, u32[]{:S(2)}) collective-permute-start(f32[64,128]{1,0:T(8,128)S(1)} %get-tuple-element.65), channel_id=1, source_target_pairs={{0,24},{4,28},{8,16},{12,20},{16,8},{20,12},{24,0},{28,4},{1,25},{... | collective-permute-start | bytes 98312 | tf_op jit(solution)/shard_map/ppermute | solution.py:564
  23.0 1.5 shard_map.98
  24.5 2.2 %collective-permute-done.7.refs_1_ = f32[64,128]{1,0:T(8,128)S(1)} collective-permute-done((f32[64,128]{1,0:T(8,128)S(1)}, f32[64,128]{1,0:T(8,128)S(1)}, u32[]{:S(2)}, u32[]{:S(2)}) %collective-permute-start.7) | collective-permute-done | bytes 32800 | tf_op jit(solution)/shard_map/ppermute | solution.py:564
  26.7 5.5 %shard_map.99 = (f32[2993,128]{1,0:T(8,128)S(1)}, f32[2993,128]{1,0:T(8,128)S(1)}, f32[5,64,128]{2,1,0:T(8,128)S(1)}, f32[2,64,128]{2,1,0:T(8,128)S(1)}, f32[2,6...) custom-call(s32[2]{0:T(128)S(1)} %pad_add_fusion.flags, ...), custom_call_target="tpu_custom_call" | custom-call | tf_op jit(solution)/shard_map/pallas_call | solution.py:574
  39.7 1.8 %collective-permute-start.11 = (f32[256,128]{1,0:T(8,128)}, f32[256,128]{1,0:T(8,128)}, u32[]{:S(2)}, u32[]{:S(2)}) collective-permute-start(f32[256,128]{1,0:T(8,128)} %get-tuple-element.71), channel_id=1, source_target_pairs={{0,1},{1,0},{2,3},{3,2},{4,5},{5,4},{6,7},{7,6},{8,9},{9,8},{10,11... | collective-permute-start | bytes 393224 | tf_op jit(solution)/shard_map/ppermute | solution.py:556
  41.5 2.2 %collective-permute-start.12 = (f32[256,128]{1,0:T(8,128)}, f32[256,128]{1,0:T(8,128)}, u32[]{:S(2)}, u32[]{:S(2)}) collective-permute-start(f32[256,128]{1,0:T(8,128)} %get-tuple-element.72), channel_id=1, source_target_pairs={{0,0},{1,2},{2,1},{3,3},{4,4},{5,6},{6,5},{7,7},{8,8},{9,10},{10,9... | collective-permute-start | bytes 393224 | tf_op jit(solution)/shard_map/ppermute | solution.py:557
  47.6 4.7 %all-to-all-start = ((f32[32,4,128]{2,1,0:T(4,128)}), f32[32,4,128]{2,1,0:T(4,128)S(1)}, u32[]{:S(2)}, u32[]{:S(2)}) async-start(f32[32,4,128]{2,1,0:T(4,128)} %bitcast.21), calls=%async_computation | async-start | bytes 131072 | tf_op jit(solution)/shard_map/all_to_all | solution.py:654
  52.3 1.5 collective-permute-start.10
  53.8 5.5 %collective-permute-start.15 = (f32[64,128]{1,0:T(8,128)}, f32[64,128]{1,0:T(8,128)S(1)}, u32[]{:S(2)}, u32[]{:S(2)}) collective-permute-start(f32[64,128]{1,0:T(8,128)} %copy-done.72), channel_id=1, source_target_pairs={{0,24},{4,28},{8,16},{12,20},{16,8},{20,12},{24,0},{28,4},{1,25},{... | collective-permute-start | bytes 98312 | tf_op jit(solution)/shard_map/ppermute | solution.py:564
  60.0 2.1 %collective-permute-start.13 = (f32[64,128]{1,0:T(8,128)}, f32[64,128]{1,0:T(8,128)S(1)}, u32[]{:S(2)}, u32[]{:S(2)}) collective-permute-start(f32[64,128]{1,0:T(8,128)} %copy-done.72), channel_id=1, source_target_pairs={{0,8},{4,12},{8,0},{12,4},{16,24},{20,28},{24,16},{28,20},{1,9},{5... | collective-permute-start | bytes 98312 | tf_op jit(solution)/shard_map/ppermute | solution.py:564
  82.4 6.1 %shard_map.101 = (f32[2993,128]{1,0:T(8,128)S(1)}, f32[2993,128]{1,0:T(8,128)S(1)}, f32[5,64,128]{2,1,0:T(8,128)S(1)}, f32[2112,128]{1,0:T(8,128)S(1)}, f32[2112...) custom-call(s32[2]{0:T(128)S(1)} %copy-done.66, ...), custom_call_target="tpu_custom_call" | custom-call | tf_op jit(solution)/shard_map/pallas_call | solution.py:574
  94.5 2.2 %collective-permute-start.19 = (f32[256,128]{1,0:T(8,128)}, f32[256,128]{1,0:T(8,128)}, u32[]{:S(2)}, u32[]{:S(2)}) collective-permute-start(f32[256,128]{1,0:T(8,128)} %get-tuple-element.91), channel_id=1, source_target_pairs={{0,0},{1,2},{2,1},{3,3},{4,4},{5,6},{6,5},{7,7},{8,8},{9,10},{10,9... | collective-permute-start | bytes 393224 | tf_op jit(solution)/shard_map/ppermute | solution.py:557
  96.7 1.4 collective-permute-done.16.xa
  100.6 4.6 %all-to-all-start.1 = ((f32[32,4,128]{2,1,0:T(4,128)}), f32[32,4,128]{2,1,0:T(4,128)S(1)}, u32[]{:S(2)}, u32[]{:S(2)}) async-start(f32[32,4,128]{2,1,0:T(4,128)} %bitcast.7), calls=%async_computation.1 | async-start | bytes 131072 | tf_op jit(solution)/shard_map/all_to_all | solution.py:654
  105.2 1.5 collective-permute-start.17
  106.7 5.7 %collective-permute-start.22 = (f32[64,128]{1,0:T(8,128)}, f32[64,128]{1,0:T(8,128)S(1)}, u32[]{:S(2)}, u32[]{:S(2)}) collective-permute-start(f32[64,128]{1,0:T(8,128)} %copy-done.73), channel_id=1, source_target_pairs={{0,24},{4,28},{8,16},{12,20},{16,8},{20,12},{24,0},{28,4},{1,25},{... | collective-permute-start | bytes 98312 | tf_op jit(solution)/shard_map/ppermute | solution.py:564
  112.4 1.9 %collective-permute-start.20 = (f32[64,128]{1,0:T(8,128)}, f32[64,128]{1,0:T(8,128)S(1)}, u32[]{:S(2)}, u32[]{:S(2)}) collective-permute-start(f32[64,128]{1,0:T(8,128)} %copy-done.73), channel_id=1, source_target_pairs={{0,8},{4,12},{8,0},{12,4},{16,24},{20,28},{24,16},{28,20},{1,9},{5... | collective-permute-start | bytes 98312 | tf_op jit(solution)/shard_map/ppermute | solution.py:564
  135.4 5.6 %shard_map.103 = (f32[2993,128]{1,0:T(8,128)S(1)}, f32[2993,128]{1,0:T(8,128)S(1)}, f32[5,64,128]{2,1,0:T(8,128)}, f32[2112,128]{1,0:T(8,128)S(1)}, f32[2112,128]{1,0:T(8,128)S(1)}, /*index=5*/f32[32,128]{1,0:T(8,128)S(1)}) custom-call(s32[2]{0:T(128)S(1)} %copy-done.67, f32[192,128]{1,0:T(8,128)S(1)} %copy-done.33, ...), custom_call_target="tpu_custom_call" | custom-call | tf_op jit(solution)/shard_map/pallas_call | solution.py:574
  141.0 10.7 %all_to_all.33 = f32[32,1,128]{2,1,0:T(1,128)S(1)} all-to-all(f32[32,1,128]{2,1,0:T(1,128)S(1)} %bitcast.22), channel_id=1, replica_groups=mesh['gx'=8,'gy'=4] {'gx','gy'}, dimensions={0} | all-to-all | bytes 32768 | tf_op jit(solution)/shard_map/all_to_all | solution.py:666
  151.7 1.9 %shard_map.104 = (f32[64,32,128]{2,1,0:T(8,128)}, f32[64,32,128]{2,1,0:T(8,128)}, f32[3]{0:T(128)}) custom-call(f32[128,128]{1,0:T(8,128)S(1)} %bitcast.17, f32[128,128]{1,0:T(8,128)S(1)} %bitcast.19, f32[32,128]{1,0:T(8,128)S(1)} %bitcast.20, f32[2112,128]{1,0:T(8,128)S(1)} %get-tuple-element.99.grho, f32[2112,128]{1,0:T(8,128)S(1)} %get-tuple-element.100.gsig, ...), custom_call_target="tpu_custom_call" | custom-call | tf_op jit(solution)/shard_map/pallas_call | solution.py:574
  (187 shorter events, 67.0 us)
Async XLA Ops:
  4.2 22.5 %collective-permute-start.2 = (f32[384,128]{1,0:T(8,128)S(1)}, f32[384,128]{1,0:T(8,128)S(1)}, u32[]{:S(2)}, u32[]{:S(2)}) collective-permute-start(f32[384,128]{1,0:T(8,128)S(1)} %get-tuple-element.56), channel_id=1, source_target_pairs={{0,1},{1,0},{2,3},{3,2},{4,5},{5,4},{6,7},{7,6},{8,9},{9,8},{10,11... | collective-permute-start | bytes 589832 | tf_op jit(solution)/shard_map/ppermute | solution.py:556
  4.8 21.9 %collective-permute-start.3 = (f32[384,128]{1,0:T(8,128)S(1)}, f32[384,128]{1,0:T(8,128)S(1)}, u32[]{:S(2)}, u32[]{:S(2)}) collective-permute-start(f32[384,128]{1,0:T(8,128)S(1)} %get-tuple-element.57), channel_id=1, source_target_pairs={{0,0},{1,2},{2,1},{3,3},{4,4},{5,6},{6,5},{7,7},{8,8},{9,10},{10,9... | collective-permute-start | bytes 589832 | tf_op jit(solution)/shard_map/ppermute | solution.py:557
  5.4 5.5 %collective-permute-start = (f32[256,128]{1,0:T(8,128)S(1)}, f32[256,128]{1,0:T(8,128)S(1)}, u32[]{:S(2)}, u32[]{:S(2)}) collective-permute-start(f32[256,128]{1,0:T(8,128)S(1)} %get-tuple-element.53), channel_id=1, source_target_pairs={{0,4},{4,0},{8,12},{12,8},{16,20},{20,16},{24,28},{28,24},{1,5},{5... | collective-permute-start | bytes 393224 | tf_op jit(solution)/shard_map/ppermute | solution.py:556
  11.5 10.3 %collective-permute-start.4 = (f32[8,128]{1,0:T(8,128)S(1)}, f32[8,128]{1,0:T(8,128)S(1)}, u32[]{:S(2)}, u32[]{:S(2)}) collective-permute-start(f32[8,128]{1,0:T(8,128)S(1)} %get-tuple-element.58), channel_id=1, source_target_pairs={{0,1},{1,0},{2,3},{3,2},{4,5},{5,4},{6,7},{7,6},{8,9},{9,8},{10,11... | collective-permute-start | bytes 12296 | tf_op jit(solution)/shard_map/ppermute | solution.py:556
  14.2 7.6 %collective-permute-start.5 = (f32[8,128]{1,0:T(8,128)S(1)}, f32[8,128]{1,0:T(8,128)S(1)}, u32[]{:S(2)}, u32[]{:S(2)}) collective-permute-start(f32[8,128]{1,0:T(8,128)S(1)} %get-tuple-element.59), channel_id=1, source_target_pairs={{0,0},{1,2},{2,1},{3,3},{4,4},{5,6},{6,5},{7,7},{8,8},{9,10},{10,9... | collective-permute-start | bytes 12296 | tf_op jit(solution)/shard_map/ppermute | solution.py:557
  14.8 9.6 %collective-permute-start.8 = (f32[64,128]{1,0:T(8,128)S(1)}, f32[64,128]{1,0:T(8,128)S(1)}, u32[]{:S(2)}, u32[]{:S(2)}) collective-permute-start(f32[64,128]{1,0:T(8,128)S(1)} %get-tuple-element.65), channel_id=1, source_target_pairs={{0,24},{4,28},{8,16},{12,20},{16,8},{20,12},{24,0},{28,4},{1,25},{... | collective-permute-start | bytes 98312 | tf_op jit(solution)/shard_map/ppermute | solution.py:564
  21.8 4.8 %collective-permute-start.7 = (f32[64,128]{1,0:T(8,128)S(1)}, f32[64,128]{1,0:T(8,128)S(1)}, u32[]{:S(2)}, u32[]{:S(2)}) collective-permute-start(f32[64,128]{1,0:T(8,128)S(1)} %get-tuple-element.65), channel_id=1, source_target_pairs={{0,16},{4,20},{8,24},{12,28},{16,0},{20,4},{24,8},{28,12},{1,17},{... | collective-permute-start | bytes 98312 | tf_op jit(solution)/shard_map/ppermute | solution.py:564
  21.8 4.8 %collective-permute-start.6 = (f32[64,128]{1,0:T(8,128)S(1)}, f32[64,128]{1,0:T(8,128)S(1)}, u32[]{:S(2)}, u32[]{:S(2)}) collective-permute-start(f32[64,128]{1,0:T(8,128)S(1)} %get-tuple-element.65), channel_id=1, source_target_pairs={{0,8},{4,12},{8,0},{12,4},{16,24},{20,28},{24,16},{28,20},{1,9},{5... | collective-permute-start | bytes 98312 | tf_op jit(solution)/shard_map/ppermute | solution.py:564
  39.7 4.8 %collective-permute-start.9 = (f32[192,128]{1,0:T(8,128)S(1)}, f32[192,128]{1,0:T(8,128)S(1)}, u32[]{:S(2)}, u32[]{:S(2)}) collective-permute-start(f32[192,128]{1,0:T(8,128)S(1)} %get-tuple-element.66), channel_id=1, source_target_pairs={{0,4},{4,0},{8,12},{12,8},{16,20},{20,16},{24,28},{28,24},{1,5},{5... | collective-permute-start | bytes 294920 | tf_op jit(solution)/shard_map/ppermute | solution.py:556
  39.7 26.0 %collective-permute-start.11 = (f32[256,128]{1,0:T(8,128)}, f32[256,128]{1,0:T(8,128)}, u32[]{:S(2)}, u32[]{:S(2)}) collective-permute-start(f32[256,128]{1,0:T(8,128)} %get-tuple-element.71), channel_id=1, source_target_pairs={{0,1},{1,0},{2,3},{3,2},{4,5},{5,4},{6,7},{7,6},{8,9},{9,8},{10,11... | collective-permute-start | bytes 393224 | tf_op jit(solution)/shard_map/ppermute | solution.py:556
  41.5 24.2 %collective-permute-start.12 = (f32[256,128]{1,0:T(8,128)}, f32[256,128]{1,0:T(8,128)}, u32[]{:S(2)}, u32[]{:S(2)}) collective-permute-start(f32[256,128]{1,0:T(8,128)} %get-tuple-element.72), channel_id=1, source_target_pairs={{0,0},{1,2},{2,1},{3,3},{4,4},{5,6},{6,5},{7,7},{8,8},{9,10},{10,9... | collective-permute-start | bytes 393224 | tf_op jit(solution)/shard_map/ppermute | solution.py:557
  47.6 18.1 %all-to-all-start = ((f32[32,4,128]{2,1,0:T(4,128)}), f32[32,4,128]{2,1,0:T(4,128)S(1)}, u32[]{:S(2)}, u32[]{:S(2)}) async-start(f32[32,4,128]{2,1,0:T(4,128)} %bitcast.21), calls=%async_computation | async-start | bytes 131072 | tf_op jit(solution)/shard_map/all_to_all | solution.py:654
  52.3 7.0 %collective-permute-start.10 = (f32[128,128]{1,0:T(8,128)}, f32[128,128]{1,0:T(8,128)S(1)}, u32[]{:S(2)}, u32[]{:S(2)}) collective-permute-start(f32[128,128]{1,0:T(8,128)} %copy-done.70), channel_id=1, source_target_pairs={{0,0},{4,8},{8,4},{12,16},{16,12},{20,24},{24,20},{28,28},{1,1},{5... | collective-permute-start | bytes 196616 | tf_op jit(solution)/shard_map/ppermute | solution.py:557
  53.8 8.9 %collective-permute-start.15 = (f32[64,128]{1,0:T(8,128)}, f32[64,128]{1,0:T(8,128)S(1)}, u32[]{:S(2)}, u32[]{:S(2)}) collective-permute-start(f32[64,128]{1,0:T(8,128)} %copy-done.72), channel_id=1, source_target_pairs={{0,24},{4,28},{8,16},{12,20},{16,8},{20,12},{24,0},{28,4},{1,25},{... | collective-permute-start | bytes 98312 | tf_op jit(solution)/shard_map/ppermute | solution.py:564
  59.4 5.1 %collective-permute-start.14 = (f32[64,128]{1,0:T(8,128)}, f32[64,128]{1,0:T(8,128)S(1)}, u32[]{:S(2)}, u32[]{:S(2)}) collective-permute-start(f32[64,128]{1,0:T(8,128)} %copy-done.72), channel_id=1, source_target_pairs={{0,16},{4,20},{8,24},{12,28},{16,0},{20,4},{24,8},{28,12},{1,17},{... | collective-permute-start | bytes 98312 | tf_op jit(solution)/shard_map/ppermute | solution.py:564
  60.0 5.1 %collective-permute-start.13 = (f32[64,128]{1,0:T(8,128)}, f32[64,128]{1,0:T(8,128)S(1)}, u32[]{:S(2)}, u32[]{:S(2)}) collective-permute-start(f32[64,128]{1,0:T(8,128)} %copy-done.72), channel_id=1, source_target_pairs={{0,8},{4,12},{8,0},{12,4},{16,24},{20,28},{24,16},{28,20},{1,9},{5... | collective-permute-start | bytes 98312 | tf_op jit(solution)/shard_map/ppermute | solution.py:564
  93.5 4.6 %collective-permute-start.16 = (f32[192,128]{1,0:T(8,128)S(1)}, f32[192,128]{1,0:T(8,128)S(1)}, u32[]{:S(2)}, u32[]{:S(2)}) collective-permute-start(f32[192,128]{1,0:T(8,128)S(1)} %get-tuple-element.85), channel_id=1, source_target_pairs={{0,4},{4,0},{8,12},{12,8},{16,20},{20,16},{24,28},{28,24},{1,5},{5... | collective-permute-start | bytes 294920 | tf_op jit(solution)/shard_map/ppermute | solution.py:556
  94.5 24.1 %collective-permute-start.18 = (f32[256,128]{1,0:T(8,128)}, f32[256,128]{1,0:T(8,128)}, u32[]{:S(2)}, u32[]{:S(2)}) collective-permute-start(f32[256,128]{1,0:T(8,128)} %get-tuple-element.90), channel_id=1, source_target_pairs={{0,1},{1,0},{2,3},{3,2},{4,5},{5,4},{6,7},{7,6},{8,9},{9,8},{10,11... | collective-permute-start | bytes 393224 | tf_op jit(solution)/shard_map/ppermute | solution.py:556
  94.5 24.1 %collective-permute-start.19 = (f32[256,128]{1,0:T(8,128)}, f32[256,128]{1,0:T(8,128)}, u32[]{:S(2)}, u32[]{:S(2)}) collective-permute-start(f32[256,128]{1,0:T(8,128)} %get-tuple-element.91), channel_id=1, source_target_pairs={{0,0},{1,2},{2,1},{3,3},{4,4},{5,6},{6,5},{7,7},{8,8},{9,10},{10,9... | collective-permute-start | bytes 393224 | tf_op jit(solution)/shard_map/ppermute | solution.py:557
  100.6 18.1 %all-to-all-start.1 = ((f32[32,4,128]{2,1,0:T(4,128)}), f32[32,4,128]{2,1,0:T(4,128)S(1)}, u32[]{:S(2)}, u32[]{:S(2)}) async-start(f32[32,4,128]{2,1,0:T(4,128)} %bitcast.7), calls=%async_computation.1 | async-start | bytes 131072 | tf_op jit(solution)/shard_map/all_to_all | solution.py:654
  105.2 7.2 %collective-permute-start.17 = (f32[128,128]{1,0:T(8,128)}, f32[128,128]{1,0:T(8,128)S(1)}, u32[]{:S(2)}, u32[]{:S(2)}) collective-permute-start(f32[128,128]{1,0:T(8,128)} %copy-done.71), channel_id=1, source_target_pairs={{0,0},{4,8},{8,4},{12,16},{16,12},{20,24},{24,20},{28,28},{1,1},{5... | collective-permute-start | bytes 196616 | tf_op jit(solution)/shard_map/ppermute | solution.py:557
  106.7 8.8 %collective-permute-start.22 = (f32[64,128]{1,0:T(8,128)}, f32[64,128]{1,0:T(8,128)S(1)}, u32[]{:S(2)}, u32[]{:S(2)}) collective-permute-start(f32[64,128]{1,0:T(8,128)} %copy-done.73), channel_id=1, source_target_pairs={{0,24},{4,28},{8,16},{12,20},{16,8},{20,12},{24,0},{28,4},{1,25},{... | collective-permute-start | bytes 98312 | tf_op jit(solution)/shard_map/ppermute | solution.py:564
  112.4 5.0 %collective-permute-start.21 = (f32[64,128]{1,0:T(8,128)}, f32[64,128]{1,0:T(8,128)S(1)}, u32[]{:S(2)}, u32[]{:S(2)}) collective-permute-start(f32[64,128]{1,0:T(8,128)} %copy-done.73), channel_id=1, source_target_pairs={{0,16},{4,20},{8,24},{12,28},{16,0},{20,4},{24,8},{28,12},{1,17},{... | collective-permute-start | bytes 98312 | tf_op jit(solution)/shard_map/ppermute | solution.py:564
  112.4 5.6 %collective-permute-start.20 = (f32[64,128]{1,0:T(8,128)}, f32[64,128]{1,0:T(8,128)S(1)}, u32[]{:S(2)}, u32[]{:S(2)}) collective-permute-start(f32[64,128]{1,0:T(8,128)} %copy-done.73), channel_id=1, source_target_pairs={{0,8},{4,12},{8,0},{12,4},{16,24},{20,28},{24,16},{28,20},{1,9},{5... | collective-permute-start | bytes 98312 | tf_op jit(solution)/shard_map/ppermute | solution.py:564
  (75 other events, 262.8 us)

commit v8 on v7

--- a/solution.py
+++ b/solution.py
@@ -83,7 +83,7 @@
     return low, high
 
 
-def first_kernel(g, flags, rho, sigma, zone, t, own, xa, xb, rims, zrims, sig_v, t_v, sems):
+def first_kernel(g, flags, rho, sigma, zone, t, own, xa, xb, sig_v, t_v, rims, zrims, sems):
     (even, _, _), _ = flags_of(g, flags)
     step = 8
     small = []
@@ -110,9 +110,11 @@
         for k in range(step):
             run = run + sig_v[c * step + k]
             total = total + run
-            seen = seen + t_v[c * step + k]
+            scaled = t_v[c * step + k] * (1.0 / g.xs)
+            t_v[c * step + k] = scaled
+            seen = seen + scaled
     own[0 : g.ny, :] = run
-    own[g.ny : 2 * g.ny, :] = total - seen * (1.0 / g.xs)
+    own[g.ny : 2 * g.ny, :] = total - seen
     for copy in small:
         copy.wait()
     at = 0
@@ -126,13 +128,12 @@
         put_pair(even, zrims[0, r].astype(F32), zrims[1, r].astype(F32), xa, xb, at)
         at += g.ny
     xa[at : at + g.ny, :] = run
-    xa[at + g.ny : at + 2 * g.ny, :] = total - seen * (1.0 / g.xs)
-
-
-def bounds_kernel(g, zones, zlow, zhigh, zone, t, low_o, high_o, t_o):
+    xa[at + g.ny : at + 2 * g.ny, :] = total - seen
+
+
+def bounds_kernel(g, zones, zlow, zhigh, zone, low_o, high_o):
     def body(x, carry):
         low_o[x], high_o[x] = bounds_of(zones, zone[x], zlow, zhigh)
-        t_o[x] = t[x] * (1.0 / g.xs)
         return carry
 
     lax.fori_loop(0, g.nx, body, 0, unroll=8)
@@ -488,6 +489,7 @@
 def later_step(g, last, flags, xa, xb, ya, yb, sums_i, own_i, grho_i, gsig_i, rho_i, sig_i, low, high,
                xlow, xhigh, ylow, yhigh, trs_i, p, q, t, table, ztable, *refs):
     others, rest = refs[: g.pairs - 1], refs[g.pairs - 1 :]
+    rest = (*rest[:2], rest[-1], *rest[2:-1]) if last else rest
     rho_e, sig_e, trs = rest[:3]
     ny = g.ny
     ar, asig = alphas(g, sums_i)
@@ -604,16 +606,16 @@
     ext_v = pltpu.VMEM((g.ext, nz), F32)
     core_scratch = [win] * 2 + [ext_v] * 2 + [win] * 2 + [pltpu.VMEM((nx * ny, nz), F32)] + [win] * 4
 
-    own, xa, xb = call(
-        functools.partial(first_kernel, g), [own_shape, xa_shape(3), xb_shape(3)],
+    own, xa, xb, sig, t = call(
+        functools.partial(first_kernel, g), [own_shape, xa_shape(3), xb_shape(3), block, block],
         [SMEM] + [HBM] * 4, (flags, *(pltpu.with_memory_space_constraint(v, pltpu.HBM) for v in (density, slowness, zone_map, time_obs))),
         [pltpu.VMEM((2, 1, 2, ny, nz), F32), pltpu.VMEM((2, 2, ny, nz), jnp.int32),
-         pltpu.VMEM((nx, ny, nz), F32), pltpu.VMEM((nx, ny, nz), F32), pltpu.SemaphoreType.DMA((4 + nx // 4,))],
+         pltpu.SemaphoreType.DMA((4 + nx // 4,))],
     )
     xa, xb = exchange("gx", xa, xb)
-    low, high, t = call(
-        functools.partial(bounds_kernel, g, zones), [block] * 3,
-        [SMEM, SMEM] + [VMEM] * 2, (zone_low, zone_high, zone_map, time_obs),
+    low, high = call(
+        functools.partial(bounds_kernel, g, zones), [block] * 2,
+        [SMEM, SMEM, VMEM], (zone_low, zone_high, zone_map),
     )
     q, p, table, ztable = call(
         functools.partial(spread_kernel, g),
@@ -622,7 +624,7 @@
     as_rows = lambda v: v.reshape(nx * ny, nz)
     ya, yb = call(
         functools.partial(sides_kernel, g, 3), [ymsg(3)] * 2,
-        [SMEM] + [VMEM] * 4, (flags, own, as_rows(density), as_rows(slowness), as_rows(zone_map)),
+        [SMEM] + [VMEM] * 4, (flags, own, as_rows(density), as_rows(sig), as_rows(zone_map)),
     )
     ya, yb = exchange("gy", ya, yb)
     ca, cb, pair = call(
@@ -637,7 +639,7 @@
         functools.partial(opening_step, g, zones),
         [ext, ext, trs_shape, xbound, xbound, ybound, ybound] + ends,
         [SMEM] * 3 + [VMEM] * (14 + len(others)),
-        (flags, zone_low, zone_high, xa, xb, ya, yb, ca, cb, own, density, slowness, p, q, t, table, ztable, *others),
+        (flags, zone_low, zone_high, xa, xb, ya, yb, ca, cb, own, density, sig, p, q, t, table, ztable, *others),
         core_scratch, 24,
     )
     rho_e, sig_e, trs, xlow, xhigh, ylow, yhigh, grho, gsig, head, own, xa, xb, ya, yb = outs
@@ -654,15 +656,17 @@
         sums = lax.all_to_all(sums, both, 0, 0, tiled=True)
         history.append(sums)
         outs = call(
-            functools.partial(later_step, g, last), [ext, ext, trs_shape] + ([flat, flat, sums_shape] if last else ends),
+            functools.partial(later_step, g, last),
+            [ext, ext] + ([flat, flat, sums_shape] if last else [trs_shape] + ends),
             [SMEM] + [VMEM] * (22 + len(others)),
             (flags, xa, xb, ya, yb, sums, own, grho, gsig, rho_e, sig_e, low, high, xlow, xhigh, ylow, yhigh, trs,
              p, q, t, table, ztable, *others),
-            core_scratch, 24,
+            core_scratch + ([pltpu.VMEM(*trs_shape)] if last else []), 24,
         )
-        rho_e, sig_e, trs, grho, gsig, head = outs[:6]
-        if not last:
-            own, xa, xb, ya, yb = outs[6:]
+        if last:
+            rho_e, sig_e, grho, gsig, head = outs
+        else:
+            rho_e, sig_e, trs, grho, gsig, head, own, xa, xb, ya, yb = outs
     history.append(lax.all_to_all(head, both, 0, 0, tiled=True))
     rho, sigma, obj = call(
         functools.partial(closing_kernel, g), [block, block, ((ITERS,), F32)],

time: 156 us -> 159 us (1.019)
  local copies, waits for them, and re-layouts: 53.9 us -> 58.1 us
    unnamed x148 -> x154, local copies, waits for them, and re-layouts: 53.9 us -> 58.1 us
  transfers between devices with their start and end apart: 25 -> 25, of which waited for: 8 -> 7; matrix products, arithmetic and copies ran while one was open for 0% -> 0% of each run, Pallas kernels for 3% -> 3%
where the time goes in v8:
time: 159 us; the launch traced here: 157 us
  local copies, waits for them, and re-layouts  58.1 us (37%)
  starting transfers between devices  51.3 us (32%)
  Pallas kernels  26.1 us (16%)
  blocking collectives  10.7 us (7%)
  waiting for transfers between devices  9.9 us (6%)
    unnamed x154, local copies, waits for them, and re-layouts  58.1 us
    pallas_call x11, Pallas kernels, call(): pl.pallas_call(body, out_shape=[jax.ShapeDtypeStruct(s, d) for s, d in sh...  26.1 us
    ppermute x9, starting transfers between devices, pair_totals(): out.append(lax.ppermute(pair, 'gx', [(i, i ^ 2 * m) for i in range(size)]))  22.8 us
    all_to_all x1, blocking collectives, local(): history.append(lax.all_to_all(head, both, 0, 0, tiled=True))  10.7 us
    all_to_all x2, starting transfers between devices, local(): sums = lax.all_to_all(sums, both, 0, 0, tiled=True)  9.72 us
    ppermute x7, starting transfers between devices, exchange(): a = lax.ppermute(a, axis, pa)  9.52 us
    ppermute x7, starting transfers between devices, exchange(): b = lax.ppermute(b, axis, pb)  9.26 us
    ppermute x9, waiting for transfers between devices, pair_totals(): out.append(lax.ppermute(pair, 'gx', [(i, i ^ 2 * m) for i in range(size)]))  6.19 us
  transfers between devices with their start and end apart: 25, of which 7 were waited for; matrix products, arithmetic and copies ran while one was open for 0% of the time, Pallas kernels for 3%

profile of v8, /device:TPU:0, one launch (start us, length us, event | category | flops | bytes accessed | tf_op | source)
XLA Modules:
  0.0 157.3 jit_solution(9213418353212082473)
XLA Ops:
  0.7 2.4 %shard_map.94 = (f32[64,128]{1,0:T(8,128)S(1)}, f32[256,128]{1,0:T(8,128)S(1)}, f32[192,128]{1,0:T(8,128)S(1)}, f32[64,32,128]{2,1,0:T(8,128)S(1)}, f32[64,32,128]{2,1,0:T(8,128)S(1)}) custom-call(s32[2]{0:T(128)S(1)} %pad_add_fusion.flags, f32[64,32,128]{2,1,0:T(8,128)} %rho.3, f32[64,32,128]{2,1,0:T(8,128)} %sigma.1, s32[64,32,128]{2,1,0:T(8,128)} %zone.3, ...), custom_call_target="tpu_custom_call" | custom-call | tf_op jit(solution)/shard_map/pallas_call | solution.py:576
  5.2 2.6 %collective-permute-start = (f32[256,128]{1,0:T(8,128)S(1)}, f32[256,128]{1,0:T(8,128)S(1)}, u32[]{:S(2)}, u32[]{:S(2)}) collective-permute-start(f32[256,128]{1,0:T(8,128)S(1)} %get-tuple-element.54), channel_id=1, source_target_pairs={{0,4},{4,0},{8,12},{12,8},{16,20},{20,16},{24,28},{28,24},{1,5},{5... | collective-permute-start | bytes 393224 | tf_op jit(solution)/shard_map/ppermute | solution.py:558
  8.5 2.3 %collective-permute-done.xa = f32[256,128]{1,0:T(8,128)S(1)} collective-permute-done((f32[256,128]{1,0:T(8,128)S(1)}, f32[256,128]{1,0:T(8,128)S(1)}, u32[]{:S(2)}, u32[]{:S(2)}) %collective-permute-start) | collective-permute-done | bytes 131104 | tf_op jit(solution)/shard_map/ppermute | solution.py:558
  11.3 2.7 %collective-permute-start.4 = (f32[8,128]{1,0:T(8,128)S(1)}, f32[8,128]{1,0:T(8,128)S(1)}, u32[]{:S(2)}, u32[]{:S(2)}) collective-permute-start(f32[8,128]{1,0:T(8,128)S(1)} %get-tuple-element.60), channel_id=1, source_target_pairs={{0,1},{1,0},{2,3},{3,2},{4,5},{5,4},{6,7},{7,6},{8,9},{9,8},{10,11... | collective-permute-start | bytes 12296 | tf_op jit(solution)/shard_map/ppermute | solution.py:558
  14.6 7.0 %collective-permute-start.8 = (f32[64,128]{1,0:T(8,128)S(1)}, f32[64,128]{1,0:T(8,128)S(1)}, u32[]{:S(2)}, u32[]{:S(2)}) collective-permute-start(f32[64,128]{1,0:T(8,128)S(1)} %get-tuple-element.67), channel_id=1, source_target_pairs={{0,24},{4,28},{8,16},{12,20},{16,8},{20,12},{24,0},{28,4},{1,25},{... | collective-permute-start | bytes 98312 | tf_op jit(solution)/shard_map/ppermute | solution.py:566
  23.5 3.0 %collective-permute-done.7.refs_1_ = f32[64,128]{1,0:T(8,128)S(1)} collective-permute-done((f32[64,128]{1,0:T(8,128)S(1)}, f32[64,128]{1,0:T(8,128)S(1)}, u32[]{:S(2)}, u32[]{:S(2)}) %collective-permute-start.7) | collective-permute-done | bytes 32800 | tf_op jit(solution)/shard_map/ppermute | solution.py:566
  26.5 5.5 %shard_map.98 = (f32[2993,128]{1,0:T(8,128)S(1)}, f32[2993,128]{1,0:T(8,128)S(1)}, f32[5,64,128]{2,1,0:T(8,128)S(1)}, f32[2,64,128]{2,1,0:T(8,128)S(1)}, f32[2,6...) custom-call(s32[2]{0:T(128)S(1)} %pad_add_fusion.flags, ...), custom_call_target="tpu_custom_call" | custom-call | tf_op jit(solution)/shard_map/pallas_call | solution.py:576
  39.5 1.8 %collective-permute-start.11 = (f32[256,128]{1,0:T(8,128)}, f32[256,128]{1,0:T(8,128)}, u32[]{:S(2)}, u32[]{:S(2)}) collective-permute-start(f32[256,128]{1,0:T(8,128)} %get-tuple-element.73), channel_id=1, source_target_pairs={{0,1},{1,0},{2,3},{3,2},{4,5},{5,4},{6,7},{7,6},{8,9},{9,8},{10,11... | collective-permute-start | bytes 393224 | tf_op jit(solution)/shard_map/ppermute | solution.py:558
  41.3 2.1 %collective-permute-start.12 = (f32[256,128]{1,0:T(8,128)}, f32[256,128]{1,0:T(8,128)}, u32[]{:S(2)}, u32[]{:S(2)}) collective-permute-start(f32[256,128]{1,0:T(8,128)} %get-tuple-element.74), channel_id=1, source_target_pairs={{0,0},{1,2},{2,1},{3,3},{4,4},{5,6},{6,5},{7,7},{8,8},{9,10},{10,9... | collective-permute-start | bytes 393224 | tf_op jit(solution)/shard_map/ppermute | solution.py:559
  47.3 4.8 %all-to-all-start = ((f32[32,4,128]{2,1,0:T(4,128)}), f32[32,4,128]{2,1,0:T(4,128)S(1)}, u32[]{:S(2)}, u32[]{:S(2)}) async-start(f32[32,4,128]{2,1,0:T(4,128)} %bitcast.21), calls=%async_computation | async-start | bytes 131072 | tf_op jit(solution)/shard_map/all_to_all | solution.py:656
  52.1 1.5 collective-permute-start.10
  53.6 5.5 %collective-permute-start.15 = (f32[64,128]{1,0:T(8,128)}, f32[64,128]{1,0:T(8,128)S(1)}, u32[]{:S(2)}, u32[]{:S(2)}) collective-permute-start(f32[64,128]{1,0:T(8,128)} %copy-done.75), channel_id=1, source_target_pairs={{0,24},{4,28},{8,16},{12,20},{16,8},{20,12},{24,0},{28,4},{1,25},{... | collective-permute-start | bytes 98312 | tf_op jit(solution)/shard_map/ppermute | solution.py:566
  59.8 2.1 %collective-permute-start.13 = (f32[64,128]{1,0:T(8,128)}, f32[64,128]{1,0:T(8,128)S(1)}, u32[]{:S(2)}, u32[]{:S(2)}) collective-permute-start(f32[64,128]{1,0:T(8,128)} %copy-done.75), channel_id=1, source_target_pairs={{0,8},{4,12},{8,0},{12,4},{16,24},{20,28},{24,16},{28,20},{1,9},{5... | collective-permute-start | bytes 98312 | tf_op jit(solution)/shard_map/ppermute | solution.py:566
  63.2 1.4 shard_map.100
  86.2 6.1 %shard_map.101 = (f32[2993,128]{1,0:T(8,128)S(1)}, f32[2993,128]{1,0:T(8,128)S(1)}, f32[5,64,128]{2,1,0:T(8,128)S(1)}, f32[2112,128]{1,0:T(8,128)S(1)}, f32[2112...) custom-call(s32[2]{0:T(128)S(1)} %copy-done.67, ...), custom_call_target="tpu_custom_call" | custom-call | tf_op jit(solution)/shard_map/pallas_call | solution.py:576
  97.3 1.9 %collective-permute-start.16 = (f32[192,128]{1,0:T(8,128)S(1)}, f32[192,128]{1,0:T(8,128)S(1)}, u32[]{:S(2)}, u32[]{:S(2)}) collective-permute-start(f32[192,128]{1,0:T(8,128)S(1)} %get-tuple-element.87), channel_id=1, source_target_pairs={{0,4},{4,0},{8,12},{12,8},{16,20},{20,16},{24,28},{28,24},{1,5},{5... | collective-permute-start | bytes 294920 | tf_op jit(solution)/shard_map/ppermute | solution.py:558
  99.2 2.1 %collective-permute-start.19 = (f32[256,128]{1,0:T(8,128)}, f32[256,128]{1,0:T(8,128)}, u32[]{:S(2)}, u32[]{:S(2)}) collective-permute-start(f32[256,128]{1,0:T(8,128)} %get-tuple-element.93), channel_id=1, source_target_pairs={{0,0},{1,2},{2,1},{3,3},{4,4},{5,6},{6,5},{7,7},{8,8},{9,10},{10,9... | collective-permute-start | bytes 393224 | tf_op jit(solution)/shard_map/ppermute | solution.py:559
  104.3 4.9 %all-to-all-start.1 = ((f32[32,4,128]{2,1,0:T(4,128)}), f32[32,4,128]{2,1,0:T(4,128)S(1)}, u32[]{:S(2)}, u32[]{:S(2)}) async-start(f32[32,4,128]{2,1,0:T(4,128)} %bitcast.7), calls=%async_computation.1 | async-start | bytes 131072 | tf_op jit(solution)/shard_map/all_to_all | solution.py:656
  109.3 1.5 collective-permute-start.17
  110.8 5.7 %collective-permute-start.22 = (f32[64,128]{1,0:T(8,128)}, f32[64,128]{1,0:T(8,128)S(1)}, u32[]{:S(2)}, u32[]{:S(2)}) collective-permute-start(f32[64,128]{1,0:T(8,128)} %copy-done.76), channel_id=1, source_target_pairs={{0,24},{4,28},{8,16},{12,20},{16,8},{20,12},{24,0},{28,4},{1,25},{... | collective-permute-start | bytes 98312 | tf_op jit(solution)/shard_map/ppermute | solution.py:566
  116.5 1.9 %collective-permute-start.20 = (f32[64,128]{1,0:T(8,128)}, f32[64,128]{1,0:T(8,128)S(1)}, u32[]{:S(2)}, u32[]{:S(2)}) collective-permute-start(f32[64,128]{1,0:T(8,128)} %copy-done.76), channel_id=1, source_target_pairs={{0,8},{4,12},{8,0},{12,4},{16,24},{20,28},{24,16},{28,20},{1,9},{5... | collective-permute-start | bytes 98312 | tf_op jit(solution)/shard_map/ppermute | solution.py:566
  139.4 5.1 %shard_map.103 = (f32[2993,128]{1,0:T(8,128)S(1)}, f32[2993,128]{1,0:T(8,128)S(1)}, f32[2112,128]{1,0:T(8,128)S(1)}, f32[2112,128]{1,0:T(8,128)S(1)}, f32[32,128]{1,0:T(8,128)S(1)}) custom-call(s32[2]{0:T(128)S(1)} %copy-done.68, f32[192,128]{1,0:T(8,128)S(1)} %copy-done.36, f32[128,128]{1,0:T(8,128)S(1)} %collective-permute-done.17.xb, ...), custom_call_target="tpu_custom_call" | custom-call | tf_op jit(solution)/shard_map/pallas_call | solution.py:576
  144.6 10.7 %all_to_all.33 = f32[32,1,128]{2,1,0:T(1,128)S(1)} all-to-all(f32[32,1,128]{2,1,0:T(1,128)S(1)} %bitcast.22), channel_id=1, replica_groups=mesh['gx'=8,'gy'=4] {'gx','gy'}, dimensions={0} | all-to-all | bytes 32768 | tf_op jit(solution)/shard_map/all_to_all | solution.py:670
  155.2 1.9 %shard_map.104 = (f32[64,32,128]{2,1,0:T(8,128)}, f32[64,32,128]{2,1,0:T(8,128)}, f32[3]{0:T(128)}) custom-call(f32[128,128]{1,0:T(8,128)S(1)} %bitcast.17, f32[128,128]{1,0:T(8,128)S(1)} %bitcast.19, f32[32,128]{1,0:T(8,128)S(1)} %bitcast.20, f32[2112,128]{1,0:T(8,128)S(1)} %get-tuple-element.101.grho, f32[2112,128]{1,0:T(8,128)S(1)} %get-tuple-element.102.gsig, ...), custom_call_target="tpu_custom_call" | custom-call | tf_op jit(solution)/shard_map/pallas_call | solution.py:576
  (193 shorter events, 69.7 us)
Async XLA Ops:
  4.0 22.5 %collective-permute-start.2 = (f32[384,128]{1,0:T(8,128)S(1)}, f32[384,128]{1,0:T(8,128)S(1)}, u32[]{:S(2)}, u32[]{:S(2)}) collective-permute-start(f32[384,128]{1,0:T(8,128)S(1)} %get-tuple-element.58), channel_id=1, source_target_pairs={{0,1},{1,0},{2,3},{3,2},{4,5},{5,4},{6,7},{7,6},{8,9},{9,8},{10,11... | collective-permute-start | bytes 589832 | tf_op jit(solution)/shard_map/ppermute | solution.py:558
  4.5 21.9 %collective-permute-start.3 = (f32[384,128]{1,0:T(8,128)S(1)}, f32[384,128]{1,0:T(8,128)S(1)}, u32[]{:S(2)}, u32[]{:S(2)}) collective-permute-start(f32[384,128]{1,0:T(8,128)S(1)} %get-tuple-element.59), channel_id=1, source_target_pairs={{0,0},{1,2},{2,1},{3,3},{4,4},{5,6},{6,5},{7,7},{8,8},{9,10},{10,9... | collective-permute-start | bytes 589832 | tf_op jit(solution)/shard_map/ppermute | solution.py:559
  5.2 5.5 %collective-permute-start = (f32[256,128]{1,0:T(8,128)S(1)}, f32[256,128]{1,0:T(8,128)S(1)}, u32[]{:S(2)}, u32[]{:S(2)}) collective-permute-start(f32[256,128]{1,0:T(8,128)S(1)} %get-tuple-element.54), channel_id=1, source_target_pairs={{0,4},{4,0},{8,12},{12,8},{16,20},{20,16},{24,28},{28,24},{1,5},{5... | collective-permute-start | bytes 393224 | tf_op jit(solution)/shard_map/ppermute | solution.py:558
  11.3 10.3 %collective-permute-start.4 = (f32[8,128]{1,0:T(8,128)S(1)}, f32[8,128]{1,0:T(8,128)S(1)}, u32[]{:S(2)}, u32[]{:S(2)}) collective-permute-start(f32[8,128]{1,0:T(8,128)S(1)} %get-tuple-element.60), channel_id=1, source_target_pairs={{0,1},{1,0},{2,3},{3,2},{4,5},{5,4},{6,7},{7,6},{8,9},{9,8},{10,11... | collective-permute-start | bytes 12296 | tf_op jit(solution)/shard_map/ppermute | solution.py:558
  14.0 7.6 %collective-permute-start.5 = (f32[8,128]{1,0:T(8,128)S(1)}, f32[8,128]{1,0:T(8,128)S(1)}, u32[]{:S(2)}, u32[]{:S(2)}) collective-permute-start(f32[8,128]{1,0:T(8,128)S(1)} %get-tuple-element.61), channel_id=1, source_target_pairs={{0,0},{1,2},{2,1},{3,3},{4,4},{5,6},{6,5},{7,7},{8,8},{9,10},{10,9... | collective-permute-start | bytes 12296 | tf_op jit(solution)/shard_map/ppermute | solution.py:559
  14.6 8.8 %collective-permute-start.8 = (f32[64,128]{1,0:T(8,128)S(1)}, f32[64,128]{1,0:T(8,128)S(1)}, u32[]{:S(2)}, u32[]{:S(2)}) collective-permute-start(f32[64,128]{1,0:T(8,128)S(1)} %get-tuple-element.67), channel_id=1, source_target_pairs={{0,24},{4,28},{8,16},{12,20},{16,8},{20,12},{24,0},{28,4},{1,25},{... | collective-permute-start | bytes 98312 | tf_op jit(solution)/shard_map/ppermute | solution.py:566
  21.6 4.8 %collective-permute-start.7 = (f32[64,128]{1,0:T(8,128)S(1)}, f32[64,128]{1,0:T(8,128)S(1)}, u32[]{:S(2)}, u32[]{:S(2)}) collective-permute-start(f32[64,128]{1,0:T(8,128)S(1)} %get-tuple-element.67), channel_id=1, source_target_pairs={{0,16},{4,20},{8,24},{12,28},{16,0},{20,4},{24,8},{28,12},{1,17},{... | collective-permute-start | bytes 98312 | tf_op jit(solution)/shard_map/ppermute | solution.py:566
  21.6 4.8 %collective-permute-start.6 = (f32[64,128]{1,0:T(8,128)S(1)}, f32[64,128]{1,0:T(8,128)S(1)}, u32[]{:S(2)}, u32[]{:S(2)}) collective-permute-start(f32[64,128]{1,0:T(8,128)S(1)} %get-tuple-element.67), channel_id=1, source_target_pairs={{0,8},{4,12},{8,0},{12,4},{16,24},{20,28},{24,16},{28,20},{1,9},{5... | collective-permute-start | bytes 98312 | tf_op jit(solution)/shard_map/ppermute | solution.py:566
  39.5 4.8 %collective-permute-start.9 = (f32[192,128]{1,0:T(8,128)S(1)}, f32[192,128]{1,0:T(8,128)S(1)}, u32[]{:S(2)}, u32[]{:S(2)}) collective-permute-start(f32[192,128]{1,0:T(8,128)S(1)} %get-tuple-element.68), channel_id=1, source_target_pairs={{0,4},{4,0},{8,12},{12,8},{16,20},{20,16},{24,28},{28,24},{1,5},{5... | collective-permute-start | bytes 294920 | tf_op jit(solution)/shard_map/ppermute | solution.py:558
  39.5 28.9 %collective-permute-start.11 = (f32[256,128]{1,0:T(8,128)}, f32[256,128]{1,0:T(8,128)}, u32[]{:S(2)}, u32[]{:S(2)}) collective-permute-start(f32[256,128]{1,0:T(8,128)} %get-tuple-element.73), channel_id=1, source_target_pairs={{0,1},{1,0},{2,3},{3,2},{4,5},{5,4},{6,7},{7,6},{8,9},{9,8},{10,11... | collective-permute-start | bytes 393224 | tf_op jit(solution)/shard_map/ppermute | solution.py:558
  41.3 27.1 %collective-permute-start.12 = (f32[256,128]{1,0:T(8,128)}, f32[256,128]{1,0:T(8,128)}, u32[]{:S(2)}, u32[]{:S(2)}) collective-permute-start(f32[256,128]{1,0:T(8,128)} %get-tuple-element.74), channel_id=1, source_target_pairs={{0,0},{1,2},{2,1},{3,3},{4,4},{5,6},{6,5},{7,7},{8,8},{9,10},{10,9... | collective-permute-start | bytes 393224 | tf_op jit(solution)/shard_map/ppermute | solution.py:559
  47.3 21.0 %all-to-all-start = ((f32[32,4,128]{2,1,0:T(4,128)}), f32[32,4,128]{2,1,0:T(4,128)S(1)}, u32[]{:S(2)}, u32[]{:S(2)}) async-start(f32[32,4,128]{2,1,0:T(4,128)} %bitcast.21), calls=%async_computation | async-start | bytes 131072 | tf_op jit(solution)/shard_map/all_to_all | solution.py:656
  52.1 7.0 %collective-permute-start.10 = (f32[128,128]{1,0:T(8,128)}, f32[128,128]{1,0:T(8,128)S(1)}, u32[]{:S(2)}, u32[]{:S(2)}) collective-permute-start(f32[128,128]{1,0:T(8,128)} %copy-done.73), channel_id=1, source_target_pairs={{0,0},{4,8},{8,4},{12,16},{16,12},{20,24},{24,20},{28,28},{1,1},{5... | collective-permute-start | bytes 196616 | tf_op jit(solution)/shard_map/ppermute | solution.py:559
  53.6 12.9 %collective-permute-start.15 = (f32[64,128]{1,0:T(8,128)}, f32[64,128]{1,0:T(8,128)S(1)}, u32[]{:S(2)}, u32[]{:S(2)}) collective-permute-start(f32[64,128]{1,0:T(8,128)} %copy-done.75), channel_id=1, source_target_pairs={{0,24},{4,28},{8,16},{12,20},{16,8},{20,12},{24,0},{28,4},{1,25},{... | collective-permute-start | bytes 98312 | tf_op jit(solution)/shard_map/ppermute | solution.py:566
  59.1 8.0 %collective-permute-start.14 = (f32[64,128]{1,0:T(8,128)}, f32[64,128]{1,0:T(8,128)S(1)}, u32[]{:S(2)}, u32[]{:S(2)}) collective-permute-start(f32[64,128]{1,0:T(8,128)} %copy-done.75), channel_id=1, source_target_pairs={{0,16},{4,20},{8,24},{12,28},{16,0},{20,4},{24,8},{28,12},{1,17},{... | collective-permute-start | bytes 98312 | tf_op jit(solution)/shard_map/ppermute | solution.py:566
  59.8 8.0 %collective-permute-start.13 = (f32[64,128]{1,0:T(8,128)}, f32[64,128]{1,0:T(8,128)S(1)}, u32[]{:S(2)}, u32[]{:S(2)}) collective-permute-start(f32[64,128]{1,0:T(8,128)} %copy-done.75), channel_id=1, source_target_pairs={{0,8},{4,12},{8,0},{12,4},{16,24},{20,28},{24,16},{28,20},{1,9},{5... | collective-permute-start | bytes 98312 | tf_op jit(solution)/shard_map/ppermute | solution.py:566
  97.3 4.6 %collective-permute-start.16 = (f32[192,128]{1,0:T(8,128)S(1)}, f32[192,128]{1,0:T(8,128)S(1)}, u32[]{:S(2)}, u32[]{:S(2)}) collective-permute-start(f32[192,128]{1,0:T(8,128)S(1)} %get-tuple-element.87), channel_id=1, source_target_pairs={{0,4},{4,0},{8,12},{12,8},{16,20},{20,16},{24,28},{28,24},{1,5},{5... | collective-permute-start | bytes 294920 | tf_op jit(solution)/shard_map/ppermute | solution.py:558
  99.2 23.6 %collective-permute-start.18 = (f32[256,128]{1,0:T(8,128)}, f32[256,128]{1,0:T(8,128)}, u32[]{:S(2)}, u32[]{:S(2)}) collective-permute-start(f32[256,128]{1,0:T(8,128)} %get-tuple-element.92), channel_id=1, source_target_pairs={{0,1},{1,0},{2,3},{3,2},{4,5},{5,4},{6,7},{7,6},{8,9},{9,8},{10,11... | collective-permute-start | bytes 393224 | tf_op jit(solution)/shard_map/ppermute | solution.py:558
  99.2 23.6 %collective-permute-start.19 = (f32[256,128]{1,0:T(8,128)}, f32[256,128]{1,0:T(8,128)}, u32[]{:S(2)}, u32[]{:S(2)}) collective-permute-start(f32[256,128]{1,0:T(8,128)} %get-tuple-element.93), channel_id=1, source_target_pairs={{0,0},{1,2},{2,1},{3,3},{4,4},{5,6},{6,5},{7,7},{8,8},{9,10},{10,9... | collective-permute-start | bytes 393224 | tf_op jit(solution)/shard_map/ppermute | solution.py:559
  104.3 18.4 %all-to-all-start.1 = ((f32[32,4,128]{2,1,0:T(4,128)}), f32[32,4,128]{2,1,0:T(4,128)S(1)}, u32[]{:S(2)}, u32[]{:S(2)}) async-start(f32[32,4,128]{2,1,0:T(4,128)} %bitcast.7), calls=%async_computation.1 | async-start | bytes 131072 | tf_op jit(solution)/shard_map/all_to_all | solution.py:656
  109.3 7.2 %collective-permute-start.17 = (f32[128,128]{1,0:T(8,128)}, f32[128,128]{1,0:T(8,128)S(1)}, u32[]{:S(2)}, u32[]{:S(2)}) collective-permute-start(f32[128,128]{1,0:T(8,128)} %copy-done.74), channel_id=1, source_target_pairs={{0,0},{4,8},{8,4},{12,16},{16,12},{20,24},{24,20},{28,28},{1,1},{5... | collective-permute-start | bytes 196616 | tf_op jit(solution)/shard_map/ppermute | solution.py:559
  110.8 8.8 %collective-permute-start.22 = (f32[64,128]{1,0:T(8,128)}, f32[64,128]{1,0:T(8,128)S(1)}, u32[]{:S(2)}, u32[]{:S(2)}) collective-permute-start(f32[64,128]{1,0:T(8,128)} %copy-done.76), channel_id=1, source_target_pairs={{0,24},{4,28},{8,16},{12,20},{16,8},{20,12},{24,0},{28,4},{1,25},{... | collective-permute-start | bytes 98312 | tf_op jit(solution)/shard_map/ppermute | solution.py:566
  116.5 5.0 %collective-permute-start.21 = (f32[64,128]{1,0:T(8,128)}, f32[64,128]{1,0:T(8,128)S(1)}, u32[]{:S(2)}, u32[]{:S(2)}) collective-permute-start(f32[64,128]{1,0:T(8,128)} %copy-done.76), channel_id=1, source_target_pairs={{0,16},{4,20},{8,24},{12,28},{16,0},{20,4},{24,8},{28,12},{1,17},{... | collective-permute-start | bytes 98312 | tf_op jit(solution)/shard_map/ppermute | solution.py:566
  116.5 5.6 %collective-permute-start.20 = (f32[64,128]{1,0:T(8,128)}, f32[64,128]{1,0:T(8,128)S(1)}, u32[]{:S(2)}, u32[]{:S(2)}) collective-permute-start(f32[64,128]{1,0:T(8,128)} %copy-done.76), channel_id=1, source_target_pairs={{0,8},{4,12},{8,0},{12,4},{16,24},{20,28},{24,16},{28,20},{1,9},{5... | collective-permute-start | bytes 98312 | tf_op jit(solution)/shard_map/ppermute | solution.py:566
  (78 other events, 284.4 us)

commit v9 on v8

--- a/solution.py
+++ b/solution.py
@@ -132,8 +132,20 @@
 
 
 def bounds_kernel(g, zones, zlow, zhigh, zone, low_o, high_o):
+    lows = [jnp.full((8, g.nz), zlow[i], F32) for i in range(zones)]
+    highs = [jnp.full((8, g.nz), zhigh[i], F32) for i in range(zones)]
+
     def body(x, carry):
-        low_o[x], high_o[x] = bounds_of(zones, zone[x], zlow, zhigh)
+        for k in range(0, g.ny, 8):
+            here = pl.ds(k, 8)
+            z = zone[x, here, :]
+            low, high = lows[0], highs[0]
+            for i in range(1, zones):
+                hit = z == i
+                low = jnp.where(hit, lows[i], low)
+                high = jnp.where(hit, highs[i], high)
+            low_o[x, here, :] = low
+            high_o[x, here, :] = high
         return carry
 
     lax.fori_loop(0, g.nx, body, 0, unroll=8)

time: 159 us -> 159 us (level)
  no operation moved by 1% of the time
where the time goes in v9:
time: 159 us; the launch traced here: 157 us
  local copies, waits for them, and re-layouts  58.1 us (37%)
  starting transfers between devices  51.3 us (32%)
  Pallas kernels  26 us (16%)
  blocking collectives  10.7 us (7%)
  waiting for transfers between devices  9.92 us (6%)
    unnamed x154, local copies, waits for them, and re-layouts  58.1 us
    pallas_call x11, Pallas kernels, call(): pl.pallas_call(body, out_shape=[jax.ShapeDtypeStruct(s, d) for s, d in sh...  26 us
    ppermute x9, starting transfers between devices, pair_totals(): out.append(lax.ppermute(pair, 'gx', [(i, i ^ 2 * m) for i in range(size)]))  22.8 us
    all_to_all x1, blocking collectives, local(): history.append(lax.all_to_all(head, both, 0, 0, tiled=True))  10.7 us
    all_to_all x2, starting transfers between devices, local(): sums = lax.all_to_all(sums, both, 0, 0, tiled=True)  9.72 us
    ppermute x7, starting transfers between devices, exchange(): a = lax.ppermute(a, axis, pa)  9.5 us
    ppermute x7, starting transfers between devices, exchange(): b = lax.ppermute(b, axis, pb)  9.26 us
    ppermute x9, waiting for transfers between devices, pair_totals(): out.append(lax.ppermute(pair, 'gx', [(i, i ^ 2 * m) for i in range(size)]))  6.19 us
  transfers between devices with their start and end apart: 25, of which 7 were waited for; matrix products, arithmetic and copies ran while one was open for 0% of the time, Pallas kernels for 3%

profile of v9, /device:TPU:0, one launch (start us, length us, event | category | flops | bytes accessed | tf_op | source)
XLA Modules:
  0.0 157.2 jit_solution(2170073489221038723)
XLA Ops:
  0.7 2.4 %shard_map.94 = (f32[64,128]{1,0:T(8,128)S(1)}, f32[256,128]{1,0:T(8,128)S(1)}, f32[192,128]{1,0:T(8,128)S(1)}, f32[64,32,128]{2,1,0:T(8,128)S(1)}, f32[64,32,128]{2,1,0:T(8,128)S(1)}) custom-call(s32[2]{0:T(128)S(1)} %pad_add_fusion.flags, f32[64,32,128]{2,1,0:T(8,128)} %rho.3, f32[64,32,128]{2,1,0:T(8,128)} %sigma.1, s32[64,32,128]{2,1,0:T(8,128)} %zone.3, ...), custom_call_target="tpu_custom_call" | custom-call | tf_op jit(solution)/shard_map/pallas_call | solution.py:588
  5.2 2.6 %collective-permute-start = (f32[256,128]{1,0:T(8,128)S(1)}, f32[256,128]{1,0:T(8,128)S(1)}, u32[]{:S(2)}, u32[]{:S(2)}) collective-permute-start(f32[256,128]{1,0:T(8,128)S(1)} %get-tuple-element.54), channel_id=1, source_target_pairs={{0,4},{4,0},{8,12},{12,8},{16,20},{20,16},{24,28},{28,24},{1,5},{5... | collective-permute-start | bytes 393224 | tf_op jit(solution)/shard_map/ppermute | solution.py:570
  8.5 2.3 %collective-permute-done.xa = f32[256,128]{1,0:T(8,128)S(1)} collective-permute-done((f32[256,128]{1,0:T(8,128)S(1)}, f32[256,128]{1,0:T(8,128)S(1)}, u32[]{:S(2)}, u32[]{:S(2)}) %collective-permute-start) | collective-permute-done | bytes 131104 | tf_op jit(solution)/shard_map/ppermute | solution.py:570
  11.3 2.7 %collective-permute-start.4 = (f32[8,128]{1,0:T(8,128)S(1)}, f32[8,128]{1,0:T(8,128)S(1)}, u32[]{:S(2)}, u32[]{:S(2)}) collective-permute-start(f32[8,128]{1,0:T(8,128)S(1)} %get-tuple-element.60), channel_id=1, source_target_pairs={{0,1},{1,0},{2,3},{3,2},{4,5},{5,4},{6,7},{7,6},{8,9},{9,8},{10,11... | collective-permute-start | bytes 12296 | tf_op jit(solution)/shard_map/ppermute | solution.py:570
  14.6 7.0 %collective-permute-start.8 = (f32[64,128]{1,0:T(8,128)S(1)}, f32[64,128]{1,0:T(8,128)S(1)}, u32[]{:S(2)}, u32[]{:S(2)}) collective-permute-start(f32[64,128]{1,0:T(8,128)S(1)} %get-tuple-element.67), channel_id=1, source_target_pairs={{0,24},{4,28},{8,16},{12,20},{16,8},{20,12},{24,0},{28,4},{1,25},{... | collective-permute-start | bytes 98312 | tf_op jit(solution)/shard_map/ppermute | solution.py:578
  23.5 3.0 %collective-permute-done.7.refs_1_ = f32[64,128]{1,0:T(8,128)S(1)} collective-permute-done((f32[64,128]{1,0:T(8,128)S(1)}, f32[64,128]{1,0:T(8,128)S(1)}, u32[]{:S(2)}, u32[]{:S(2)}) %collective-permute-start.7) | collective-permute-done | bytes 32800 | tf_op jit(solution)/shard_map/ppermute | solution.py:578
  26.5 5.5 %shard_map.98 = (f32[2993,128]{1,0:T(8,128)S(1)}, f32[2993,128]{1,0:T(8,128)S(1)}, f32[5,64,128]{2,1,0:T(8,128)S(1)}, f32[2,64,128]{2,1,0:T(8,128)S(1)}, f32[2,6...) custom-call(s32[2]{0:T(128)S(1)} %pad_add_fusion.flags, ...), custom_call_target="tpu_custom_call" | custom-call | tf_op jit(solution)/shard_map/pallas_call | solution.py:588
  39.5 1.8 %collective-permute-start.11 = (f32[256,128]{1,0:T(8,128)}, f32[256,128]{1,0:T(8,128)}, u32[]{:S(2)}, u32[]{:S(2)}) collective-permute-start(f32[256,128]{1,0:T(8,128)} %get-tuple-element.73), channel_id=1, source_target_pairs={{0,1},{1,0},{2,3},{3,2},{4,5},{5,4},{6,7},{7,6},{8,9},{9,8},{10,11... | collective-permute-start | bytes 393224 | tf_op jit(solution)/shard_map/ppermute | solution.py:570
  41.3 2.1 %collective-permute-start.12 = (f32[256,128]{1,0:T(8,128)}, f32[256,128]{1,0:T(8,128)}, u32[]{:S(2)}, u32[]{:S(2)}) collective-permute-start(f32[256,128]{1,0:T(8,128)} %get-tuple-element.74), channel_id=1, source_target_pairs={{0,0},{1,2},{2,1},{3,3},{4,4},{5,6},{6,5},{7,7},{8,8},{9,10},{10,9... | collective-permute-start | bytes 393224 | tf_op jit(solution)/shard_map/ppermute | solution.py:571
  47.3 4.8 %all-to-all-start = ((f32[32,4,128]{2,1,0:T(4,128)}), f32[32,4,128]{2,1,0:T(4,128)S(1)}, u32[]{:S(2)}, u32[]{:S(2)}) async-start(f32[32,4,128]{2,1,0:T(4,128)} %bitcast.21), calls=%async_computation | async-start | bytes 131072 | tf_op jit(solution)/shard_map/all_to_all | solution.py:668
  52.1 1.5 collective-permute-start.10
  53.6 5.5 %collective-permute-start.15 = (f32[64,128]{1,0:T(8,128)}, f32[64,128]{1,0:T(8,128)S(1)}, u32[]{:S(2)}, u32[]{:S(2)}) collective-permute-start(f32[64,128]{1,0:T(8,128)} %copy-done.75), channel_id=1, source_target_pairs={{0,24},{4,28},{8,16},{12,20},{16,8},{20,12},{24,0},{28,4},{1,25},{... | collective-permute-start | bytes 98312 | tf_op jit(solution)/shard_map/ppermute | solution.py:578
  59.8 2.1 %collective-permute-start.13 = (f32[64,128]{1,0:T(8,128)}, f32[64,128]{1,0:T(8,128)S(1)}, u32[]{:S(2)}, u32[]{:S(2)}) collective-permute-start(f32[64,128]{1,0:T(8,128)} %copy-done.75), channel_id=1, source_target_pairs={{0,8},{4,12},{8,0},{12,4},{16,24},{20,28},{24,16},{28,20},{1,9},{5... | collective-permute-start | bytes 98312 | tf_op jit(solution)/shard_map/ppermute | solution.py:578
  71.9 1.4 copy-done.12
  86.1 6.1 %shard_map.101 = (f32[2993,128]{1,0:T(8,128)S(1)}, f32[2993,128]{1,0:T(8,128)S(1)}, f32[5,64,128]{2,1,0:T(8,128)S(1)}, f32[2112,128]{1,0:T(8,128)S(1)}, f32[2112...) custom-call(s32[2]{0:T(128)S(1)} %copy-done.67, ...), custom_call_target="tpu_custom_call" | custom-call | tf_op jit(solution)/shard_map/pallas_call | solution.py:588
  97.1 1.9 %collective-permute-start.16 = (f32[192,128]{1,0:T(8,128)S(1)}, f32[192,128]{1,0:T(8,128)S(1)}, u32[]{:S(2)}, u32[]{:S(2)}) collective-permute-start(f32[192,128]{1,0:T(8,128)S(1)} %get-tuple-element.87), channel_id=1, source_target_pairs={{0,4},{4,0},{8,12},{12,8},{16,20},{20,16},{24,28},{28,24},{1,5},{5... | collective-permute-start | bytes 294920 | tf_op jit(solution)/shard_map/ppermute | solution.py:570
  99.0 2.1 %collective-permute-start.19 = (f32[256,128]{1,0:T(8,128)}, f32[256,128]{1,0:T(8,128)}, u32[]{:S(2)}, u32[]{:S(2)}) collective-permute-start(f32[256,128]{1,0:T(8,128)} %get-tuple-element.93), channel_id=1, source_target_pairs={{0,0},{1,2},{2,1},{3,3},{4,4},{5,6},{6,5},{7,7},{8,8},{9,10},{10,9... | collective-permute-start | bytes 393224 | tf_op jit(solution)/shard_map/ppermute | solution.py:571
  104.2 4.9 %all-to-all-start.1 = ((f32[32,4,128]{2,1,0:T(4,128)}), f32[32,4,128]{2,1,0:T(4,128)S(1)}, u32[]{:S(2)}, u32[]{:S(2)}) async-start(f32[32,4,128]{2,1,0:T(4,128)} %bitcast.7), calls=%async_computation.1 | async-start | bytes 131072 | tf_op jit(solution)/shard_map/all_to_all | solution.py:668
  109.2 1.5 collective-permute-start.17
  110.6 5.7 %collective-permute-start.22 = (f32[64,128]{1,0:T(8,128)}, f32[64,128]{1,0:T(8,128)S(1)}, u32[]{:S(2)}, u32[]{:S(2)}) collective-permute-start(f32[64,128]{1,0:T(8,128)} %copy-done.76), channel_id=1, source_target_pairs={{0,24},{4,28},{8,16},{12,20},{16,8},{20,12},{24,0},{28,4},{1,25},{... | collective-permute-start | bytes 98312 | tf_op jit(solution)/shard_map/ppermute | solution.py:578
  116.4 1.9 %collective-permute-start.20 = (f32[64,128]{1,0:T(8,128)}, f32[64,128]{1,0:T(8,128)S(1)}, u32[]{:S(2)}, u32[]{:S(2)}) collective-permute-start(f32[64,128]{1,0:T(8,128)} %copy-done.76), channel_id=1, source_target_pairs={{0,8},{4,12},{8,0},{12,4},{16,24},{20,28},{24,16},{28,20},{1,9},{5... | collective-permute-start | bytes 98312 | tf_op jit(solution)/shard_map/ppermute | solution.py:578
  139.3 5.1 %shard_map.103 = (f32[2993,128]{1,0:T(8,128)S(1)}, f32[2993,128]{1,0:T(8,128)S(1)}, f32[2112,128]{1,0:T(8,128)S(1)}, f32[2112,128]{1,0:T(8,128)S(1)}, f32[32,128]{1,0:T(8,128)S(1)}) custom-call(s32[2]{0:T(128)S(1)} %copy-done.68, f32[192,128]{1,0:T(8,128)S(1)} %copy-done.36, f32[128,128]{1,0:T(8,128)S(1)} %collective-permute-done.17.xb, ...), custom_call_target="tpu_custom_call" | custom-call | tf_op jit(solution)/shard_map/pallas_call | solution.py:588
  144.4 10.7 %all_to_all.33 = f32[32,1,128]{2,1,0:T(1,128)S(1)} all-to-all(f32[32,1,128]{2,1,0:T(1,128)S(1)} %bitcast.22), channel_id=1, replica_groups=mesh['gx'=8,'gy'=4] {'gx','gy'}, dimensions={0} | all-to-all | bytes 32768 | tf_op jit(solution)/shard_map/all_to_all | solution.py:682
  155.1 1.9 %shard_map.104 = (f32[64,32,128]{2,1,0:T(8,128)}, f32[64,32,128]{2,1,0:T(8,128)}, f32[3]{0:T(128)}) custom-call(f32[128,128]{1,0:T(8,128)S(1)} %bitcast.17, f32[128,128]{1,0:T(8,128)S(1)} %bitcast.19, f32[32,128]{1,0:T(8,128)S(1)} %bitcast.20, f32[2112,128]{1,0:T(8,128)S(1)} %get-tuple-element.101.grho, f32[2112,128]{1,0:T(8,128)S(1)} %get-tuple-element.102.gsig, ...), custom_call_target="tpu_custom_call" | custom-call | tf_op jit(solution)/shard_map/pallas_call | solution.py:588
  (193 shorter events, 69.6 us)
Async XLA Ops:
  4.0 22.5 %collective-permute-start.2 = (f32[384,128]{1,0:T(8,128)S(1)}, f32[384,128]{1,0:T(8,128)S(1)}, u32[]{:S(2)}, u32[]{:S(2)}) collective-permute-start(f32[384,128]{1,0:T(8,128)S(1)} %get-tuple-element.58), channel_id=1, source_target_pairs={{0,1},{1,0},{2,3},{3,2},{4,5},{5,4},{6,7},{7,6},{8,9},{9,8},{10,11... | collective-permute-start | bytes 589832 | tf_op jit(solution)/shard_map/ppermute | solution.py:570
  4.5 21.9 %collective-permute-start.3 = (f32[384,128]{1,0:T(8,128)S(1)}, f32[384,128]{1,0:T(8,128)S(1)}, u32[]{:S(2)}, u32[]{:S(2)}) collective-permute-start(f32[384,128]{1,0:T(8,128)S(1)} %get-tuple-element.59), channel_id=1, source_target_pairs={{0,0},{1,2},{2,1},{3,3},{4,4},{5,6},{6,5},{7,7},{8,8},{9,10},{10,9... | collective-permute-start | bytes 589832 | tf_op jit(solution)/shard_map/ppermute | solution.py:571
  5.2 5.5 %collective-permute-start = (f32[256,128]{1,0:T(8,128)S(1)}, f32[256,128]{1,0:T(8,128)S(1)}, u32[]{:S(2)}, u32[]{:S(2)}) collective-permute-start(f32[256,128]{1,0:T(8,128)S(1)} %get-tuple-element.54), channel_id=1, source_target_pairs={{0,4},{4,0},{8,12},{12,8},{16,20},{20,16},{24,28},{28,24},{1,5},{5... | collective-permute-start | bytes 393224 | tf_op jit(solution)/shard_map/ppermute | solution.py:570
  11.3 10.3 %collective-permute-start.4 = (f32[8,128]{1,0:T(8,128)S(1)}, f32[8,128]{1,0:T(8,128)S(1)}, u32[]{:S(2)}, u32[]{:S(2)}) collective-permute-start(f32[8,128]{1,0:T(8,128)S(1)} %get-tuple-element.60), channel_id=1, source_target_pairs={{0,1},{1,0},{2,3},{3,2},{4,5},{5,4},{6,7},{7,6},{8,9},{9,8},{10,11... | collective-permute-start | bytes 12296 | tf_op jit(solution)/shard_map/ppermute | solution.py:570
  14.0 7.6 %collective-permute-start.5 = (f32[8,128]{1,0:T(8,128)S(1)}, f32[8,128]{1,0:T(8,128)S(1)}, u32[]{:S(2)}, u32[]{:S(2)}) collective-permute-start(f32[8,128]{1,0:T(8,128)S(1)} %get-tuple-element.61), channel_id=1, source_target_pairs={{0,0},{1,2},{2,1},{3,3},{4,4},{5,6},{6,5},{7,7},{8,8},{9,10},{10,9... | collective-permute-start | bytes 12296 | tf_op jit(solution)/shard_map/ppermute | solution.py:571
  14.6 8.8 %collective-permute-start.8 = (f32[64,128]{1,0:T(8,128)S(1)}, f32[64,128]{1,0:T(8,128)S(1)}, u32[]{:S(2)}, u32[]{:S(2)}) collective-permute-start(f32[64,128]{1,0:T(8,128)S(1)} %get-tuple-element.67), channel_id=1, source_target_pairs={{0,24},{4,28},{8,16},{12,20},{16,8},{20,12},{24,0},{28,4},{1,25},{... | collective-permute-start | bytes 98312 | tf_op jit(solution)/shard_map/ppermute | solution.py:578
  21.6 4.8 %collective-permute-start.7 = (f32[64,128]{1,0:T(8,128)S(1)}, f32[64,128]{1,0:T(8,128)S(1)}, u32[]{:S(2)}, u32[]{:S(2)}) collective-permute-start(f32[64,128]{1,0:T(8,128)S(1)} %get-tuple-element.67), channel_id=1, source_target_pairs={{0,16},{4,20},{8,24},{12,28},{16,0},{20,4},{24,8},{28,12},{1,17},{... | collective-permute-start | bytes 98312 | tf_op jit(solution)/shard_map/ppermute | solution.py:578
  21.6 4.8 %collective-permute-start.6 = (f32[64,128]{1,0:T(8,128)S(1)}, f32[64,128]{1,0:T(8,128)S(1)}, u32[]{:S(2)}, u32[]{:S(2)}) collective-permute-start(f32[64,128]{1,0:T(8,128)S(1)} %get-tuple-element.67), channel_id=1, source_target_pairs={{0,8},{4,12},{8,0},{12,4},{16,24},{20,28},{24,16},{28,20},{1,9},{5... | collective-permute-start | bytes 98312 | tf_op jit(solution)/shard_map/ppermute | solution.py:578
  39.5 4.8 %collective-permute-start.9 = (f32[192,128]{1,0:T(8,128)S(1)}, f32[192,128]{1,0:T(8,128)S(1)}, u32[]{:S(2)}, u32[]{:S(2)}) collective-permute-start(f32[192,128]{1,0:T(8,128)S(1)} %get-tuple-element.68), channel_id=1, source_target_pairs={{0,4},{4,0},{8,12},{12,8},{16,20},{20,16},{24,28},{28,24},{1,5},{5... | collective-permute-start | bytes 294920 | tf_op jit(solution)/shard_map/ppermute | solution.py:570
  39.5 28.8 %collective-permute-start.11 = (f32[256,128]{1,0:T(8,128)}, f32[256,128]{1,0:T(8,128)}, u32[]{:S(2)}, u32[]{:S(2)}) collective-permute-start(f32[256,128]{1,0:T(8,128)} %get-tuple-element.73), channel_id=1, source_target_pairs={{0,1},{1,0},{2,3},{3,2},{4,5},{5,4},{6,7},{7,6},{8,9},{9,8},{10,11... | collective-permute-start | bytes 393224 | tf_op jit(solution)/shard_map/ppermute | solution.py:570
  41.3 26.9 %collective-permute-start.12 = (f32[256,128]{1,0:T(8,128)}, f32[256,128]{1,0:T(8,128)}, u32[]{:S(2)}, u32[]{:S(2)}) collective-permute-start(f32[256,128]{1,0:T(8,128)} %get-tuple-element.74), channel_id=1, source_target_pairs={{0,0},{1,2},{2,1},{3,3},{4,4},{5,6},{6,5},{7,7},{8,8},{9,10},{10,9... | collective-permute-start | bytes 393224 | tf_op jit(solution)/shard_map/ppermute | solution.py:571
  47.3 20.9 %all-to-all-start = ((f32[32,4,128]{2,1,0:T(4,128)}), f32[32,4,128]{2,1,0:T(4,128)S(1)}, u32[]{:S(2)}, u32[]{:S(2)}) async-start(f32[32,4,128]{2,1,0:T(4,128)} %bitcast.21), calls=%async_computation | async-start | bytes 131072 | tf_op jit(solution)/shard_map/all_to_all | solution.py:668
  52.1 7.0 %collective-permute-start.10 = (f32[128,128]{1,0:T(8,128)}, f32[128,128]{1,0:T(8,128)S(1)}, u32[]{:S(2)}, u32[]{:S(2)}) collective-permute-start(f32[128,128]{1,0:T(8,128)} %copy-done.73), channel_id=1, source_target_pairs={{0,0},{4,8},{8,4},{12,16},{16,12},{20,24},{24,20},{28,28},{1,1},{5... | collective-permute-start | bytes 196616 | tf_op jit(solution)/shard_map/ppermute | solution.py:571
  53.6 12.8 %collective-permute-start.15 = (f32[64,128]{1,0:T(8,128)}, f32[64,128]{1,0:T(8,128)S(1)}, u32[]{:S(2)}, u32[]{:S(2)}) collective-permute-start(f32[64,128]{1,0:T(8,128)} %copy-done.75), channel_id=1, source_target_pairs={{0,24},{4,28},{8,16},{12,20},{16,8},{20,12},{24,0},{28,4},{1,25},{... | collective-permute-start | bytes 98312 | tf_op jit(solution)/shard_map/ppermute | solution.py:578
  59.1 7.9 %collective-permute-start.14 = (f32[64,128]{1,0:T(8,128)}, f32[64,128]{1,0:T(8,128)S(1)}, u32[]{:S(2)}, u32[]{:S(2)}) collective-permute-start(f32[64,128]{1,0:T(8,128)} %copy-done.75), channel_id=1, source_target_pairs={{0,16},{4,20},{8,24},{12,28},{16,0},{20,4},{24,8},{28,12},{1,17},{... | collective-permute-start | bytes 98312 | tf_op jit(solution)/shard_map/ppermute | solution.py:578
  59.8 7.9 %collective-permute-start.13 = (f32[64,128]{1,0:T(8,128)}, f32[64,128]{1,0:T(8,128)S(1)}, u32[]{:S(2)}, u32[]{:S(2)}) collective-permute-start(f32[64,128]{1,0:T(8,128)} %copy-done.75), channel_id=1, source_target_pairs={{0,8},{4,12},{8,0},{12,4},{16,24},{20,28},{24,16},{28,20},{1,9},{5... | collective-permute-start | bytes 98312 | tf_op jit(solution)/shard_map/ppermute | solution.py:578
  97.1 4.6 %collective-permute-start.16 = (f32[192,128]{1,0:T(8,128)S(1)}, f32[192,128]{1,0:T(8,128)S(1)}, u32[]{:S(2)}, u32[]{:S(2)}) collective-permute-start(f32[192,128]{1,0:T(8,128)S(1)} %get-tuple-element.87), channel_id=1, source_target_pairs={{0,4},{4,0},{8,12},{12,8},{16,20},{20,16},{24,28},{28,24},{1,5},{5... | collective-permute-start | bytes 294920 | tf_op jit(solution)/shard_map/ppermute | solution.py:570
  99.0 23.6 %collective-permute-start.18 = (f32[256,128]{1,0:T(8,128)}, f32[256,128]{1,0:T(8,128)}, u32[]{:S(2)}, u32[]{:S(2)}) collective-permute-start(f32[256,128]{1,0:T(8,128)} %get-tuple-element.92), channel_id=1, source_target_pairs={{0,1},{1,0},{2,3},{3,2},{4,5},{5,4},{6,7},{7,6},{8,9},{9,8},{10,11... | collective-permute-start | bytes 393224 | tf_op jit(solution)/shard_map/ppermute | solution.py:570
  99.0 23.6 %collective-permute-start.19 = (f32[256,128]{1,0:T(8,128)}, f32[256,128]{1,0:T(8,128)}, u32[]{:S(2)}, u32[]{:S(2)}) collective-permute-start(f32[256,128]{1,0:T(8,128)} %get-tuple-element.93), channel_id=1, source_target_pairs={{0,0},{1,2},{2,1},{3,3},{4,4},{5,6},{6,5},{7,7},{8,8},{9,10},{10,9... | collective-permute-start | bytes 393224 | tf_op jit(solution)/shard_map/ppermute | solution.py:571
  104.2 18.4 %all-to-all-start.1 = ((f32[32,4,128]{2,1,0:T(4,128)}), f32[32,4,128]{2,1,0:T(4,128)S(1)}, u32[]{:S(2)}, u32[]{:S(2)}) async-start(f32[32,4,128]{2,1,0:T(4,128)} %bitcast.7), calls=%async_computation.1 | async-start | bytes 131072 | tf_op jit(solution)/shard_map/all_to_all | solution.py:668
  109.2 7.2 %collective-permute-start.17 = (f32[128,128]{1,0:T(8,128)}, f32[128,128]{1,0:T(8,128)S(1)}, u32[]{:S(2)}, u32[]{:S(2)}) collective-permute-start(f32[128,128]{1,0:T(8,128)} %copy-done.74), channel_id=1, source_target_pairs={{0,0},{4,8},{8,4},{12,16},{16,12},{20,24},{24,20},{28,28},{1,1},{5... | collective-permute-start | bytes 196616 | tf_op jit(solution)/shard_map/ppermute | solution.py:571
  110.6 8.8 %collective-permute-start.22 = (f32[64,128]{1,0:T(8,128)}, f32[64,128]{1,0:T(8,128)S(1)}, u32[]{:S(2)}, u32[]{:S(2)}) collective-permute-start(f32[64,128]{1,0:T(8,128)} %copy-done.76), channel_id=1, source_target_pairs={{0,24},{4,28},{8,16},{12,20},{16,8},{20,12},{24,0},{28,4},{1,25},{... | collective-permute-start | bytes 98312 | tf_op jit(solution)/shard_map/ppermute | solution.py:578
  116.3 5.0 %collective-permute-start.21 = (f32[64,128]{1,0:T(8,128)}, f32[64,128]{1,0:T(8,128)S(1)}, u32[]{:S(2)}, u32[]{:S(2)}) collective-permute-start(f32[64,128]{1,0:T(8,128)} %copy-done.76), channel_id=1, source_target_pairs={{0,16},{4,20},{8,24},{12,28},{16,0},{20,4},{24,8},{28,12},{1,17},{... | collective-permute-start | bytes 98312 | tf_op jit(solution)/shard_map/ppermute | solution.py:578
  116.4 5.6 %collective-permute-start.20 = (f32[64,128]{1,0:T(8,128)}, f32[64,128]{1,0:T(8,128)S(1)}, u32[]{:S(2)}, u32[]{:S(2)}) collective-permute-start(f32[64,128]{1,0:T(8,128)} %copy-done.76), channel_id=1, source_target_pairs={{0,8},{4,12},{8,0},{12,4},{16,24},{20,28},{24,16},{28,20},{1,9},{5... | collective-permute-start | bytes 98312 | tf_op jit(solution)/shard_map/ppermute | solution.py:578
  (78 other events, 284.3 us)
